TPU v7x, 32 devices: a whole 2x2x4 slice. The times are simulated.
32 devices in a mesh: fsdp: 16 (over z, y, x), dp: 2 (over core).
Axes of the slice: x: 2, y: 2, z: 4, core: 2. Of those that a mesh axis runs over, the one named last changes fastest.
Arguments:
- token_ids: int32 [32, 512], P(('fsdp', 'dp')), may hold values from 0 to 30719, as said below
- labels: int32 [32, 512], P(('fsdp', 'dp')), may hold values 0 or 1
- loss_mask: int32 [32, 512], P(('fsdp', 'dp')), may hold values from 0 to 1, as said below
- batch_of: int32 [32], P(('fsdp', 'dp')), may hold values from 0 to 1, as said below
- layer_in: float32 [1, 1024, 8192], P(None, None, ('fsdp', 'dp'))
- layer_down: float32 [1, 4096, 1024], P(None, ('fsdp', 'dp')), may hold values from -0.09375 to 0.09375
- word_table: float32 [30720, 1024], P(('fsdp', 'dp')), may hold values from -0.3 to 0.3
- side_mat: float32 [1536, 1024], P(('fsdp', 'dp'))
- vectors: float32 [16384], P(('fsdp', 'dp'))
- in_rows: float32 [1, 3, 1024], replicated, may hold values from 1e-07 to 1e-05
- in_cols: float32 [1, 8192], P(None, ('fsdp', 'dp')), may hold values from 1e-07 to 1e-05
- down_rows: float32 [1, 4096], P(None, ('fsdp', 'dp')), may hold values from 1e-07 to 1e-05
- down_cols: float32 [1, 1024], replicated, may hold values from 1e-07 to 1e-05
- word_rows: float32 [30720], P(('fsdp', 'dp')), may hold values from 1e-12 to 1e-10
- word_cols: float32 [1024], replicated, may hold values from 1e-12 to 1e-10
- side_rows: float32 [1536], P(('fsdp', 'dp')), may hold values from 1e-07 to 1e-05
- side_cols: float32 [2, 1024], replicated, may hold values from 1e-07 to 1e-05
- vec_moment: float32 [16384], P(('fsdp', 'dp')), as said below
Outputs:
- loss: float32 [], replicated
- new_in: float32 [1, 1024, 8192], P(None, None, ('fsdp', 'dp'))
- new_in_rows: float32 [1, 3, 1024], replicated
- new_in_cols: float32 [1, 8192], P(None, ('fsdp', 'dp'))
- in_copy: bfloat16 [1, 1024, 8192], P(None, None, ('fsdp', 'dp'))
- new_down: float32 [1, 4096, 1024], P(None, ('fsdp', 'dp'))
- new_down_rows: float32 [1, 4096], P(None, ('fsdp', 'dp'))
- new_down_cols: float32 [1, 1024], replicated
- down_copy: bfloat16 [1, 4096, 1024], P(None, ('fsdp', 'dp'))
- new_word: float32 [30720, 1024], P(('fsdp', 'dp'))
- new_word_rows: float32 [30720], P(('fsdp', 'dp'))
- new_word_cols: float32 [1024], replicated
- word_copy: bfloat16 [30720, 1024], P(('fsdp', 'dp'))
- new_side: float32 [1536, 1024], P(('fsdp', 'dp'))
- new_side_rows: float32 [1536], P(('fsdp', 'dp'))
- new_side_cols: float32 [2, 1024], replicated
- side_copy: bfloat16 [1536, 1024], P(('fsdp', 'dp'))
- new_vectors: float32 [16384], P(('fsdp', 'dp'))
- new_moment: float32 [16384], P(('fsdp', 'dp'))
- vector_copy: bfloat16 [16384], P(('fsdp', 'dp'))
Inputs may be any that keep to these rules, and one draw needn't show every extreme that they name: `token_ids`: the 512 tokens of one device (its 1 sequence along fsdp+dp) fall at most 32 times into one block of 960 consecutive vocabulary rows, and in every device some block gets exactly 32. `loss_mask`: position 0 of every sequence counts. `batch_of`: each of the 2 micro-batches holds 16 sequences. `vec_moment`: every entry is positive.
All inputs are finite; a program needn't handle non-finite values. No bound on the sum of `labels` on one device may be relied on, other than what follows from the above.
Results may differ from a plain program's by a relative error of at most 0.0055.
The roundings to bfloat16 on the way count: a program that leaves them out, or rounds other values in their place, can miss the bound.
Values may be sent and summed in bfloat16 or wider, within the bound.
A program may use at most 256 MiB of HBM per device.

v0:
```python
import jax
import jax.numpy as jnp
from jax import lax
from jax.sharding import PartitionSpec as P

D = 1024
HEADS = 16
HEAD_DIM = 64
FF = 4096
VOCAB = 30720
SEQ_LEN = 512
LAYERS = 1
MICRO = 2


learn_rate = 0.02
decay_rate = 0.5
tiny_square = 1e-30
norm_epsilon = 1e-12
precise = lax.Precision.HIGHEST


def layer_norm(inputs, norm_gain, norm_shift):
    center = inputs - jnp.mean(inputs, axis=-1, keepdims=True)
    spread = jnp.mean(center * center, axis=-1, keepdims=True)
    return center * lax.rsqrt(spread + norm_epsilon) * norm_gain + norm_shift


def norm_back(inputs, norm_gain, norm_shift, cotangent):
    result, pull = jax.vjp(layer_norm, inputs, norm_gain, norm_shift)
    return pull(cotangent)


def exact_gelu(inputs):
    return jax.nn.gelu(inputs, approximate=False)


def gelu_back(inputs, cotangent):
    result, pull = jax.vjp(exact_gelu, inputs)
    return pull(cotangent)[0]


def multiply(left_side, right_side):
    return jnp.dot(left_side, right_side, preferred_element_type=jnp.float32)


def multiply_left(left_side, right_side):
    return lax.dot_general(
        left_side, right_side, (((0,), (0,)), ((), ())), preferred_element_type=jnp.float32
    )


def multiply_right(left_side, right_side):
    return lax.dot_general(
        left_side, right_side, (((1,), (1,)), ((), ())), preferred_element_type=jnp.float32
    )


def piece_bounds():
    return [0, D, 2 * D, 3 * D, 4 * D, 5 * D, 5 * D + FF, 6 * D + FF, 7 * D + FF, 8 * D + FF]


def layer_slices(all_vectors, layer_index):
    bounds = piece_bounds()
    offset = layer_index * (8 * D + FF)
    return [
        all_vectors[offset + bounds[slot_index] : offset + bounds[slot_index + 1]]
        for slot_index in range(9)
    ]


def segment_index(position):
    piece_width = 8 * D + FF
    inner = position % piece_width
    layer_of = position // piece_width
    bounds = piece_bounds()[1:-1]
    local_segment = sum(((inner >= bound).astype(jnp.int32) for bound in bounds))
    tail = 9 * LAYERS + (position - LAYERS * piece_width) // D
    return jnp.where(position < LAYERS * piece_width, 9 * layer_of + local_segment, tail)


def segment_sizes():
    sizes = []
    sizes = sizes + [D, D, D, D, D, FF, D, D, D]
    return jnp.array(sizes + [D, D, D, D], jnp.float32)


def attend(queries, key_rows, values):
    scores = jnp.einsum(
        "qhe,khe->hqk", queries, key_rows, preferred_element_type=jnp.float32
    ) * HEAD_DIM ** (-0.5)
    peak_score = jnp.max(scores, axis=-1, keepdims=True)
    exponent = jnp.exp(scores - peak_score)
    running = jnp.sum(exponent, axis=-1, keepdims=True)
    soft_probs = exponent / running
    context = jnp.einsum(
        "hqk,khe->qhe", soft_probs.astype(jnp.bfloat16), values, preferred_element_type=jnp.float32
    )
    return (context, peak_score + jnp.log(running))


def attend_back(queries, key_rows, values, log_total, d_context):
    score_scale = HEAD_DIM ** (-0.5)
    scores = (
        jnp.einsum("qhe,khe->hqk", queries, key_rows, preferred_element_type=jnp.float32)
        * score_scale
    )
    soft_probs = jnp.exp(scores - log_total)
    d_values = jnp.einsum(
        "hqk,qhe->khe",
        soft_probs.astype(jnp.bfloat16),
        d_context,
        preferred_element_type=jnp.float32,
    )
    d_probs = jnp.einsum("qhe,khe->hqk", d_context, values, preferred_element_type=jnp.float32)
    d_scores = soft_probs * (d_probs - jnp.sum(d_probs * soft_probs, axis=-1, keepdims=True))
    d_scores_low = d_scores.astype(jnp.bfloat16)
    d_queries = (
        jnp.einsum("hqk,khe->qhe", d_scores_low, key_rows, preferred_element_type=jnp.float32)
        * score_scale
    )
    d_keys = (
        jnp.einsum("hqk,qhe->khe", d_scores_low, queries, preferred_element_type=jnp.float32)
        * score_scale
    )
    return jnp.stack([d_queries, d_keys, d_values], axis=1)


def layer_forward(hidden, weight_in, weight_down, pieces, seq_dev):
    bias_q, bias_v, bias_o, gain_a, shift_a, bias_up, bias_down, gain_b, shift_b = pieces
    tokens = hidden.shape[0]
    length = tokens // seq_dev
    hidden_low = hidden.astype(jnp.bfloat16)
    joint_bias = jnp.concatenate([bias_q, jnp.zeros_like(bias_q), bias_v])
    projected = (multiply(hidden_low, weight_in[:, : 3 * D]) + joint_bias).astype(jnp.bfloat16)
    heads_view = projected.reshape(seq_dev, length, 3, HEADS, HEAD_DIM)
    context, log_total = jax.vmap(attend)(
        heads_view[:, :, 0], heads_view[:, :, 1], heads_view[:, :, 2]
    )
    context_low = context.reshape(tokens, D).astype(jnp.bfloat16)
    mid_in = hidden + (multiply(context_low, weight_in[:, 3 * D : 4 * D]) + bias_o)
    middle = layer_norm(mid_in, gain_a, shift_a)
    middle_low = middle.astype(jnp.bfloat16)
    lifted = multiply(middle_low, weight_in[:, 4 * D :]) + bias_up
    active_low = exact_gelu(lifted).astype(jnp.bfloat16)
    out_in = middle + (multiply(active_low, weight_down) + bias_down)
    output = layer_norm(out_in, gain_b, shift_b)
    return (
        output,
        (
            hidden_low,
            projected,
            log_total,
            context_low,
            mid_in,
            middle_low,
            lifted,
            active_low,
            out_in,
        ),
    )


def layer_backward(grad_out, weight_in, weight_down, pieces, kept, seq_dev):
    bias_q, bias_v, bias_o, gain_a, shift_a, bias_up, bias_down, gain_b, shift_b = pieces
    (
        hidden_low,
        projected,
        log_total,
        context_low,
        mid_in,
        middle_low,
        lifted,
        active_low,
        out_in,
    ) = kept
    tokens = mid_in.shape[0]
    length = tokens // seq_dev
    d_out_in, d_gain_b, d_shift_b = norm_back(out_in, gain_b, shift_b, grad_out)
    d_down_low = d_out_in.astype(jnp.bfloat16)
    grad_down = multiply_left(active_low, d_down_low)
    d_lifted_low = gelu_back(lifted, multiply_right(d_down_low, weight_down)).astype(jnp.bfloat16)
    grad_up = multiply_left(middle_low, d_lifted_low)
    d_middle = d_out_in + multiply_right(d_lifted_low, weight_in[:, 4 * D :])
    d_mid_in, d_gain_a, d_shift_a = norm_back(mid_in, gain_a, shift_a, d_middle)
    d_attended_low = d_mid_in.astype(jnp.bfloat16)
    grad_out_proj = multiply_left(context_low, d_attended_low)
    d_context_low = multiply_right(d_attended_low, weight_in[:, 3 * D : 4 * D]).astype(jnp.bfloat16)
    heads_view = projected.reshape(seq_dev, length, 3, HEADS, HEAD_DIM)
    d_heads = jax.vmap(attend_back)(
        heads_view[:, :, 0],
        heads_view[:, :, 1],
        heads_view[:, :, 2],
        log_total,
        d_context_low.reshape(seq_dev, length, HEADS, HEAD_DIM),
    )
    d_projected_low = d_heads.reshape(tokens, 3 * D).astype(jnp.bfloat16)
    grad_joint = multiply_left(hidden_low, d_projected_low)
    d_hidden = d_mid_in + multiply_right(d_projected_low, weight_in[:, : 3 * D])
    joint_sums = jnp.sum(d_projected_low.astype(jnp.float32), axis=0)
    grad_pieces = jnp.concatenate(
        [
            joint_sums[:D],
            joint_sums[2 * D :],
            jnp.sum(d_attended_low.astype(jnp.float32), axis=0),
            d_gain_a,
            d_shift_a,
            jnp.sum(d_lifted_low.astype(jnp.float32), axis=0),
            jnp.sum(d_down_low.astype(jnp.float32), axis=0),
            d_gain_b,
            d_shift_b,
        ]
    )
    return (
        d_hidden,
        jnp.concatenate([grad_joint, grad_out_proj, grad_up], axis=1),
        grad_down,
        grad_pieces,
    )


def fetch_layer(in_low, down_low, layer_index):
    return (
        lax.all_gather(in_low[layer_index], ("fsdp", "dp"), axis=1, tiled=True),
        lax.all_gather(down_low[layer_index], ("fsdp", "dp"), axis=0, tiled=True),
    )


def refetch_layer(in_low, down_low, layer_index):
    return (
        lax.all_gather(in_low[layer_index], ("fsdp", "dp"), axis=1, tiled=True),
        lax.all_gather(down_low[layer_index], ("fsdp", "dp"), axis=0, tiled=True),
    )


def local(
    token_ids,
    labels,
    loss_mask,
    batch_of,
    layer_in,
    layer_down,
    word_table,
    side_mat,
    vectors,
    in_rows,
    in_cols,
    down_rows,
    down_cols,
    word_rows,
    word_cols,
    side_rows,
    side_cols,
    vec_moment,
):
    seq_dev, length = token_ids.shape
    tokens = seq_dev * length
    n_fsdp = lax.axis_size("fsdp")
    n_dp = lax.axis_size("dp")
    n_blocks = n_fsdp * n_dp
    my_index = lax.axis_index(("fsdp", "dp"))
    mask_float = loss_mask.astype(jnp.float32)
    member = (batch_of[:, None] == jnp.arange(MICRO)[None, :]).astype(jnp.float32)
    local_counts = jnp.sum(member * jnp.sum(mask_float, axis=1)[:, None], axis=0)
    counts = lax.psum(local_counts, ("fsdp", "dp"))
    seq_count = jnp.sum(member * counts[None, :], axis=1)
    token_weight = (mask_float / (seq_count * MICRO)[:, None]).reshape(tokens)
    label_float = labels.astype(jnp.float32).reshape(tokens)
    side_full, vector_full = (
        lax.all_gather(side_mat.astype(jnp.bfloat16), ("fsdp", "dp"), axis=0, tiled=True),
        lax.all_gather(vectors.astype(jnp.bfloat16), ("fsdp", "dp"), axis=0, tiled=True),
    )
    all_vectors = vector_full.astype(jnp.float32)
    pos_rows = side_full[:SEQ_LEN].astype(jnp.float32)
    head_mat = side_full[SEQ_LEN:]
    global_offset = LAYERS * (8 * D + FF)
    gain_emb = all_vectors[global_offset : global_offset + D]
    shift_emb = all_vectors[global_offset + D : global_offset + 2 * D]
    head_bias = all_vectors[global_offset + 2 * D : global_offset + 3 * D]
    predictor = all_vectors[global_offset + 3 * D : global_offset + 4 * D]
    predictor_low = vector_full[global_offset + 3 * D : global_offset + 4 * D]
    block_rows = word_table.shape[0]
    capacity = max(2, 2 * tokens // n_blocks)
    flat_ids = token_ids.reshape(tokens)
    blocks = flat_ids // block_rows
    onehot = (blocks[:, None] == jnp.arange(n_blocks)[None, :]).astype(jnp.int32)
    rank = jnp.sum(jnp.cumsum(onehot, axis=0) * onehot, axis=1) - 1
    slot = blocks * capacity + rank
    bucket_ids = jnp.full((n_blocks * capacity,), -1, jnp.int32).at[slot].set(flat_ids)
    asked = lax.all_to_all(
        lax.all_to_all(
            bucket_ids.reshape(n_fsdp, n_dp, capacity),
            "fsdp",
            split_axis=0,
            concat_axis=0,
            tiled=True,
        ),
        "dp",
        split_axis=1,
        concat_axis=1,
        tiled=True,
    )
    valid = (asked >= 0).reshape(-1)
    safe_row = jnp.clip(asked.reshape(-1) - my_index * block_rows, 0, block_rows - 1)
    found = jnp.take(word_table.astype(jnp.bfloat16), safe_row, axis=0)
    found = jnp.where(valid[:, None], found, jnp.zeros_like(found)).reshape(
        n_fsdp, n_dp, capacity, D
    )
    returned = lax.all_to_all(
        lax.all_to_all(found, "fsdp", split_axis=0, concat_axis=0, tiled=True),
        "dp",
        split_axis=1,
        concat_axis=1,
        tiled=True,
    )
    own_rows = jnp.take(returned.reshape(n_blocks * capacity, D), slot, axis=0).reshape(
        seq_dev, length, D
    )
    in_low = layer_in.astype(jnp.bfloat16)
    down_low = layer_down.astype(jnp.bfloat16)
    embedded = (own_rows.astype(jnp.float32) + pos_rows[None, :, :]).reshape(tokens, D)
    hidden = layer_norm(embedded, gain_emb, shift_emb)
    layer_index = 0
    fetched_in, fetched_down = fetch_layer(in_low, down_low, layer_index)
    hidden, kept = layer_forward(
        hidden, fetched_in, fetched_down, layer_slices(all_vectors, layer_index), seq_dev
    )
    kept_levels = [kept]
    final_low = hidden.astype(jnp.bfloat16)
    head_pre = multiply(final_low, head_mat) + head_bias
    head_act_low = exact_gelu(head_pre).astype(jnp.bfloat16)
    logits = multiply(head_act_low, predictor_low)
    local_loss = jnp.sum(token_weight * (jax.nn.softplus(logits) - label_float * logits))
    d_logits = token_weight * (jax.nn.sigmoid(logits) - label_float)
    d_predictor = jnp.sum(d_logits[:, None] * head_act_low.astype(jnp.float32), axis=0)
    d_head_low = gelu_back(head_pre, d_logits[:, None] * predictor[None, :]).astype(jnp.bfloat16)
    grad_head = multiply_left(final_low, d_head_low)
    d_head_bias = jnp.sum(d_head_low.astype(jnp.float32), axis=0)
    d_hidden = multiply_right(d_head_low, head_mat)
    layer_grads = [None] * LAYERS
    in_parts = [None] * LAYERS
    down_parts = [None] * LAYERS
    for layer_index in reversed(range(LAYERS)):
        fetched_in, fetched_down = refetch_layer(in_low, down_low, layer_index)
        d_hidden, grad_in_part, grad_down_part, grad_pieces = layer_backward(
            d_hidden,
            fetched_in,
            fetched_down,
            layer_slices(all_vectors, layer_index),
            kept_levels[layer_index],
            seq_dev,
        )
        in_parts[layer_index] = grad_in_part
        down_parts[layer_index] = grad_down_part
        layer_grads[layer_index] = grad_pieces
    d_embedded, d_gain_emb, d_shift_emb = norm_back(embedded, gain_emb, shift_emb, d_hidden)
    grad_pos = jnp.sum(d_embedded.reshape(seq_dev, length, D), axis=0)
    grad_vector = jnp.concatenate(layer_grads + [d_gain_emb, d_shift_emb, d_head_bias, d_predictor])
    grad_buckets = jnp.zeros((n_blocks * capacity, D), jnp.float32).at[slot].set(d_embedded)
    arrived = lax.all_to_all(
        lax.all_to_all(
            grad_buckets.reshape(n_fsdp, n_dp, capacity, D).astype(jnp.bfloat16),
            "fsdp",
            split_axis=0,
            concat_axis=0,
            tiled=True,
        ),
        "dp",
        split_axis=1,
        concat_axis=1,
        tiled=True,
    ).astype(jnp.float32)
    arrived = jnp.where(valid[:, None], arrived.reshape(-1, D), 0.0)
    grad_word = jax.ops.segment_sum(arrived, safe_row, num_segments=block_rows)
    grad_in, grad_down, grad_side, grad_vec = (
        lax.psum_scatter(jnp.stack(in_parts), ("fsdp", "dp"), scatter_dimension=2, tiled=True),
        lax.psum_scatter(jnp.stack(down_parts), ("fsdp", "dp"), scatter_dimension=1, tiled=True),
        lax.psum_scatter(
            jnp.concatenate([grad_pos, grad_head], axis=0),
            ("fsdp", "dp"),
            scatter_dimension=0,
            tiled=True,
        ),
        lax.psum_scatter(grad_vector, ("fsdp", "dp"), scatter_dimension=0, tiled=True),
    )
    col_local = layer_in.shape[2]
    col_global = my_index * col_local + jnp.arange(col_local)
    sub_onehot = jnp.stack(
        [col_global < 3 * D, (col_global >= 3 * D) & (col_global < 4 * D), col_global >= 4 * D],
        axis=1,
    ).astype(jnp.float32)
    sub_width = jnp.array([3 * D, D, FF], jnp.float32)
    square_in = grad_in * grad_in + tiny_square
    cols_new_in = decay_rate * in_cols + (1.0 - decay_rate) * jnp.mean(square_in, axis=1)
    row_part_in = jnp.einsum("lij,js->lsi", square_in, sub_onehot, precision=precise)
    square_down = grad_down * grad_down + tiny_square
    rows_new_down = decay_rate * down_rows + (1.0 - decay_rate) * jnp.mean(square_down, axis=2)
    col_part_down = jnp.sum(square_down, axis=1)
    total_part_down = jnp.sum(rows_new_down, axis=1)
    square_word = grad_word * grad_word + tiny_square
    rows_new_word = decay_rate * word_rows + (1.0 - decay_rate) * jnp.mean(square_word, axis=1)
    col_part_word = jnp.sum(square_word, axis=0)
    total_part_word = jnp.sum(rows_new_word)
    side_local = side_mat.shape[0]
    row_global = my_index * side_local + jnp.arange(side_local)
    which_mat = jnp.stack([row_global < SEQ_LEN, row_global >= SEQ_LEN], axis=1).astype(jnp.float32)
    side_counts = jnp.array([SEQ_LEN, D], jnp.float32)
    square_side = grad_side * grad_side + tiny_square
    rows_new_side = decay_rate * side_rows + (1.0 - decay_rate) * jnp.mean(square_side, axis=1)
    col_part_side = jnp.einsum("id,is->sd", square_side, which_mat, precision=precise)
    total_part_side = jnp.dot(rows_new_side, which_mat, precision=precise)
    vec_local = vectors.shape[0]
    seg_onehot = (
        segment_index(my_index * vec_local + jnp.arange(vec_local))[:, None]
        == jnp.arange(9 * LAYERS + 4)[None, :]
    ).astype(jnp.float32)
    new_moment = decay_rate * vec_moment + (1.0 - decay_rate) * (grad_vec * grad_vec + tiny_square)
    vec_update = grad_vec * lax.rsqrt(new_moment)
    seg_part = jnp.dot(vec_update * vec_update, seg_onehot, precision=precise)
    summed = lax.psum(
        (
            row_part_in,
            col_part_down,
            total_part_down,
            col_part_word,
            total_part_word,
            col_part_side,
            total_part_side,
            seg_part,
            local_loss,
        ),
        ("fsdp", "dp"),
    )
    (
        row_sum_in,
        col_sum_down,
        total_down,
        col_sum_word,
        total_word,
        col_sum_side,
        total_side,
        seg_squares,
        loss_total,
    ) = summed[:9]
    rows_new_in = decay_rate * in_rows + (1.0 - decay_rate) * row_sum_in / sub_width[None, :, None]
    mean_in = jnp.mean(rows_new_in, axis=2)
    row_sel_in = jnp.einsum("lsi,js->lij", rows_new_in, sub_onehot, precision=precise)
    mean_sel_in = jnp.einsum("ls,js->lj", mean_in, sub_onehot, precision=precise)
    update_in = grad_in * lax.rsqrt(row_sel_in * cols_new_in[:, None, :] / mean_sel_in[:, None, :])
    cols_new_down = decay_rate * down_cols + (1.0 - decay_rate) * col_sum_down / FF
    mean_down = total_down / FF
    update_down = grad_down * lax.rsqrt(
        rows_new_down[:, :, None] * cols_new_down[:, None, :] / mean_down[:, None, None]
    )
    cols_new_word = decay_rate * word_cols + (1.0 - decay_rate) * col_sum_word / VOCAB
    mean_word = total_word / VOCAB
    update_word = grad_word * lax.rsqrt(rows_new_word[:, None] * cols_new_word[None, :] / mean_word)
    cols_new_side = (
        decay_rate * side_cols + (1.0 - decay_rate) * col_sum_side / side_counts[:, None]
    )
    mean_side = total_side / side_counts
    col_sel_side = jnp.dot(which_mat, cols_new_side, precision=precise)
    mean_sel_side = jnp.dot(which_mat, mean_side, precision=precise)
    update_side = grad_side * lax.rsqrt(
        rows_new_side[:, None] * col_sel_side / mean_sel_side[:, None]
    )
    squares_in, squares_down, squares_word, squares_side = lax.psum(
        (
            jnp.einsum("lij,js->ls", update_in * update_in, sub_onehot, precision=precise),
            jnp.sum(update_down * update_down, axis=(1, 2)),
            jnp.sum(update_word * update_word),
            jnp.einsum("id,is->s", update_side * update_side, which_mat, precision=precise),
        ),
        ("fsdp", "dp"),
    )
    scale_in = jnp.maximum(1.0, jnp.sqrt(squares_in / (D * sub_width[None, :])))
    scale_sel_in = jnp.einsum("ls,js->lj", scale_in, sub_onehot, precision=precise)
    new_in = layer_in - learn_rate * update_in / scale_sel_in[:, None, :]
    scale_down = jnp.maximum(1.0, jnp.sqrt(squares_down / (FF * D)))
    new_down = layer_down - learn_rate * update_down / scale_down[:, None, None]
    scale_word = jnp.maximum(1.0, jnp.sqrt(squares_word / (VOCAB * D)))
    new_word = word_table - learn_rate * update_word / scale_word
    scale_side = jnp.maximum(1.0, jnp.sqrt(squares_side / (side_counts * D)))
    new_side = (
        side_mat
        - learn_rate * update_side / jnp.dot(which_mat, scale_side, precision=precise)[:, None]
    )
    seg_scale = jnp.maximum(1.0, jnp.sqrt(seg_squares / segment_sizes()))
    new_vectors = vectors - learn_rate * vec_update / jnp.dot(
        seg_onehot, seg_scale, precision=precise
    )
    return (
        loss_total,
        new_in,
        rows_new_in,
        cols_new_in,
        new_in.astype(jnp.bfloat16),
        new_down,
        rows_new_down,
        cols_new_down,
        new_down.astype(jnp.bfloat16),
        new_word,
        rows_new_word,
        cols_new_word,
        new_word.astype(jnp.bfloat16),
        new_side,
        rows_new_side,
        cols_new_side,
        new_side.astype(jnp.bfloat16),
        new_vectors,
        new_moment,
        new_vectors.astype(jnp.bfloat16),
    )


def solution(mesh):
    return jax.shard_map(
        local,
        mesh=mesh,
        in_specs=(
            P(("fsdp", "dp"), None),
            P(("fsdp", "dp"), None),
            P(("fsdp", "dp"), None),
            P(("fsdp", "dp")),
            P(None, None, ("fsdp", "dp")),
            P(None, ("fsdp", "dp"), None),
            P(("fsdp", "dp"), None),
            P(("fsdp", "dp"), None),
            P(("fsdp", "dp")),
            P(),
            P(None, ("fsdp", "dp")),
            P(None, ("fsdp", "dp")),
            P(),
            P(("fsdp", "dp")),
            P(),
            P(("fsdp", "dp")),
            P(),
            P(("fsdp", "dp")),
        ),
        out_specs=(
            P(),
            P(None, None, ("fsdp", "dp")),
            P(),
            P(None, ("fsdp", "dp")),
            P(None, None, ("fsdp", "dp")),
            P(None, ("fsdp", "dp"), None),
            P(None, ("fsdp", "dp")),
            P(),
            P(None, ("fsdp", "dp"), None),
            P(("fsdp", "dp"), None),
            P(("fsdp", "dp")),
            P(),
            P(("fsdp", "dp"), None),
            P(("fsdp", "dp"), None),
            P(("fsdp", "dp")),
            P(),
            P(("fsdp", "dp"), None),
            P(("fsdp", "dp")),
            P(("fsdp", "dp")),
            P(("fsdp", "dp")),
        ),
        check_vma=False,
    )
```

profile of v0, /device:TPU:0, one launch (start us, length us, event | category | flops | bytes accessed | tf_op | source)
XLA Modules:
  0.0 1342.4 jit_solution(17235930349054690688)
XLA Ops:
  51.6 78.3 %psum.98 = f32[2]{0:T(128)S(1)} all-reduce(f32[2]{0:T(128)S(1)} %compare_select_fusion.6), channel_id=1, replica_groups=mesh['fsdp'=16,'dp'=2] {'fsdp','dp'}, use_global_device_ids=true, to_apply=%region_1.0 | all-reduce | flops 2 | bytes 16 | tf_op jit(solution)/shard_map/psum | solution.py:265
  131.2 42.0 %all-gather.2 = bf16[32,1,512]{2,1,0:T(2,128)(2,1)S(1)} all-gather(bf16[1,1,512]{2,1,0:T(2,128)(2,1)S(1)} %reshape.854), channel_id=1, replica_groups=mesh['fsdp'=16,'dp'=2] {'fsdp','dp'}, dimensions={0}, use_global_device_ids=true | all-gather | bytes 33792 | tf_op jit(solution)/shard_map/all_gather | solution.py:271
  186.6 47.6 %all-gather.9.cloned.1.call-done = bf16[1,1024,8192]{2,1,0:T(8,128)(2,1)} async-done(((bf16[1,1024,256]{2,1,0:T(8,128)(2,1)}), bf16[1,1024,8192]{2,1,0:T(8,128)(2,1)}) %all-gather.9.cloned.1.call-update) | async-done | bytes 16777232 | tf_op jit(solution)/shard_map/all_gather | solution.py:224
  234.2 8.7 add_convert_fusion.1
  253.5 8.6 fusion
  275.4 26.7 %multiply_convert_fusion.1 = (bf16[512,4096]{1,0:T(8,128)(2,1)}, f32[512,4096]{1,0:T(8,128)}, f32[512,4096]{1,0:T(8,128)}) fusion(f32[4096]{0:T(1024)S(1)} %bitcast.252, bf16[1024,8192]{1,0:T(8,128)(2,1)} %bitcast.296, f32[512,1024]{1,0:T(8,128)S(1)} %get-tuple-element.204, f32[1024]{0:T(1024)S(1)} %bitcast.279, f32[1024]{0:T(1024)S(1)} %bitcast.257, ...), kind=kOutput, calls=%fused_computation.25 | convolution fusion | flops 4436000768 | bytes 31485952 | tf_op jit(solution)/shard_map/dot_general | solution.py:44
  302.2 10.8 all-gather.11.cloned.1.call-done
  313.0 10.0 fusion.186
  335.7 15.6 %convert_reduce_fusion = (f32[4096]{0:T(1024)}, bf16[512,4096]{1,0:T(8,128)(2,1)}) fusion(f32[512,4096]{1,0:T(8,128)} %get-tuple-element.180, bf16[512,1024]{1,0:T(8,128)(2,1)S(1)} %get-tuple-element.162, bf16[1,4096,1024]{2,1,0:T(8,128)(2,1)} %all-gather.11.cloned.1.call-done, f32[512,4096]{1,0:T(8,128)} %get-tuple-element.205, f32[4096]{0:T(1024)S(1)} %bitcast.253), kind=kOutput, calls=%fused_computation.22 | convolution fusion | flops 4330614784 | bytes 30441472 | tf_op jit(solution)/shard_map/dot_general | solution.py:54
  351.4 9.5 multiply_reduce_fusion.6
  370.8 11.7 multiply_reduce_fusion
  382.5 12.5 multiply_convert_fusion
  421.3 8.8 fusion.168
  442.6 10.4 convolution_bitcast_fusion
  457.8 8.8 fusion.158
  466.7 8.5 fusion.162
  475.2 21.3 %maximum_bitcast_fusion = f32[1,1024,8192]{2,1,0:T(8,128)} fusion(f32[1024,4096]{1,0:T(8,128)} %fusion.162, f32[1024,1024]{1,0:T(8,128)S(1)} %copy-done.17, f32[1024,3072]{1,0:T(8,128)} %fusion.158), kind=kLoop, calls=%fused_computation.5 | loop fusion | flops 16777216 | bytes 67108864 | tf_op jit(solution)/shard_map/stack | solution.py:376
  510.5 50.4 %all-reduce.5.cloned.1.call-done = f32[16384]{0:T(1024)} async-done(((f32[16384]{0:T(1024)}), f32[16384]{0:T(1024)}) %all-reduce.5.cloned.1.call-update) | async-done | bytes 65552
  567.7 11.6 scatter_custom_fusion.2
  583.0 97.6 %reduce-scatter.8.cloned.1.call-done = f32[48,1024]{1,0:T(8,128)} async-done(((f32[1536,1024]{1,0:T(8,128)}), f32[48,1024]{1,0:T(8,128)}) %reduce-scatter.8.cloned.1.call-update) | async-done | bytes 196624 | tf_op jit(solution)/shard_map/reduce_scatter | solution.py:378
  682.9 181.7 %reduce-scatter.6.cloned.1.call-done = f32[1,128,1024]{2,1,0:T(8,128)} async-done(((f32[1,4096,1024]{2,1,0:T(8,128)}), f32[1,128,1024]{2,1,0:T(8,128)}) %reduce-scatter.6.cloned.1.call-update) | async-done | bytes 524304 | tf_op jit(solution)/shard_map/reduce_scatter | solution.py:377
  866.4 356.6 %reduce-scatter.4.cloned.1.call-done = f32[1,1024,256]{2,1,0:T(8,128)} async-done(((f32[1,1024,8192]{2,1,0:T(8,128)}), f32[1,1024,256]{2,1,0:T(8,128)}) %reduce-scatter.4.cloned.1.call-update) | async-done | bytes 1048592 | tf_op jit(solution)/shard_map/reduce_scatter | solution.py:376
  1225.0 48.2 %all-reduce.2 = (f32[1,3,1024]{2,1,0:T(4,128)S(1)}, f32[1]{0:T(128)}, f32[1,1024]{1,0:T(1,128)S(1)}, f32[]{:T(128)}, f32[1024]{0:T(1024)S(1)}, /*index=5*/f32[2,1024]{1,0:T(2,128)S(1)}, f32[2]{0:T(128)S(1)}) all-reduce(f32[1,3,1024]{2,1,0:T(4,128)S(1)} %convolution_bitcast_fusion.1, ...), channel_id=1, replica_groups=mesh['fsdp'=16,'dp'=2] {'fsdp','dp'}, use_global_device_ids=true, to_apply=%region_23.24 | all-reduce | flops 7172 | bytes 57376 | tf_op jit(solution)/shard_map/psum | solution.py:420
  1283.3 39.8 %all-reduce.1 = (f32[]{:T(128)}, f32[1,3]{1,0:T(1,128)S(1)}, f32[1]{0:T(128)}, f32[]{:T(128)}, f32[2]{0:T(128)S(1)}, /*index=5*/f32[13]{0:T(128)S(1)}) all-reduce(f32[]{:T(128)} %get-tuple-element.199, f32[1,3]{1,0:T(1,128)S(1)} %fusion.189, f32[1]{0:T(128)} %bitcast.70, ...), channel_id=1, replica_groups=mesh['fsdp'=16,'dp'=2] {'fsdp','dp'}, use_global_device_ids=true, to_apply=%region_16.17 | all-reduce | flops 21 | bytes 168 | tf_op jit(solution)/shard_map/psum | solution.py:420
  (389 shorter events, 196.8 us)
Async XLA Ops:
  7.2 174.7 %all-gather.7.cloned.1.call-start = ((), (), s32[]{:S(2)}) async-start(), calls=%async_computation.9 | async-start | bytes 3244032 | tf_op jit(solution)/shard_map/all_gather | solution.py:270
  8.9 225.4 %all-gather.9.cloned.1.call-start = ((), (), s32[]{:S(2)}) async-start(), calls=%async_computation.13 | async-start | bytes 17301504 | tf_op jit(solution)/shard_map/all_gather | solution.py:224
  12.7 160.6 %copy-start.66 = (s32[512,1]{0,1:T(1,128)}, s32[512,1]{0,1:T(1,128)S(1)}, u32[]{:S(2)}) copy-start(s32[512,1]{0,1:T(1,128)S(1)} %compare_select_fusion.2) | copy-start | bytes 6148
  15.8 15.7 %all-to-all-start = ((s32[16,2,32]{2,1,0:T(2,128)}), s32[16,2,32]{2,1,0:T(2,128)S(1)}, u32[]{:S(2)}, u32[]{:S(2)}) async-start(s32[16,2,32]{2,1,0:T(2,128)} %reshape.796), calls=%async_computation | async-start | bytes 32768 | tf_op jit(solution)/shard_map/all_to_all | solution.py:291
  44.9 128.5 %all-to-all-start.2 = ((bf16[16,2,32,1024]{3,2,1,0:T(8,128)(2,1)}), bf16[16,2,32,1024]{3,2,1,0:T(8,128)(2,1)S(1)}, u32[]{:S(2)}, u32[]{:S(2)}) async-start(bf16[16,2,32,1024]{3,2,1,0:T(8,128)(2,1)} %select_select_fusion), calls=%async_computation.2 | async-start | bytes 4194304 | tf_op jit(solution)/shard_map/all_to_all | solution.py:310
  48.8 264.2 %all-gather.11.cloned.1.call-start = ((), (), s32[]{:S(2)}) async-start(), calls=%async_computation.14 | async-start | bytes 8650752 | tf_op jit(solution)/shard_map/all_gather | solution.py:225
  51.5 509.4 %all-reduce.5.cloned.1.call-start = ((), (), s32[]{:S(2)}) async-start(), calls=%async_computation.15 | async-start | bytes 131072
  173.3 150.1 %copy-start.81 = (f32[2,1,512]{2,1,0:T(1,128)}, f32[2,1,512]{2,1,0:T(1,128)S(1)}, u32[]{:S(2)}) copy-start(f32[2,1,512]{2,1,0:T(1,128)S(1)} %get-tuple-element.186) | copy-start | bytes 12292
  173.3 161.4 %copy-start.55 = (f32[2,1,512]{2,1,0:T(1,128)}, f32[2,1,512]{2,1,0:T(1,128)S(1)}, u32[]{:S(2)}) copy-start(f32[2,1,512]{2,1,0:T(1,128)S(1)} %get-tuple-element.185) | copy-start | bytes 12292
  173.3 187.6 %copy-start.53 = (f32[2,1,512]{2,1,0:T(1,128)}, f32[2,1,512]{2,1,0:T(1,128)S(1)}, u32[]{:S(2)}) copy-start(f32[2,1,512]{2,1,0:T(1,128)S(1)} %get-tuple-element.188) | copy-start | bytes 12292
  433.5 247.1 %reduce-scatter.8.cloned.1.call-start = ((), (), s32[]{:S(2)}) async-start(), calls=%async_computation.12 | async-start | bytes 6488064 | tf_op jit(solution)/shard_map/reduce_scatter | solution.py:378
  441.4 423.2 %reduce-scatter.6.cloned.1.call-start = ((), (), s32[]{:S(2)}) async-start(), calls=%async_computation.11 | async-start | bytes 17301504 | tf_op jit(solution)/shard_map/reduce_scatter | solution.py:377
  453.1 769.9 %reduce-scatter.4.cloned.1.call-start = ((), (), s32[]{:S(2)}) async-start(), calls=%async_computation.10 | async-start | bytes 34603008 | tf_op jit(solution)/shard_map/reduce_scatter | solution.py:376
  505.9 56.1 %all-to-all-start.4 = ((bf16[16,2,32,1024]{3,2,1,0:T(8,128)(2,1)}), bf16[16,2,32,1024]{3,2,1,0:T(8,128)(2,1)S(1)}, u32[]{:S(2)}, u32[]{:S(2)}) async-start(bf16[16,2,32,1024]{3,2,1,0:T(8,128)(2,1)} %bitcast.72), calls=%async_computation.6 | async-start | bytes 4194304 | tf_op jit(solution)/shard_map/all_to_all | solution.py:361
  561.7 772.3 %copy-start.68 = (f32[512]{0:T(512)}, f32[512]{0:T(512)S(1)}, u32[]{:S(2)}) copy-start(f32[512]{0:T(512)S(1)} %get-tuple-element.158) | copy-start | bytes 6148
  579.4 286.4 %copy-start.92 = (f32[1,128]{1,0:T(1,128)S(1)}, f32[1,128]{1,0:T(1,128)}, u32[]{:S(2)}) copy-start(f32[1,128]{1,0:T(1,128)} %param.32) | copy-start | bytes 1540
  579.4 693.8 %copy-start.91 = (f32[2]{0:T(128)S(1)}, f32[2]{0:T(128)}, u32[]{:S(2)}) copy-start(f32[2]{0:T(128)} %constant.178) | copy-start | bytes 28
  579.4 693.9 %copy-start.64 = (f32[2,1024]{1,0:T(2,128)S(1)}, f32[2,1024]{1,0:T(2,128)}, u32[]{:S(2)}) copy-start(f32[2,1024]{1,0:T(2,128)} %param.37) | copy-start | bytes 24580
  582.4 692.4 %copy-start.60 = (f32[1,3,1024]{2,0,1:T(1,128)S(1)}, f32[1,3,1024]{2,0,1:T(1,128)}, u32[]{:S(2)}) copy-start(f32[1,3,1024]{2,0,1:T(1,128)} %param.30) | copy-start | bytes 36868
  582.4 692.4 %copy-start.90 = (f32[3]{0:T(128)S(1)}, f32[3]{0:T(128)}, u32[]{:S(2)}) copy-start(f32[3]{0:T(128)} %constant.177) | copy-start | bytes 40
  582.4 693.5 %copy-start.88 = (f32[1,256]{1,0:T(1,128)S(1)}, f32[1,256]{1,0:T(1,128)}, u32[]{:S(2)}) copy-start(f32[1,256]{1,0:T(1,128)} %param.31) | copy-start | bytes 3076
  583.0 740.7 %copy-start.41 = (f32[960]{0:T(1024)}, f32[960]{0:T(1024)S(1)}, u32[]{:S(2)}) copy-start(f32[960]{0:T(1024)S(1)} %get-tuple-element.170) | copy-start | bytes 11524
  681.7 595.1 %copy-start.96 = (f32[48]{0:T(128)}, f32[48]{0:T(128)S(1)}, u32[]{:S(2)}) copy-start(f32[48]{0:T(128)S(1)} %multiply_add_fusion.16) | copy-start | bytes 580
  866.4 466.5 %copy-start.73 = (f32[1,128]{1,0:T(1,128)}, f32[1,128]{1,0:T(1,128)S(1)}, u32[]{:S(2)}) copy-start(f32[1,128]{1,0:T(1,128)S(1)} %get-tuple-element.172) | copy-start | bytes 1540
  (92 other events, 1982.3 us)
Sparse Core Ops, SparseCore 0:
  11.4 73.6 all-gather.6
  88.6 145.5 all-gather.8
  237.7 75.2 all-gather.10
  433.6 127.2 all-reduce.4
  566.4 114.1 reduce-scatter.7
  682.8 181.8 reduce-scatter.5
  866.9 356.0 reduce-scatter.3
where the time goes:
time: 1350 us; the launch traced here: 1340 us
  waiting for transfers between devices  750 us (56%)
  blocking collectives  223 us (17%)
  matrix products  180 us (13%)
  other arithmetic  115 us (9%)
  local copies, waits for them, and re-layouts  37.6 us (3%)
  between operations  19.9 us (1%)
  starting transfers between devices  16.8 us (1%)
    reduce_scatter x1, waiting for transfers between devices, local(): lax.psum_scatter(jnp.stack(in_parts), ('fsdp', 'dp'), scatter_dimension=2...  357 us
    reduce_scatter x1, waiting for transfers between devices, local(): lax.psum_scatter(jnp.stack(down_parts), ('fsdp', 'dp'), scatter_dimension...  182 us
    reduce_scatter x1, waiting for transfers between devices, local(): lax.psum_scatter(jnp.concatenate([grad_pos, grad_head], axis=0), ('fsdp',...  97.6 us
    psum x2, blocking collectives, local(): lax.psum((row_part_in, col_part_down, total_part_down, col_part_word, tot...  87.9 us
    psum x1, blocking collectives, local(): counts = lax.psum(local_counts, ('fsdp', 'dp'))  78.3 us
    dot_general x6, matrix products, multiply(): return jnp.dot(left_side, right_side, preferred_element_type=jnp.float32)  55.2 us
    unnamed x8, waiting for transfers between devices  50.5 us
    all_gather x1, waiting for transfers between devices, fetch_layer(): lax.all_gather(in_low[layer_index], ('fsdp', 'dp'), axis=1, tiled=True)  47.6 us
  transfers between devices with their start and end apart: 10, of which 7 were waited for; matrix products, arithmetic and copies ran while one was open for 14% of the time, Pallas kernels for 0%

commit v1 on v0

v1 whole, which is shorter than its diff:
```python
import functools
import math

import jax
import jax.numpy as jnp
from jax import lax
from jax.experimental import pallas as pl
from jax.experimental.pallas import tpu as pltpu
from jax.sharding import PartitionSpec as P

D = 1024
HEADS = 16
HEAD_DIM = 64
FF = 4096
VOCAB = 30720
SEQ_LEN = 512
LAYERS = 1
MICRO = 2
BOTH = ("fsdp", "dp")
LOW = jnp.bfloat16
MESH = pl.DeviceIdType.MESH
ALL = slice(None)


learn_rate = 0.02
decay_rate = 0.5
tiny_square = 1e-30
norm_epsilon = 1e-12
precise = lax.Precision.HIGHEST


def layer_norm(inputs, norm_gain, norm_shift):
    center = inputs - jnp.mean(inputs, axis=-1, keepdims=True)
    spread = jnp.mean(center * center, axis=-1, keepdims=True)
    return center * lax.rsqrt(spread + norm_epsilon) * norm_gain + norm_shift


def norm_back(inputs, norm_gain, norm_shift, cotangent):
    result, pull = jax.vjp(layer_norm, inputs, norm_gain, norm_shift)
    return pull(cotangent)


def exact_gelu(inputs):
    return jax.nn.gelu(inputs, approximate=False)


def gelu_back(inputs, cotangent):
    result, pull = jax.vjp(exact_gelu, inputs)
    return pull(cotangent)[0]


def multiply(left_side, right_side):
    return jnp.dot(left_side, right_side, preferred_element_type=jnp.float32)


def multiply_left(left_side, right_side):
    return lax.dot_general(
        left_side, right_side, (((0,), (0,)), ((), ())), preferred_element_type=jnp.float32
    )


def multiply_right(left_side, right_side):
    return lax.dot_general(
        left_side, right_side, (((1,), (1,)), ((), ())), preferred_element_type=jnp.float32
    )


def piece_bounds():
    return [0, D, 2 * D, 3 * D, 4 * D, 5 * D, 5 * D + FF, 6 * D + FF, 7 * D + FF, 8 * D + FF]


def layer_slices(all_vectors, layer_index):
    bounds = piece_bounds()
    offset = layer_index * (8 * D + FF)
    return [
        all_vectors[offset + bounds[slot_index] : offset + bounds[slot_index + 1]]
        for slot_index in range(9)
    ]


def segment_index(position):
    piece_width = 8 * D + FF
    inner = position % piece_width
    layer_of = position // piece_width
    bounds = piece_bounds()[1:-1]
    local_segment = sum(((inner >= bound).astype(jnp.int32) for bound in bounds))
    tail = 9 * LAYERS + (position - LAYERS * piece_width) // D
    return jnp.where(position < LAYERS * piece_width, 9 * layer_of + local_segment, tail)


def segment_sizes():
    sizes = []
    sizes = sizes + [D, D, D, D, D, FF, D, D, D]
    return jnp.array(sizes + [D, D, D, D], jnp.float32)


def attend(queries, key_rows, values):
    scores = jnp.einsum(
        "qhe,khe->hqk", queries, key_rows, preferred_element_type=jnp.float32
    ) * HEAD_DIM ** (-0.5)
    peak_score = jnp.max(scores, axis=-1, keepdims=True)
    exponent = jnp.exp(scores - peak_score)
    running = jnp.sum(exponent, axis=-1, keepdims=True)
    soft_probs = exponent / running
    context = jnp.einsum(
        "hqk,khe->qhe", soft_probs.astype(jnp.bfloat16), values, preferred_element_type=jnp.float32
    )
    return (context, peak_score + jnp.log(running))


def attend_back(queries, key_rows, values, log_total, d_context):
    score_scale = HEAD_DIM ** (-0.5)
    scores = (
        jnp.einsum("qhe,khe->hqk", queries, key_rows, preferred_element_type=jnp.float32)
        * score_scale
    )
    soft_probs = jnp.exp(scores - log_total)
    d_values = jnp.einsum(
        "hqk,qhe->khe",
        soft_probs.astype(jnp.bfloat16),
        d_context,
        preferred_element_type=jnp.float32,
    )
    d_probs = jnp.einsum("qhe,khe->hqk", d_context, values, preferred_element_type=jnp.float32)
    d_scores = soft_probs * (d_probs - jnp.sum(d_probs * soft_probs, axis=-1, keepdims=True))
    d_scores_low = d_scores.astype(jnp.bfloat16)
    d_queries = (
        jnp.einsum("hqk,khe->qhe", d_scores_low, key_rows, preferred_element_type=jnp.float32)
        * score_scale
    )
    d_keys = (
        jnp.einsum("hqk,qhe->khe", d_scores_low, queries, preferred_element_type=jnp.float32)
        * score_scale
    )
    return jnp.stack([d_queries, d_keys, d_values], axis=1)


def layer_forward(hidden, weight_in, weight_down, pieces, seq_dev):
    bias_q, bias_v, bias_o, gain_a, shift_a, bias_up, bias_down, gain_b, shift_b = pieces
    tokens = hidden.shape[0]
    length = tokens // seq_dev
    hidden_low = hidden.astype(jnp.bfloat16)
    joint_bias = jnp.concatenate([bias_q, jnp.zeros_like(bias_q), bias_v])
    projected = (multiply_right(hidden_low, weight_in[: 3 * D]) + joint_bias).astype(jnp.bfloat16)
    heads_view = projected.reshape(seq_dev, length, 3, HEADS, HEAD_DIM)
    context, log_total = jax.vmap(attend)(
        heads_view[:, :, 0], heads_view[:, :, 1], heads_view[:, :, 2]
    )
    context_low = context.reshape(tokens, D).astype(jnp.bfloat16)
    mid_in = hidden + (multiply_right(context_low, weight_in[3 * D : 4 * D]) + bias_o)
    middle = layer_norm(mid_in, gain_a, shift_a)
    middle_low = middle.astype(jnp.bfloat16)
    lifted = multiply_right(middle_low, weight_in[4 * D :]) + bias_up
    active_low = exact_gelu(lifted).astype(jnp.bfloat16)
    out_in = middle + (multiply(active_low, weight_down) + bias_down)
    output = layer_norm(out_in, gain_b, shift_b)
    return (
        output,
        (
            hidden_low,
            projected,
            log_total,
            context_low,
            mid_in,
            middle_low,
            lifted,
            active_low,
            out_in,
        ),
    )


def layer_backward(grad_out, weight_in, weight_down, pieces, kept, seq_dev):
    bias_q, bias_v, bias_o, gain_a, shift_a, bias_up, bias_down, gain_b, shift_b = pieces
    (
        hidden_low,
        projected,
        log_total,
        context_low,
        mid_in,
        middle_low,
        lifted,
        active_low,
        out_in,
    ) = kept
    tokens = mid_in.shape[0]
    length = tokens // seq_dev
    d_out_in, d_gain_b, d_shift_b = norm_back(out_in, gain_b, shift_b, grad_out)
    d_down_low = d_out_in.astype(jnp.bfloat16)
    grad_down = multiply_left(active_low, d_down_low)
    d_lifted_low = gelu_back(lifted, multiply_right(d_down_low, weight_down)).astype(jnp.bfloat16)
    grad_up = multiply_left(d_lifted_low, middle_low)
    d_middle = d_out_in + multiply(d_lifted_low, weight_in[4 * D :])
    d_mid_in, d_gain_a, d_shift_a = norm_back(mid_in, gain_a, shift_a, d_middle)
    d_attended_low = d_mid_in.astype(jnp.bfloat16)
    grad_out_proj = multiply_left(d_attended_low, context_low)
    d_context_low = multiply(d_attended_low, weight_in[3 * D : 4 * D]).astype(jnp.bfloat16)
    heads_view = projected.reshape(seq_dev, length, 3, HEADS, HEAD_DIM)
    d_heads = jax.vmap(attend_back)(
        heads_view[:, :, 0],
        heads_view[:, :, 1],
        heads_view[:, :, 2],
        log_total,
        d_context_low.reshape(seq_dev, length, HEADS, HEAD_DIM),
    )
    d_projected_low = d_heads.reshape(tokens, 3 * D).astype(jnp.bfloat16)
    grad_joint = multiply_left(d_projected_low, hidden_low)
    d_hidden = d_mid_in + multiply(d_projected_low, weight_in[: 3 * D])
    joint_sums = jnp.sum(d_projected_low.astype(jnp.float32), axis=0)
    grad_pieces = jnp.concatenate(
        [
            joint_sums[:D],
            joint_sums[2 * D :],
            jnp.sum(d_attended_low.astype(jnp.float32), axis=0),
            d_gain_a,
            d_shift_a,
            jnp.sum(d_lifted_low.astype(jnp.float32), axis=0),
            jnp.sum(d_down_low.astype(jnp.float32), axis=0),
            d_gain_b,
            d_shift_b,
        ]
    )
    return (
        d_hidden,
        [grad_joint, grad_out_proj, grad_up],
        grad_down,
        grad_pieces,
    )


def place():
    block = lax.axis_index("fsdp")
    return block // 4, (block // 2) % 2, block % 2, lax.axis_index("dp")


def device(z, y, x, c):
    return ((z * 2 + y) * 2 + x, c)


def my_rank():
    return lax.axis_index("fsdp") * 2 + lax.axis_index("dp")


def by_rank(index):
    return (index // 2, index % 2)


def neighbours(z, y, x, c):
    return (
        device(z, y, 1 - x, c),
        device(z, 1 - y, x, c),
        device(z, y, x, 1 - c),
        [device((z + k) % 4, y, x, c) for k in (1, 2, 3)],
    )


def enter(n):
    me = my_rank()
    barrier = pltpu.get_barrier_semaphore()

    def greet(step, carry):
        pl.semaphore_signal(
            barrier, inc=1, device_id=by_rank((me + step) % n), device_id_type=MESH
        )
        return carry

    lax.fori_loop(1, n, greet, 0)
    pl.semaphore_wait(barrier, n - 1)


class Copies:
    def __init__(self, send, recv):
        self.send, self.recv, self.begun = send, recv, []

    def start(self, src, dst, target):
        slot = len(self.begun)
        copy = pltpu.make_async_remote_copy(
            src_ref=src,
            dst_ref=dst,
            send_sem=self.send.at[slot],
            recv_sem=self.recv.at[slot],
            device_id=target,
            device_id_type=MESH,
        )
        copy.start()
        self.begun.append(copy)
        return copy

    def drain(self):
        for copy in self.begun:
            copy.wait_send()


def exchange_copy(src, dst, send, recv, step, n):
    me = my_rank()
    target = (me + step) % n
    return pltpu.make_async_remote_copy(
        src_ref=src.at[target],
        dst_ref=dst.at[me],
        send_sem=send.at[step],
        recv_sem=recv.at[step],
        device_id=by_rank(target),
        device_id_type=MESH,
    )


def exchange_start(src, dst, send, recv, n):
    def begin(step, carry):
        exchange_copy(src, dst, send, recv, step, n).start()
        return carry

    lax.fori_loop(1, n, begin, 0)


def exchange_wait(src, dst, send, recv, n):
    def finish(step, carry):
        exchange_copy(src, dst, send, recv, step, n).wait()
        return carry

    lax.fori_loop(1, n, finish, 0)


def pipeline(order, chunks):
    live = [iter(chunk) for chunk in chunks]
    for index in order:
        next(live[index], None)


def gather_order(plan):
    first = [i for i, p in enumerate(plan) if p[3]]
    rest = [i for i, p in enumerate(plan) if not p[3]]
    order = first + rest + first + first
    for step in range(len(rest) + 4):
        order += [rest[i] for i in range(min(step, len(rest) - 1), -1, -1) if 0 <= step - i < 4]
    return order + first + first


def gather_kernel(plan, count, *refs):
    local, out = refs[:count], refs[count + 1 : 2 * count + 1]
    found, rows = refs[count], refs[2 * count + 1]
    send, recv, own_sem, row_send, row_recv = refs[2 * count + 2 :]
    z, y, x, c = place()
    n = 32
    me = my_rank()
    enter(n)
    copies = Copies(send, recv)
    own = []
    for i in range(count):
        own.append(pltpu.make_async_copy(local[i], out[i].at[z, y, x, c], own_sem.at[i]))
    own.append(pltpu.make_async_copy(found.at[me], rows.at[me], own_sem.at[count]))
    for copy in own:
        copy.start()
    to_x, to_y, to_core, to_z = neighbours(z, y, x, c)

    def pass_on(ref, where, target):
        return copies.start(ref.at[where], ref.at[where], target)

    landed = set()

    def own_there(i):
        if i not in landed:
            own[i].wait()
            landed.add(i)

    def chunk(i, start, size, plane_first):
        ref, mine, half = out[i], local[i], size // 2
        part, low, high = pl.ds(start, size), pl.ds(start, half), pl.ds(start + half, half)
        last = []
        if not plane_first:
            along = [copies.start(mine.at[part], ref.at[z, y, x, c, part], t) for t in to_z]
            yield
            for copy in along:
                copy.wait_recv()
            own_there(i)
            first = pass_on(ref, (ALL, y, x, c, low), to_x)
            second = pass_on(ref, (ALL, y, x, c, high), to_y)
            last.append(pass_on(ref, (ALL, y, x, c, part), to_core))
            yield
            first.wait_recv()
            second.wait_recv()
            first = pass_on(ref, (ALL, y, ALL, c, low), to_y)
            second = pass_on(ref, (ALL, ALL, x, c, high), to_x)
            last.append(pass_on(ref, (ALL, y, 1 - x, c, low), to_core))
            last.append(pass_on(ref, (ALL, 1 - y, x, c, high), to_core))
            yield
            first.wait_recv()
            second.wait_recv()
            last.append(pass_on(ref, (ALL, 1 - y, ALL, c, low), to_core))
            last.append(pass_on(ref, (ALL, ALL, 1 - x, c, high), to_core))
        else:
            first = copies.start(mine.at[low], ref.at[z, y, x, c, low], to_x)
            second = copies.start(mine.at[high], ref.at[z, y, x, c, high], to_y)
            last.append(copies.start(mine.at[part], ref.at[z, y, x, c, part], to_core))
            yield
            first.wait_recv()
            second.wait_recv()
            own_there(i)
            first = pass_on(ref, (z, y, ALL, c, low), to_y)
            second = pass_on(ref, (z, ALL, x, c, high), to_x)
            last.append(pass_on(ref, (z, y, 1 - x, c, low), to_core))
            last.append(pass_on(ref, (z, 1 - y, x, c, high), to_core))
            yield
            first.wait_recv()
            second.wait_recv()
            along = [pass_on(ref, (z, ALL, ALL, c, part), t) for t in to_z]
            last.append(pass_on(ref, (z, 1 - y, ALL, c, low), to_core))
            last.append(pass_on(ref, (z, ALL, 1 - x, c, high), to_core))
            yield
            for k in (1, 2, 3):
                along[k - 1].wait_recv()
                last.append(pass_on(ref, ((z + 4 - k) % 4, ALL, ALL, c, part), to_core))
        yield
        for copy in last:
            copy.wait_recv()
        yield

    chunks = [chunk(*p) for p in plan]
    exchange_start(found, rows, row_send, row_recv, n)
    pipeline(gather_order(plan), chunks)
    for live in chunks:
        next(live, None)
    exchange_wait(found, rows, row_send, row_recv, n)
    copies.drain()
    for i in range(count + 1):
        own_there(i)


def gather_plan(heights, plane_rows):
    plan = []
    for i, height in enumerate(heights):
        start = 0
        for size in plane_rows.get(i, ()):
            plan.append((i, start, size, True))
            start += size
        while start < height:
            size = 64 if height - start >= 64 else height - start
            plan.append((i, start, size, False))
            start += size
    return plan


def gather_weights(arrays, found):
    count = len(arrays)
    plan = gather_plan([a.shape[0] for a in arrays], {1: (32,)})
    total = sum(15 if p[3] else 12 for p in plan)
    hbm = pl.BlockSpec(memory_space=pl.ANY)
    vmem = pl.BlockSpec(memory_space=pltpu.VMEM)
    dma = pltpu.SemaphoreType.DMA
    return pl.pallas_call(
        functools.partial(gather_kernel, plan, count),
        name="gather_weights",
        out_shape=tuple(jax.ShapeDtypeStruct((4, 2, 2, 2) + a.shape, a.dtype) for a in arrays)
        + (jax.ShapeDtypeStruct(found.shape, found.dtype),),
        in_specs=[vmem] * count + [hbm],
        out_specs=tuple([hbm] * (count + 1)),
        scratch_shapes=[dma((total,)), dma((total,)), dma((count + 1,)), dma((32,)), dma((32,))],
        compiler_params=pltpu.CompilerParams(collective_id=0, has_side_effects=True),
    )(*arrays, found)


def add_blocks(dst, other, shape, at_dst, at_other):
    def body(index, carry):
        where = []
        for extent in reversed(shape):
            where.append(index % extent)
            index = index // extent
        where = tuple(reversed(where))
        d, o = at_dst(*where), at_other(*where)
        total = dst[d].astype(jnp.float32) + other[o].astype(jnp.float32)
        dst[d] = total.astype(dst.dtype)
        return carry

    lax.fori_loop(0, math.prod(shape), body, 0)


def scatter_kernel(plan, count, *refs):
    grads, buckets, vector = refs[:count], refs[count], refs[count + 1]
    out = refs[count + 2 : 2 * count + 2]
    arrived, vector_all = refs[2 * count + 2 : 2 * count + 4]
    rest = refs[2 * count + 4 :]
    scratch = [rest[7 * i : 7 * i + 7] for i in range(count)]
    send, recv, load, own_sem, row_send, row_recv, vec_send, vec_recv = rest[7 * count :]
    z, y, x, c = place()
    n = 32
    me = my_rank()
    enter(n)
    copies = Copies(send, recv)
    to_x, to_y, to_core, to_z = neighbours(z, y, x, c)
    own = [
        pltpu.make_async_copy(buckets.at[me], arrived.at[me], own_sem.at[0]),
        pltpu.make_async_copy(vector.at[me], vector_all.at[me], own_sem.at[1]),
    ]
    for copy in own:
        copy.start()

    def chunk(slot, i, start, low_size, high_size):
        held, from_core, low_1, high_1, low_2, high_2, from_z = scratch[i]
        grad, size = grads[i], low_size + high_size
        part = pl.ds(start, size)
        low, high = pl.ds(start, low_size), pl.ds(start + low_size, high_size)
        core = copies.start(grad.at[:, :, :, 1 - c, part], from_core.at[:, :, :, part], to_core)
        mine = pltpu.make_async_copy(
            grad.at[:, :, :, c, part], held.at[:, :, :, part], load.at[slot]
        )
        mine.start()
        yield
        mine.wait()
        core.wait_recv()

        add_blocks(
            held,
            from_core,
            (4, 2, 2),
            lambda a, b, d: (a, b, d, part),
            lambda a, b, d: (a, b, d, part),
        )
        first = copies.start(held.at[:, 1 - y, :, low], low_1.at[:, :, low], to_y)
        second = copies.start(held.at[:, :, 1 - x, high], high_1.at[:, :, high], to_x)
        yield
        first.wait_recv()
        second.wait_recv()
        add_blocks(
            held, low_1, (4, 2), lambda a, d: (a, y, d, low), lambda a, d: (a, d, low)
        )
        add_blocks(
            held, high_1, (4, 2), lambda a, b: (a, b, x, high), lambda a, b: (a, b, high)
        )
        first = copies.start(held.at[:, y, 1 - x, low], low_2.at[:, low], to_x)
        second = copies.start(held.at[:, 1 - y, x, high], high_2.at[:, high], to_y)
        yield
        first.wait_recv()
        second.wait_recv()
        add_blocks(held, low_2, (4,), lambda a: (a, y, x, low), lambda a: (a, low))
        add_blocks(held, high_2, (4,), lambda a: (a, y, x, high), lambda a: (a, high))
        along = [
            copies.start(held.at[(z + k) % 4, y, x, part], from_z.at[k - 1, part], to_z[k - 1])
            for k in (1, 2, 3)
        ]
        yield
        for copy in along:
            copy.wait_recv()
        total = held[z, y, x, part].astype(jnp.float32)
        for k in range(3):
            total = total + from_z[k, part].astype(jnp.float32)
        out[i][part] = total
        yield

    chunks = [chunk(slot, *p) for slot, p in enumerate(plan)]
    order = list(range(len(plan)))
    for step in range(len(plan) + 4):
        order += [i for i in range(min(step, len(plan) - 1), -1, -1) if 0 <= step - i < 4]
    exchange_start(vector, vector_all, vec_send, vec_recv, n)
    live = [iter(one) for one in chunks]
    for index in order[: len(plan)]:
        next(live[index])
    exchange_start(buckets, arrived, row_send, row_recv, n)
    for index in order[len(plan) :]:
        next(live[index])
    exchange_wait(vector, vector_all, vec_send, vec_recv, n)
    exchange_wait(buckets, arrived, row_send, row_recv, n)
    copies.drain()
    for copy in own:
        copy.wait()


def scatter_plan(heights):
    plan = []
    for i, height in enumerate(heights):
        start = 0
        while start < height:
            size = min(64, height - start)
            low = (size // 2 + 15) // 16 * 16
            plan.append((i, start, low, size - low))
            start += size
    return plan


def scatter_grads(arrays, buckets, vector):
    count = len(arrays)
    heights = [a.shape[4] for a in arrays]
    plan = scatter_plan(heights)
    total = 8 * len(plan)
    hbm = pl.BlockSpec(memory_space=pl.ANY)
    vmem = pl.BlockSpec(memory_space=pltpu.VMEM)
    dma = pltpu.SemaphoreType.DMA
    scratch = []
    for h in heights:
        for lead in ((4, 2, 2), (4, 2, 2), (4, 2), (4, 2), (4,), (4,), (3,)):
            scratch.append(pltpu.VMEM(lead + (h, D), LOW))
    return pl.pallas_call(
        functools.partial(scatter_kernel, plan, count),
        name="scatter_grads",
        out_shape=tuple(jax.ShapeDtypeStruct((h, D), jnp.float32) for h in heights)
        + (
            jax.ShapeDtypeStruct(buckets.shape, buckets.dtype),
            jax.ShapeDtypeStruct(vector.shape, vector.dtype),
        ),
        in_specs=[hbm] * (count + 2),
        out_specs=tuple([vmem] * count + [hbm, hbm]),
        scratch_shapes=scratch
        + [
            dma((total,)),
            dma((total,)),
            dma((len(plan),)),
            dma((2,)),
            dma((32,)),
            dma((32,)),
            dma((32,)),
            dma((32,)),
        ],
        compiler_params=pltpu.CompilerParams(
            collective_id=1, has_side_effects=True, vmem_limit_bytes=60 * 1024 * 1024
        ),
    )(*arrays, buckets, vector)


def sum_kernel(values, out, landed, total, send, recv, send_again, recv_again):
    n = 32
    me = my_rank()
    enter(n)
    exchange_start(values, landed, send, recv, n)
    landed[me] = values[me]
    exchange_wait(values, landed, send, recv, n)

    def add(index, carry):
        return carry + landed[index]

    total[...] = lax.fori_loop(0, n, add, jnp.zeros(total.shape, jnp.float32))
    out[me] = total[...]

    def copy(step):
        target = (me + step) % n
        return pltpu.make_async_remote_copy(
            src_ref=total,
            dst_ref=out.at[me],
            send_sem=send_again.at[step],
            recv_sem=recv_again.at[step],
            device_id=by_rank(target),
            device_id_type=MESH,
        )

    def begin(step, carry):
        copy(step).start()
        return carry

    def finish(step, carry):
        copy(step).wait()
        return carry

    lax.fori_loop(1, n, begin, 0)
    lax.fori_loop(1, n, finish, 0)


def sum_over_devices(flat):
    n = lax.axis_size(BOTH)
    if not special():
        return lax.psum(flat, BOTH)
    unit = n * 128
    lines = -(-flat.shape[0] // unit)
    values = jnp.pad(flat, (0, lines * unit - flat.shape[0])).reshape(n, lines, 128)
    vmem = pl.BlockSpec(memory_space=pltpu.VMEM)
    dma = pltpu.SemaphoreType.DMA
    result = pl.pallas_call(
        sum_kernel,
        name="sum_over_devices",
        out_shape=jax.ShapeDtypeStruct(values.shape, jnp.float32),
        in_specs=[vmem],
        out_specs=vmem,
        scratch_shapes=[
            pltpu.VMEM(values.shape, jnp.float32),
            pltpu.VMEM(values.shape[1:], jnp.float32),
            dma((n,)),
            dma((n,)),
            dma((n,)),
            dma((n,)),
        ],
        compiler_params=pltpu.CompilerParams(collective_id=2, has_side_effects=True),
    )(values)
    return result.reshape(-1)[: flat.shape[0]]


def special():
    return lax.axis_size("fsdp") == 16 and lax.axis_size("dp") == 2


def swap(blocks):
    shape = blocks.shape
    n_fsdp, n_dp = lax.axis_size("fsdp"), lax.axis_size("dp")
    split = blocks.reshape((n_fsdp, n_dp) + shape[1:])
    half = lax.all_to_all(split, "fsdp", split_axis=0, concat_axis=0, tiled=True)
    return lax.all_to_all(half, "dp", split_axis=1, concat_axis=1, tiled=True).reshape(shape)

def gather_blocks(arrays, found):
    if special():
        gathered = gather_weights(arrays, found)
        return [g.reshape((-1, a.shape[-1])) for g, a in zip(gathered, arrays)], gathered[-1]
    full = [lax.all_gather(a, BOTH, axis=0, tiled=True) for a in arrays]
    return full, swap(found)


def reduce_blocks(grads, buckets, vector):
    n = lax.axis_size(BOTH)
    if special():
        blocks = [g.astype(LOW).reshape(4, 2, 2, 2, -1, g.shape[-1]) for g in grads]
        shaped = vector.reshape(n, -1, 128)
        *parts, arrived, pieces = scatter_grads(blocks, buckets, shaped)
        return parts, arrived, jnp.sum(pieces, axis=0).reshape(-1)
    parts = [
        lax.psum_scatter(g.astype(jnp.float32), BOTH, scatter_dimension=0, tiled=True)
        for g in grads
    ]
    return (
        parts,
        swap(buckets),
        lax.psum_scatter(vector, BOTH, scatter_dimension=0, tiled=True),
    )


def factor_stats(gradient, rows_new):
    square = gradient * gradient
    return jnp.sum(square + tiny_square, axis=0), jnp.sum(square / rows_new[:, None], axis=0)


def clip_of(weighted, cols_new, mean_rows, size):
    mean_square = jnp.sum(weighted / cols_new, axis=-1) * mean_rows / size
    return jnp.maximum(1.0, jnp.sqrt(mean_square))


def local(
    token_ids,
    labels,
    loss_mask,
    batch_of,
    layer_in,
    layer_down,
    word_table,
    side_mat,
    vectors,
    in_rows,
    in_cols,
    down_rows,
    down_cols,
    word_rows,
    word_cols,
    side_rows,
    side_cols,
    vec_moment,
):
    seq_dev, length = token_ids.shape
    tokens = seq_dev * length
    n_blocks = lax.axis_size(BOTH)
    my_index = lax.axis_index(BOTH)
    mask_float = loss_mask.astype(jnp.float32)
    member = batch_of[:, None] == jnp.arange(MICRO)[None, :]
    local_counts = jnp.sum(member * jnp.sum(loss_mask, axis=1)[:, None], axis=0)
    block_rows = word_table.shape[0]
    capacity = max(2, 2 * tokens // n_blocks)
    flat_ids = token_ids.reshape(tokens)
    blocks = flat_ids // block_rows
    onehot = (blocks[:, None] == jnp.arange(n_blocks)[None, :]).astype(jnp.int32)
    rank = jnp.sum(jnp.cumsum(onehot, axis=0) * onehot, axis=1) - 1
    slot = blocks * capacity + rank
    bucket_ids = jnp.full((n_blocks * capacity,), -1, jnp.int32).at[slot].set(flat_ids)
    message = jnp.concatenate(
        [
            bucket_ids.reshape(n_blocks, capacity),
            jnp.broadcast_to(local_counts.astype(jnp.int32)[None, :], (n_blocks, MICRO)),
        ],
        axis=1,
    )
    answer = swap(message)
    asked = answer[:, :capacity].reshape(-1)
    counts = jnp.sum(answer[:, capacity:], axis=0).astype(jnp.float32)
    asked_row = jnp.where(asked >= 0, asked - my_index * block_rows, -1)
    found = jnp.take(
        word_table.astype(LOW), jnp.clip(asked_row, 0, block_rows - 1), axis=0
    ).reshape(n_blocks, capacity, D)
    seq_count = jnp.sum(member * counts[None, :], axis=1)
    token_weight = (mask_float / (seq_count * MICRO)[:, None]).reshape(tokens)
    label_float = labels.astype(jnp.float32).reshape(tokens)

    side_rows_local = side_mat.shape[0]
    vec_local = vectors.shape[0]
    vector_row = jnp.pad(vectors.astype(LOW).reshape(1, -1), ((0, 15), (0, D - vec_local)))
    (side_all, weight_in, weight_down), returned = gather_blocks(
        [
            jnp.concatenate([side_mat.astype(LOW), vector_row], axis=0),
            layer_in[0].astype(LOW).T,
            layer_down[0].astype(LOW),
        ],
        found,
    )
    side_all = side_all.reshape(n_blocks, side_rows_local + 16, D)
    side_full = side_all[:, :side_rows_local].reshape(-1, D)
    vector_full = side_all[:, side_rows_local, :vec_local].reshape(-1)
    all_vectors = vector_full.astype(jnp.float32)
    pos_rows = side_full[:SEQ_LEN].astype(jnp.float32)
    head_mat = side_full[SEQ_LEN:]
    global_offset = LAYERS * (8 * D + FF)
    gain_emb = all_vectors[global_offset : global_offset + D]
    shift_emb = all_vectors[global_offset + D : global_offset + 2 * D]
    head_bias = all_vectors[global_offset + 2 * D : global_offset + 3 * D]
    predictor = all_vectors[global_offset + 3 * D : global_offset + 4 * D]
    predictor_low = vector_full[global_offset + 3 * D : global_offset + 4 * D]
    to_slot = (slot[:, None] == jnp.arange(n_blocks * capacity)[None, :]).astype(LOW)
    own_rows = multiply(to_slot, returned.reshape(n_blocks * capacity, D))
    embedded = (own_rows.reshape(seq_dev, length, D) + pos_rows[None, :, :]).reshape(tokens, D)
    hidden = layer_norm(embedded, gain_emb, shift_emb)
    pieces = layer_slices(all_vectors, 0)
    hidden, kept = layer_forward(hidden, weight_in, weight_down, pieces, seq_dev)
    final_low = hidden.astype(LOW)
    head_pre = multiply(final_low, head_mat) + head_bias
    head_act_low = exact_gelu(head_pre).astype(LOW)
    logits = multiply(head_act_low, predictor_low)
    local_loss = jnp.sum(token_weight * (jax.nn.softplus(logits) - label_float * logits))
    d_logits = token_weight * (jax.nn.sigmoid(logits) - label_float)
    d_predictor = jnp.sum(d_logits[:, None] * head_act_low.astype(jnp.float32), axis=0)
    d_head_low = gelu_back(head_pre, d_logits[:, None] * predictor[None, :]).astype(LOW)
    grad_head = multiply_left(final_low, d_head_low)
    d_head_bias = jnp.sum(d_head_low.astype(jnp.float32), axis=0)
    d_hidden = multiply_right(d_head_low, head_mat)
    d_hidden, grads_in, grad_down, grad_pieces = layer_backward(
        d_hidden, weight_in, weight_down, pieces, kept, seq_dev
    )
    d_embedded, d_gain_emb, d_shift_emb = norm_back(embedded, gain_emb, shift_emb, d_hidden)
    grad_pos = jnp.sum(d_embedded.reshape(seq_dev, length, D), axis=0)
    grad_vector = jnp.concatenate([grad_pieces, d_gain_emb, d_shift_emb, d_head_bias, d_predictor])
    buckets = (
        multiply_left(to_slot, d_embedded.astype(LOW))
        .astype(LOW)
        .reshape(n_blocks, capacity, D)
    )
    kind = LOW if special() else jnp.float32
    (grad_side, grad_in_t, grad_down), arrived, grad_vec = reduce_blocks(
        [
            jnp.concatenate([grad_pos.astype(kind), grad_head.astype(kind)], axis=0),
            jnp.concatenate([g.astype(kind) for g in grads_in], axis=0),
            grad_down,
        ],
        buckets,
        grad_vector,
    )
    from_slot = (asked_row[None, :] == jnp.arange(block_rows)[:, None]).astype(LOW)
    grad_word = multiply(from_slot, arrived.reshape(n_blocks * capacity, D))
    grad_in = grad_in_t.T

    col_local = layer_in.shape[2]
    col_global = my_index * col_local + jnp.arange(col_local)
    sub_cols = jnp.stack(
        [col_global < 3 * D, (col_global >= 3 * D) & (col_global < 4 * D), col_global >= 4 * D]
    ).astype(jnp.float32)
    sub_width = jnp.array([3 * D, D, FF], jnp.float32)
    square_in = grad_in * grad_in
    in_cols_new = decay_rate * in_cols[0] + (1.0 - decay_rate) * jnp.mean(
        square_in + tiny_square, axis=0
    )
    row_part_in = jnp.stack(
        [jnp.sum((square_in + tiny_square) * pick[None, :], axis=1) for pick in sub_cols]
    )
    row_weighted_in = jnp.stack(
        [jnp.sum(square_in * (pick / in_cols_new)[None, :], axis=1) for pick in sub_cols]
    )

    def rows_of(gradient, rows_old):
        return decay_rate * rows_old + (1.0 - decay_rate) * jnp.mean(
            gradient * gradient + tiny_square, axis=1
        )

    rows_new_down = rows_of(grad_down, down_rows[0])
    col_down, weighted_down = factor_stats(grad_down, rows_new_down)
    rows_new_word = rows_of(grad_word, word_rows)
    col_word, weighted_word = factor_stats(grad_word, rows_new_word)
    row_global = my_index * side_rows_local + jnp.arange(side_rows_local)
    is_pos = row_global < SEQ_LEN
    which = jnp.stack([is_pos, jnp.logical_not(is_pos)]).astype(jnp.float32)
    side_counts = jnp.array([SEQ_LEN, D], jnp.float32)
    rows_new_side = rows_of(grad_side, side_rows)
    square_side = grad_side * grad_side
    col_side = jnp.stack(
        [jnp.sum((square_side + tiny_square) * pick[:, None], axis=0) for pick in which]
    )
    weighted_side = jnp.stack(
        [jnp.sum(square_side * (pick / rows_new_side)[:, None], axis=0) for pick in which]
    )
    total_side = jnp.sum(which * rows_new_side[None, :], axis=1)
    seg_onehot = (
        segment_index(my_index * vec_local + jnp.arange(vec_local))[:, None]
        == jnp.arange(9 * LAYERS + 4)[None, :]
    )
    new_moment = decay_rate * vec_moment + (1.0 - decay_rate) * (grad_vec * grad_vec + tiny_square)
    vec_update = grad_vec * lax.rsqrt(new_moment)
    seg_part = jnp.sum(jnp.where(seg_onehot, (vec_update * vec_update)[:, None], 0.0), axis=0)
    parts = [
        row_part_in,
        row_weighted_in,
        col_down,
        weighted_down,
        col_word,
        weighted_word,
        col_side,
        weighted_side,
        total_side,
        jnp.sum(rows_new_down)[None],
        jnp.sum(rows_new_word)[None],
        seg_part,
        local_loss[None],
    ]
    summed = sum_over_devices(jnp.concatenate([p.reshape(-1) for p in parts]))
    sums, offset = [], 0
    for p in parts:
        sums.append(summed[offset : offset + p.size].reshape(p.shape))
        offset += p.size
    (
        row_sum_in,
        row_weighted_in,
        col_down,
        weighted_down,
        col_word,
        weighted_word,
        col_side,
        weighted_side,
        total_side,
        total_down,
        total_word,
        seg_squares,
        loss_total,
    ) = sums
    half = 1.0 - decay_rate
    rows_new_in = decay_rate * in_rows[0] + half * row_sum_in / sub_width[:, None]
    mean_in = jnp.mean(rows_new_in, axis=1)
    scale_in = clip_of(row_weighted_in, rows_new_in, mean_in, D * sub_width)

    def choose(options):
        return jnp.sum(sub_cols[:, None, :] * options[:, :, None], axis=0)

    row_sel_in = choose(rows_new_in)
    factor_in = jnp.sum(sub_cols * (learn_rate / scale_in)[:, None], axis=0)
    mean_sel_in = jnp.sum(sub_cols * mean_in[:, None], axis=0)
    new_in = layer_in[0] - factor_in[None, :] * grad_in * lax.rsqrt(
        row_sel_in * in_cols_new[None, :] / mean_sel_in[None, :]
    )
    cols_new_down = decay_rate * down_cols[0] + half * col_down / FF
    mean_down = total_down[0] / FF
    scale_down = clip_of(weighted_down, cols_new_down, mean_down, FF * D)
    new_down = layer_down[0] - (learn_rate / scale_down) * grad_down * lax.rsqrt(
        rows_new_down[:, None] * cols_new_down[None, :] / mean_down
    )
    cols_new_word = decay_rate * word_cols + half * col_word / VOCAB
    mean_word = total_word[0] / VOCAB
    scale_word = clip_of(weighted_word, cols_new_word, mean_word, VOCAB * D)
    new_word = word_table - (learn_rate / scale_word) * grad_word * lax.rsqrt(
        rows_new_word[:, None] * cols_new_word[None, :] / mean_word
    )
    cols_new_side = decay_rate * side_cols + half * col_side / side_counts[:, None]
    mean_side = total_side / side_counts
    scale_side = clip_of(weighted_side, cols_new_side, mean_side, side_counts * D)
    col_sel_side = jnp.where(is_pos[:, None], cols_new_side[0][None, :], cols_new_side[1][None, :])
    mean_sel_side = jnp.where(is_pos, mean_side[0], mean_side[1])
    factor_side = learn_rate / jnp.where(is_pos, scale_side[0], scale_side[1])
    new_side = side_mat - factor_side[:, None] * grad_side * lax.rsqrt(
        rows_new_side[:, None] * col_sel_side / mean_sel_side[:, None]
    )
    seg_scale = jnp.maximum(1.0, jnp.sqrt(seg_squares / segment_sizes()))
    vec_scale = jnp.sum(jnp.where(seg_onehot, seg_scale[None, :], 0.0), axis=1)
    new_vectors = vectors - learn_rate * vec_update / vec_scale
    return (
        loss_total[0],
        new_in[None],
        rows_new_in[None],
        in_cols_new[None],
        new_in.astype(LOW)[None],
        new_down[None],
        rows_new_down[None],
        cols_new_down[None],
        new_down.astype(LOW)[None],
        new_word,
        rows_new_word,
        cols_new_word,
        new_word.astype(LOW),
        new_side,
        rows_new_side,
        cols_new_side,
        new_side.astype(LOW),
        new_vectors,
        new_moment,
        new_vectors.astype(LOW),
    )


def solution(mesh):
    return jax.shard_map(
        local,
        mesh=mesh,
        in_specs=(
            P(("fsdp", "dp"), None),
            P(("fsdp", "dp"), None),
            P(("fsdp", "dp"), None),
            P(("fsdp", "dp")),
            P(None, None, ("fsdp", "dp")),
            P(None, ("fsdp", "dp"), None),
            P(("fsdp", "dp"), None),
            P(("fsdp", "dp"), None),
            P(("fsdp", "dp")),
            P(),
            P(None, ("fsdp", "dp")),
            P(None, ("fsdp", "dp")),
            P(),
            P(("fsdp", "dp")),
            P(),
            P(("fsdp", "dp")),
            P(),
            P(("fsdp", "dp")),
        ),
        out_specs=(
            P(),
            P(None, None, ("fsdp", "dp")),
            P(),
            P(None, ("fsdp", "dp")),
            P(None, None, ("fsdp", "dp")),
            P(None, ("fsdp", "dp"), None),
            P(None, ("fsdp", "dp")),
            P(),
            P(None, ("fsdp", "dp"), None),
            P(("fsdp", "dp"), None),
            P(("fsdp", "dp")),
            P(),
            P(("fsdp", "dp"), None),
            P(("fsdp", "dp"), None),
            P(("fsdp", "dp")),
            P(),
            P(("fsdp", "dp"), None),
            P(("fsdp", "dp")),
            P(("fsdp", "dp")),
            P(("fsdp", "dp")),
        ),
        check_vma=False,
    )
```

time: 1350 us -> 739 us (0.55)
  waiting for transfers between devices: 750 us -> 0.01 us
  Pallas kernels: 0 us -> 411 us
  blocking collectives: 223 us -> 4.21 us
  matrix products: 180 us -> 158 us
  other arithmetic: 115 us -> 99.7 us
    reduce_scatter x3 -> x0, waiting for transfers between devices: 636 us -> none  [the longest x1 357 us: local(): lax.psum_scatter(jnp.stack(in_parts), ('fsdp', 'dp'), scatter_dimension=2...]
    pallas_call x0 -> x3, Pallas kernels: none -> 411 us  [the longest x1 224 us: gather_weights(): pl.pallas_call(functools.partial(gather_kernel, plan, count), name='gathe...]
    psum x3 -> x0, blocking collectives: 166 us -> none  [the longest x2 87.9 us: local(): lax.psum((row_part_in, col_part_down, total_part_down, col_part_word, tot...]
    all_gather x3 -> x0, waiting for transfers between devices: 58.4 us -> none  [the longest x1 47.6 us: fetch_layer(): lax.all_gather(in_low[layer_index], ('fsdp', 'dp'), axis=1, tiled=True)]
    unnamed x8 -> x0, waiting for transfers between devices: 50.5 us -> none
    all_gather x1 -> x0, blocking collectives: 42 us -> none  [local(): lax.all_gather(vectors.astype(jnp.bfloat16), ('fsdp', 'dp'), axis=0, tile...]
    another operation x5 -> x4, other arithmetic: 22.5 us -> 1.24 us  [the longest x1 21.3 us: local(): jnp.stack(in_parts)]
    dot_general x6 -> x8, matrix products: 55.2 us -> 34.1 us  [multiply(): return jnp.dot(left_side, right_side, preferred_element_type=jnp.float32)]
  transfers between devices with their start and end apart: 10 -> 1, of which waited for: 7 -> 0; matrix products, arithmetic and copies ran while one was open for 14% -> 2% of each run, Pallas kernels for 0% -> 0%
where the time goes in v1:
time: 739 us; the launch traced here: 734 us
  Pallas kernels  411 us (56%)
  matrix products  158 us (21%)
  other arithmetic  99.7 us (13%)
  local copies, waits for them, and re-layouts  47 us (6%)
  starting transfers between devices  8.34 us (1%)
    pallas_call x1, Pallas kernels, gather_weights(): pl.pallas_call(functools.partial(gather_kernel, plan, count), name='gathe...  224 us
    pallas_call x1, Pallas kernels, scatter_grads(): pl.pallas_call(functools.partial(scatter_kernel, plan, count), name='scat...  170 us
    dot_general x5, matrix products, multiply_right(): lax.dot_general(left_side, right_side, (((1,), (1,)), ((), ())), preferre...  57 us
    dot_general x8, matrix products, multiply(): return jnp.dot(left_side, right_side, preferred_element_type=jnp.float32)  34.1 us
    dot_general x6, matrix products, multiply_left(): lax.dot_general(left_side, right_side, (((0,), (0,)), ((), ())), preferre...  27.9 us
    pallas_call x1, Pallas kernels, sum_over_devices(): pl.pallas_call(sum_kernel, name='sum_over_devices', out_shape=jax.ShapeDt...  17 us
  transfers between devices with their start and end apart: 1, of which 0 were waited for; matrix products, arithmetic and copies ran while one was open for 2% of the time, Pallas kernels for 0%

profile of v1, /device:TPU:0, one launch (start us, length us, event | category | flops | bytes accessed | tf_op | source)
XLA Modules:
  0.0 734.5 jit_solution(5984215790862898067)
XLA Ops:
  11.8 8.3 %all-to-all-start = ((s32[16,2,34]{2,1,0:T(2,128)}), s32[16,2,34]{2,1,0:T(2,128)S(1)}, u32[]{:S(2)}, u32[]{:S(2)}) async-start(s32[16,2,34]{2,1,0:T(2,128)} %pad_add_fusion), calls=%async_computation | async-start | bytes 32768 | tf_op jit(solution)/shard_map/all_to_all | solution.py:690
  40.9 5.3 gather_fusion
  49.4 223.7 %gather_weights.1 = (bf16[4,2,2,2,64,1024]{5,4,3,2,1,0:T(8,128)(2,1)}, bf16[4,2,2,2,256,1024]{5,4,3,2,1,0:T(8,128)(2,1)}, bf16[4,2,2,2,128,1024]{5,4,3,2,1,0:T(8,128)(2,1)}, bf16[32,32,1024]{2,1,0:T(8,128)(2,1)}) custom-call(bf16[64,1024]{1,0:T(8,128)(2,1)} %fusion.65.refs_0_, bf16[256,1024]{1,0:T(8,128)(2,1)} %fusion.63.refs_1_, ...), custom_call_target="tpu_custom_call" | custom-call | tf_op jit(solution)/shard_map/gather_weights/pallas_call | solution.py:449
  279.4 8.3 %slice.260 = bf16[2,2,2,2,256,1024]{5,4,3,2,1,0:T(8,128)(2,1)} slice(bf16[4,2,2,2,256,1024]{5,4,3,2,1,0:T(8,128)(2,1)} %get-tuple-element.31), slice={[2:4], [0:2], [0:2], [0:2], [0:256], [0:1024]} | slice | bytes 16777216 | tf_op jit(solution)/shard_map/slice | solution.py:153
  287.7 7.9 %add_convert_fusion.1 = bf16[512,3072]{1,0:T(8,128)(2,1)} fusion(bf16[8192,1024]{1,0:T(8,128)(2,1)} %bitcast.266, f32[3072]{0:T(1024)S(1)} %pad_maximum_fusion.4, f32[512,1024]{1,0:T(8,128)S(1)} %get-tuple-element.281, f32[1024]{0:T(1024)S(1)} %bitcast.341, f32[1024]{0:T(1024)S(1)} %bitcast.318, f32[512]{0:T(512)S(1)} %fusion.96, ...), kind=kOutput, calls=%fused_computation.37 | convolution fusion | flops 3226992640 | bytes 11558912 | tf_op jit(solution)/shard_map/dot_general | solution.py:63
  298.8 7.0 multiply_reduce_fusion.1
  305.8 8.6 %fusion = f32[16,512]{1,0:T(8,128)S(1)} fusion(f32[16,512,512]{1,2,0:T(8,128)} %get-tuple-element.283, f32[16,512]{1,0:T(8,128)S(1)} %get-tuple-element.282), kind=kLoop, calls=%fused_computation.8 | loop fusion | flops 12574720 | bytes 16842752 | tf_op jit(solution)/shard_map/vmap()/reduce_sum | solution.py:103
  315.0 8.9 %fusion.52 = bf16[16,64,512]{2,1,0:T(8,128)(2,1)} fusion(f32[16,512,512]{1,2,0:T(8,128)} %get-tuple-element.283, f32[16,512]{1,0:T(8,128)S(1)} %fusion, f32[16,512]{1,0:T(8,128)S(1)} %get-tuple-element.282, bf16[1,512,3,16,64]{1,4,3,2,0:T(8,128)(2,1)S(1)} %bitcast.248), kind=kOutput, calls=%fused_computation.124 | convolution fusion | flops 554172416 | bytes 18939904 | tf_op jit(solution)/shard_map/vmap(hqk,khe->qhe)/dot_general | solution.py:105
  330.1 27.6 %multiply_convert_fusion.1 = (bf16[512,4096]{1,0:T(8,128)(2,1)S(1)}, f32[512,4096]{1,0:T(8,128)}, f32[512,4096]{1,0:T(8,128)}) fusion(f32[4096]{0:T(1024)S(1)} %bitcast.307, bf16[4096,1024]{1,0:T(8,128)(2,1)} %bitcast.256, f32[512,1024]{1,0:T(8,128)S(1)} %get-tuple-element.285, f32[1024]{0:T(1024)S(1)} %bitcast.344, f32[1024]{0:T(1024)S(1)} %bitcast.323, ...), kind=kOutput, calls=%fused_computation.17 | convolution fusion | flops 4436000768 | bytes 31485952 | tf_op jit(solution)/shard_map/dot_general | solution.py:63
  357.8 4.8 fusion.144
  362.9 5.6 multiply_convert_fusion.2
  377.8 15.0 %convert_reduce_fusion = (f32[4096]{0:T(1024)S(1)}, bf16[512,4096]{1,0:T(8,128)(2,1)}) fusion(f32[512,4096]{1,0:T(8,128)} %get-tuple-element.230, f32[512,4096]{1,0:T(8,128)} %get-tuple-element.286, f32[4096]{0:T(1024)S(1)} %bitcast.308, bf16[512,1024]{1,0:T(8,128)(2,1)} %get-tuple-element.214, bf16[4096,1024]{1,0:T(8,128)(2,1)} %bitcast.359), kind=kOutput, calls=%fused_computation.14 | convolution fusion | flops 4330614784 | bytes 30441472 | tf_op jit(solution)/shard_map/dot_general | solution.py:63
  392.8 7.0 multiply_reduce_fusion.6
  408.1 7.3 convolution_convert_fusion.1
  415.4 6.8 convolution_convert_fusion
  423.0 7.7 %fusion.47 = bf16[1,512,1,16,64]{1,4,3,2,0:T(8,128)(2,1)S(1)} fusion(bf16[512,16,64]{0,2,1:T(8,128)(2,1)S(1)} %bitcast.253, f32[16,512,512]{1,2,0:T(8,128)} %get-tuple-element.283, f32[16,512]{1,0:T(8,128)S(1)} %copy-done.20), kind=kOutput, calls=%fused_computation.123 | convolution fusion | flops 549453824 | bytes 18907136 | tf_op jit(solution)/shard_map/vmap(hqk,qhe->khe)/dot_general | solution.py:118
  430.7 11.3 %multiply_reduce_fusion = (f32[16,512]{1,0:T(8,128)S(1)}, f32[16,512,512]{1,2,0:T(8,128)}) fusion(f32[16,512,512]{1,2,0:T(8,128)} %get-tuple-element.283, f32[16,512]{1,0:T(8,128)S(1)} %copy-done.20, bf16[512,16,64]{0,2,1:T(8,128)(2,1)S(1)} %bitcast.254, bf16[1,512,3,16,64]{1,4,3,2,0:T(8,128)(2,1)S(1)} %bitcast.249), kind=kOutput, calls=%fused_computation.4 | convolution fusion | flops 553639936 | bytes 35717120 | tf_op jit(solution)/shard_map/vmap(qhe,khe->hqk)/dot_general | solution.py:124
  441.9 11.8 %multiply_convert_fusion = bf16[16,512,512]{1,2,0:T(8,128)(2,1)S(1)} fusion(f32[16,512,512]{1,2,0:T(8,128)} %get-tuple-element.293, f32[16,512,512]{1,2,0:T(8,128)} %get-tuple-element.283, f32[16,512]{1,0:T(8,128)S(1)} %get-tuple-element.292, f32[16,512]{1,0:T(8,128)S(1)} %copy-done.20), kind=kLoop, calls=%fused_computation.3 | loop fusion | flops 20971520 | bytes 42008576 | tf_op jit(solution)/shard_map/vmap()/convert_element_type | solution.py:126
  460.1 8.1 %multiply_reduce_fusion.4 = (f32[1024]{0:T(1024)S(1)}, f32[512]{0:T(512)S(1)}, f32[1024]{0:T(1024)S(1)}, f32[512,1024]{1,0:T(8,128)}) fusion(f32[512,1024]{1,0:T(8,128)S(1)} %copy-done.7, f32[512]{0:T(512)S(1)} %copy-done.39, f32[512]{0:T(512)S(1)} %copy-done.30, f32[1024]{0:T(1024)S(1)} %bitcast.320, bf16[512,3072]{0,1:T(8,128)(2,1)S(1)} %bitcast.273, ...), kind=kOutput, calls=%fused_computation.67 | convolution fusion | flops 3226465792 | bytes 15749120 | tf_op jit(solution)/shard_map/dot_general | solution.py:53
  468.2 5.6 convolution_convert_fusion.2
  486.6 8.8 %pad_maximum_fusion = bf16[8192,1024]{1,0:T(8,128)(2,1)} fusion(bf16[4096,1024]{1,0:T(8,128)(2,1)S(1)} %bitcast.262, bf16[1024,1024]{1,0:T(8,128)(2,1)S(1)} %copy-done.14, bf16[3072,1024]{1,0:T(8,128)(2,1)S(1)} %bitcast.264), kind=kLoop, calls=%fused_computation.2 | loop fusion | flops 50331648 | bytes 33554432 | tf_op jit(solution)/shard_map/concatenate | solution.py:837
  495.5 170.1 %scatter_grads.1 = (f32[48,1024]{1,0:T(8,128)}, f32[256,1024]{1,0:T(8,128)}, f32[128,1024]{1,0:T(8,128)}, bf16[32,32,1024]{2,1,0:T(8,128)(2,1)}, f32[32,4,128]{2,1,0:T(4,128)}) custom-call(bf16[4,2,2,2,48,1024]{5,4,3,2,1,0:T(8,128)(2,1)} %bitcast.252, bf16[4,2,2,2,256,1024]{5,4,3,2,1,0:T(8,128)(2,1)} %bitcast.246, ...), custom_call_target="tpu_custom_call" | custom-call | tf_op jit(solution)/shard_map/scatter_grads/pallas_call | solution.py:590
  682.6 17.0 %sum_over_devices.1 = f32[32,4,128]{2,1,0:T(4,128)} custom-call(f32[32,4,128]{2,1,0:T(4,128)} %bitcast.280), custom_call_target="tpu_custom_call" | custom-call | tf_op jit(solution)/shard_map/sum_over_devices/pallas_call | solution.py:663
  726.5 6.8 fusion.123
  (364 shorter events, 128.9 us)
Async XLA Ops:
  7.8 269.6 %copy-start.61 = (s32[512]{0:T(512)}, s32[512]{0:T(512)S(1)}, u32[]{:S(2)}) copy-start(s32[512]{0:T(512)S(1)} %get-tuple-element.270) | copy-start | bytes 6148
  11.8 22.5 %all-to-all-start = ((s32[16,2,34]{2,1,0:T(2,128)}), s32[16,2,34]{2,1,0:T(2,128)S(1)}, u32[]{:S(2)}, u32[]{:S(2)}) async-start(s32[16,2,34]{2,1,0:T(2,128)} %pad_add_fusion), calls=%async_computation | async-start | bytes 32768 | tf_op jit(solution)/shard_map/all_to_all | solution.py:690
  277.4 47.9 %copy-start.35 = (f32[2,1,512]{2,1,0:T(1,128)}, f32[2,1,512]{2,1,0:T(1,128)S(1)}, u32[]{:S(2)}) copy-start(f32[2,1,512]{2,1,0:T(1,128)S(1)} %get-tuple-element.257) | copy-start | bytes 12292
  277.4 47.8 %copy-start.50 = (f32[2,1,512]{2,1,0:T(1,128)}, f32[2,1,512]{2,1,0:T(1,128)S(1)}, u32[]{:S(2)}) copy-start(f32[2,1,512]{2,1,0:T(1,128)S(1)} %get-tuple-element.256) | copy-start | bytes 12292
  279.0 46.2 %copy-start.29 = (f32[512]{0:T(512)}, f32[512]{0:T(512)S(1)}, u32[]{:S(2)}) copy-start(f32[512]{0:T(512)S(1)} %broadcast_multiply_fusion.3) | copy-start | bytes 6148
  279.4 45.9 %copy-start.38 = (f32[512]{0:T(512)}, f32[512]{0:T(512)S(1)}, u32[]{:S(2)}) copy-start(f32[512]{0:T(512)S(1)} %fusion.96) | copy-start | bytes 6148
  325.3 32.5 %slice-start.6 = ((s8[8388608]{0:T(1024)(128)(4,1)}), s8[4194304]{0:T(1024)(128)(4,1)S(1)}, s32[]{:S(2)}) async-start(s8[8388608]{0:T(1024)(128)(4,1)} %bitcast.360), calls=%async_computation.8 | async-start | bytes 8388608
  495.4 171.4 %copy-start.46 = (f32[2,48]{1,0:T(2,128)S(1)}, f32[2,48]{1,0:T(2,128)}, u32[]{:S(2)}) copy-start(f32[2,48]{1,0:T(2,128)} %copy-done.45) | copy-start | bytes 1156
  495.4 171.4 %copy-start.68 = (f32[48]{0:T(128)S(1)}, f32[48]{0:T(128)}, u32[]{:S(2)}) copy-start(f32[48]{0:T(128)} %param.36) | copy-start | bytes 580
  495.4 171.4 %copy-start.64 = (pred[1,48]{1,0:T(4,128)(4,1)S(1)}, pred[1,48]{1,0:T(4,128)(4,1)}, u32[]{:S(2)}) copy-start(pred[1,48]{1,0:T(4,128)(4,1)} %copy-done.63) | copy-start | bytes 148
  495.4 171.4 %copy-start.66 = (pred[1,48]{1,0:T(4,128)(4,1)S(1)}, pred[1,48]{1,0:T(4,128)(4,1)}, u32[]{:S(2)}) copy-start(pred[1,48]{1,0:T(4,128)(4,1)} %copy-done.65) | copy-start | bytes 148
  495.4 172.8 %copy-start.71 = (f32[1,128]{1,0:T(1,128)S(1)}, f32[1,128]{1,0:T(1,128)}, u32[]{:S(2)}) copy-start(f32[1,128]{1,0:T(1,128)} %param.32) | copy-start | bytes 1540
  495.4 176.2 %copy-start.25 = (f32[3,256]{1,0:T(4,128)S(1)}, f32[3,256]{1,0:T(4,128)}, u32[]{:S(2)}) copy-start(f32[3,256]{1,0:T(4,128)} %get-tuple-element.209) | copy-start | bytes 9220
  495.5 176.2 %copy-start.67 = (f32[1,256]{1,0:T(1,128)S(1)}, f32[1,256]{1,0:T(1,128)}, u32[]{:S(2)}) copy-start(f32[1,256]{1,0:T(1,128)} %param.31) | copy-start | bytes 3076
  666.8 66.5 %copy-start.47 = (f32[48]{0:T(128)}, f32[48]{0:T(128)S(1)}, u32[]{:S(2)}) copy-start(f32[48]{0:T(128)S(1)} %get-tuple-element.206) | copy-start | bytes 580
  671.6 44.6 %copy-start.37 = (f32[1,256]{1,0:T(1,128)}, f32[1,256]{1,0:T(1,128)S(1)}, u32[]{:S(2)}) copy-start(f32[1,256]{1,0:T(1,128)S(1)} %get-tuple-element.208) | copy-start | bytes 3076
  672.9 49.4 %copy-start.44 = (f32[512]{0:T(512)}, f32[512]{0:T(512)S(1)}, u32[]{:S(2)}) copy-start(f32[512]{0:T(512)S(1)} %get-tuple-element.200) | copy-start | bytes 6148
  677.7 48.8 %copy-start.24 = (f32[960]{0:T(1024)}, f32[960]{0:T(1024)S(1)}, u32[]{:S(2)}) copy-start(f32[960]{0:T(1024)S(1)} %get-tuple-element.202) | copy-start | bytes 11524
  679.0 31.0 %copy-start.43 = (f32[2,1024]{1,0:T(2,128)S(1)}, f32[2,1024]{1,0:T(2,128)}, u32[]{:S(2)}) copy-start(f32[2,1024]{1,0:T(2,128)} %param.37) | copy-start | bytes 24580
  679.0 31.0 %copy-start.56 = (f32[2]{0:T(128)S(1)}, f32[2]{0:T(128)}, u32[]{:S(2)}) copy-start(f32[2]{0:T(128)} %constant.319) | copy-start | bytes 28
  679.0 31.2 %copy-start.72 = (f32[2]{0:T(128)S(1)}, f32[2]{0:T(128)}, u32[]{:S(2)}) copy-start(f32[2]{0:T(128)} %constant.325) | copy-start | bytes 28
  679.8 36.3 %copy-start.69 = (f32[3]{0:T(128)S(1)}, f32[3]{0:T(128)}, u32[]{:S(2)}) copy-start(f32[3]{0:T(128)} %constant.324) | copy-start | bytes 40
  679.8 36.3 %copy-start.53 = (pred[3,256]{1,0:T(4,128)(4,1)S(1)}, pred[3,256]{1,0:T(4,128)(4,1)}, u32[]{:S(2)}) copy-start(pred[3,256]{1,0:T(4,128)(4,1)} %get-tuple-element.210) | copy-start | bytes 2308
  679.8 36.4 %copy-start.4 = (f32[1,1024,256]{1,2,0:T(8,128)S(1)}, f32[1,1024,256]{1,2,0:T(8,128)}, u32[]{:S(2)}) copy-start(f32[1,1024,256]{1,2,0:T(8,128)} %copy-done.3) | copy-start | bytes 3145732
  (65 other events, 589.4 us)

commit v2 on v1

--- a/solution.py
+++ b/solution.py
@@ -150,9 +150,9 @@
     mid_in = hidden + (multiply_right(context_low, weight_in[3 * D : 4 * D]) + bias_o)
     middle = layer_norm(mid_in, gain_a, shift_a)
     middle_low = middle.astype(jnp.bfloat16)
-    lifted = multiply_right(middle_low, weight_in[4 * D :]) + bias_up
+    lifted = multiply_right(weight_in[4 * D :], middle_low) + bias_up[:, None]
     active_low = exact_gelu(lifted).astype(jnp.bfloat16)
-    out_in = middle + (multiply(active_low, weight_down) + bias_down)
+    out_in = middle + (multiply_left(active_low, weight_down) + bias_down)
     output = layer_norm(out_in, gain_b, shift_b)
     return (
         output,
@@ -187,13 +187,10 @@
     length = tokens // seq_dev
     d_out_in, d_gain_b, d_shift_b = norm_back(out_in, gain_b, shift_b, grad_out)
     d_down_low = d_out_in.astype(jnp.bfloat16)
-    grad_down = multiply_left(active_low, d_down_low)
-    d_lifted_low = gelu_back(lifted, multiply_right(d_down_low, weight_down)).astype(jnp.bfloat16)
-    grad_up = multiply_left(d_lifted_low, middle_low)
-    d_middle = d_out_in + multiply(d_lifted_low, weight_in[4 * D :])
+    d_lifted_low = gelu_back(lifted, multiply_right(weight_down, d_down_low)).astype(jnp.bfloat16)
+    d_middle = d_out_in + multiply_left(d_lifted_low, weight_in[4 * D :])
     d_mid_in, d_gain_a, d_shift_a = norm_back(mid_in, gain_a, shift_a, d_middle)
     d_attended_low = d_mid_in.astype(jnp.bfloat16)
-    grad_out_proj = multiply_left(d_attended_low, context_low)
     d_context_low = multiply(d_attended_low, weight_in[3 * D : 4 * D]).astype(jnp.bfloat16)
     heads_view = projected.reshape(seq_dev, length, 3, HEADS, HEAD_DIM)
     d_heads = jax.vmap(attend_back)(
@@ -204,7 +201,6 @@
         d_context_low.reshape(seq_dev, length, HEADS, HEAD_DIM),
     )
     d_projected_low = d_heads.reshape(tokens, 3 * D).astype(jnp.bfloat16)
-    grad_joint = multiply_left(d_projected_low, hidden_low)
     d_hidden = d_mid_in + multiply(d_projected_low, weight_in[: 3 * D])
     joint_sums = jnp.sum(d_projected_low.astype(jnp.float32), axis=0)
     grad_pieces = jnp.concatenate(
@@ -214,7 +210,7 @@
             jnp.sum(d_attended_low.astype(jnp.float32), axis=0),
             d_gain_a,
             d_shift_a,
-            jnp.sum(d_lifted_low.astype(jnp.float32), axis=0),
+            jnp.sum(d_lifted_low.astype(jnp.float32), axis=1),
             jnp.sum(d_down_low.astype(jnp.float32), axis=0),
             d_gain_b,
             d_shift_b,
@@ -222,8 +218,16 @@
     )
     return (
         d_hidden,
-        [grad_joint, grad_out_proj, grad_up],
-        grad_down,
+        (
+            active_low,
+            d_down_low,
+            d_lifted_low,
+            middle_low,
+            d_projected_low.T,
+            hidden_low,
+            d_attended_low.T,
+            context_low,
+        ),
         grad_pieces,
     )
 
@@ -254,26 +258,35 @@
     )
 
 
-def enter(n):
+def greet(n):
     me = my_rank()
     barrier = pltpu.get_barrier_semaphore()
 
-    def greet(step, carry):
+    def one(step, carry):
         pl.semaphore_signal(
             barrier, inc=1, device_id=by_rank((me + step) % n), device_id_type=MESH
         )
         return carry
 
-    lax.fori_loop(1, n, greet, 0)
-    pl.semaphore_wait(barrier, n - 1)
+    lax.fori_loop(1, n, one, 0)
+
+
+def welcome(n):
+    pl.semaphore_wait(pltpu.get_barrier_semaphore(), n - 1)
+
+
+def enter(n):
+    greet(n)
+    welcome(n)
 
 
 class Copies:
     def __init__(self, send, recv):
-        self.send, self.recv, self.begun = send, recv, []
+        self.send, self.recv, self.begun, self.count = send, recv, {}, 0
 
     def start(self, src, dst, target):
-        slot = len(self.begun)
+        slot = self.count
+        self.count += 1
         copy = pltpu.make_async_remote_copy(
             src_ref=src,
             dst_ref=dst,
@@ -283,11 +296,14 @@
             device_id_type=MESH,
         )
         copy.start()
-        self.begun.append(copy)
+        self.begun[id(copy)] = copy
         return copy
 
+    def sent(self, copy):
+        self.begun.pop(id(copy)).wait_send()
+
     def drain(self):
-        for copy in self.begun:
+        for copy in self.begun.values():
             copy.wait_send()
 
 
@@ -320,36 +336,85 @@
     lax.fori_loop(1, n, finish, 0)
 
 
-def pipeline(order, chunks):
-    live = [iter(chunk) for chunk in chunks]
-    for index in order:
-        next(live[index], None)
-
-
-def gather_order(plan):
+LEAD, LOOK = 3, 2
+TILES = ((64,), (64, 64, 64), (64, 64))
+PLANE = {1: 64}
+
+
+def gather_steps(plan):
     first = [i for i, p in enumerate(plan) if p[3]]
     rest = [i for i, p in enumerate(plan) if not p[3]]
-    order = first + rest + first + first
+    order, task = first + rest[:LEAD] + first, 0
     for step in range(len(rest) + 4):
-        order += [rest[i] for i in range(min(step, len(rest) - 1), -1, -1) if 0 <= step - i < 4]
+        if step + LEAD < len(rest):
+            order.append(rest[step + LEAD])
+        order += [rest[i] for i in range(min(step, len(rest) - 1), -1, -1) if step - i < 4]
+        if step == LOOK:
+            order += first
+        if step >= LOOK and task < 4:
+            task += 1
+            order.append(-task)
     return order + first + first
 
 
+def count_from(index, shape, axis):
+    return lax.broadcasted_iota(jnp.int32, shape, axis) == index
+
+
+def one_hot(mask):
+    return jnp.where(mask, 1.0, 0.0).astype(LOW)
+
+
+def fill_slots(blocks, values, tally, to_slot, message):
+    n, capacity, lanes = message.shape
+    tokens = blocks.shape[1]
+    owner = blocks[...]
+    member = count_from(owner, (n, tokens), 0)
+    earlier = one_hot(
+        lax.broadcasted_iota(jnp.int32, (tokens, tokens), 0)
+        < lax.broadcasted_iota(jnp.int32, (tokens, tokens), 1)
+    )
+    ahead = multiply(one_hot(member), earlier)
+    rank = jnp.sum(jnp.where(member, ahead, 0.0), axis=0, keepdims=True).astype(jnp.int32)
+    slot = owner * capacity + rank
+    to_slot[...] = one_hot(count_from(slot, (n * capacity, tokens), 0))
+    listed = multiply(to_slot[...], values[...]) + tally[...]
+    message[...] = listed.reshape(n, capacity, lanes)
+
+
+def look_up(index, answer, table, from_slot, found):
+    n, capacity, lanes = answer.shape
+    group = n // 4
+    part = pl.ds(index * group, group)
+    wanted = answer[part].reshape(group * capacity, lanes)
+    row = (wanted[:, 0:1] * 256.0 + wanted[:, 1:2]).astype(jnp.int32)
+    row = jnp.where(wanted[:, 2:3] > 0.5, row, -1)
+    hot = one_hot(count_from(row, (group * capacity, table.shape[0]), 1))
+    from_slot[part] = hot.reshape(group, capacity, -1)
+    found[part] = multiply(hot, table[...]).astype(LOW).reshape(group, capacity, -1)
+
+
 def gather_kernel(plan, count, *refs):
-    local, out = refs[:count], refs[count + 1 : 2 * count + 1]
-    found, rows = refs[count], refs[2 * count + 1]
-    send, recv, own_sem, row_send, row_recv = refs[2 * count + 2 :]
+    local = refs[:count]
+    blocks, values, tally, table = refs[count : count + 4]
+    out = refs[count + 4 : 2 * count + 4]
+    rows, to_slot, from_slot, answer = refs[2 * count + 4 : 2 * count + 8]
+    message, found, send, recv, own_sem, ask_send, ask_recv, row_send, row_recv = refs[
+        2 * count + 8 :
+    ]
     z, y, x, c = place()
     n = 32
     me = my_rank()
-    enter(n)
+    greet(n)
+    fill_slots(blocks, values, tally, to_slot, message)
+    answer[me] = message[me]
+    welcome(n)
     copies = Copies(send, recv)
+    exchange_start(message, answer, ask_send, ask_recv, n)
     own = []
     for i in range(count):
         own.append(pltpu.make_async_copy(local[i], out[i].at[z, y, x, c], own_sem.at[i]))
-    own.append(pltpu.make_async_copy(found.at[me], rows.at[me], own_sem.at[count]))
-    for copy in own:
-        copy.start()
+        own[i].start()
     to_x, to_y, to_core, to_z = neighbours(z, y, x, c)
 
     def pass_on(ref, where, target):
@@ -415,47 +480,71 @@
         yield
 
     chunks = [chunk(*p) for p in plan]
-    exchange_start(found, rows, row_send, row_recv, n)
-    pipeline(gather_order(plan), chunks)
-    for live in chunks:
-        next(live, None)
+    keep = pltpu.make_async_copy(found.at[me], rows.at[me], own_sem.at[count])
+    for index in gather_steps(plan):
+        if index >= 0:
+            next(chunks[index], None)
+            continue
+        task = -index - 1
+        if task == 0:
+            exchange_wait(message, answer, ask_send, ask_recv, n)
+        look_up(task, answer, table, from_slot, found)
+        if task == 3:
+            keep.start()
+            exchange_start(found, rows, row_send, row_recv, n)
     exchange_wait(found, rows, row_send, row_recv, n)
+    keep.wait()
     copies.drain()
-    for i in range(count + 1):
+    for i in range(count):
         own_there(i)
 
 
-def gather_plan(heights, plane_rows):
+def gather_plan(heights):
     plan = []
     for i, height in enumerate(heights):
         start = 0
-        for size in plane_rows.get(i, ()):
-            plan.append((i, start, size, True))
-            start += size
-        while start < height:
-            size = 64 if height - start >= 64 else height - start
+        if i in PLANE:
+            plan.append((i, 0, PLANE[i], True))
+            start = PLANE[i]
+        for size in TILES[i]:
             plan.append((i, start, size, False))
             start += size
+        assert start == height
     return plan
 
 
-def gather_weights(arrays, found):
+def gather_weights(arrays, blocks, values, tally, table):
     count = len(arrays)
-    plan = gather_plan([a.shape[0] for a in arrays], {1: (32,)})
+    n, capacity = 32, 32
+    tokens = blocks.shape[1]
+    plan = gather_plan([a.shape[0] for a in arrays])
     total = sum(15 if p[3] else 12 for p in plan)
     hbm = pl.BlockSpec(memory_space=pl.ANY)
     vmem = pl.BlockSpec(memory_space=pltpu.VMEM)
     dma = pltpu.SemaphoreType.DMA
+    shape = jax.ShapeDtypeStruct
     return pl.pallas_call(
         functools.partial(gather_kernel, plan, count),
         name="gather_weights",
-        out_shape=tuple(jax.ShapeDtypeStruct((4, 2, 2, 2) + a.shape, a.dtype) for a in arrays)
-        + (jax.ShapeDtypeStruct(found.shape, found.dtype),),
-        in_specs=[vmem] * count + [hbm],
-        out_specs=tuple([hbm] * (count + 1)),
-        scratch_shapes=[dma((total,)), dma((total,)), dma((count + 1,)), dma((32,)), dma((32,))],
+        out_shape=tuple(shape((4, 2, 2, 2) + a.shape, a.dtype) for a in arrays)
+        + (
+            shape((n, capacity, D), LOW),
+            shape((n * capacity, tokens), LOW),
+            shape((n, capacity, table.shape[0]), LOW),
+            shape((n, capacity, 128), jnp.float32),
+        ),
+        in_specs=[vmem] * (count + 4),
+        out_specs=tuple([hbm] * (count + 1) + [vmem] * 3),
+        scratch_shapes=[
+            pltpu.VMEM((n, capacity, 128), jnp.float32),
+            pltpu.VMEM((n, capacity, D), LOW),
+            dma((total,)),
+            dma((total,)),
+            dma((count + 1,)),
+        ]
+        + [dma((n,))] * 4,
         compiler_params=pltpu.CompilerParams(collective_id=0, has_side_effects=True),
-    )(*arrays, found)
+    )(*arrays, blocks, values, tally, table)
 
 
 def add_blocks(dst, other, shape, at_dst, at_other):
@@ -473,13 +562,46 @@
     lax.fori_loop(0, math.prod(shape), body, 0)
 
 
-def scatter_kernel(plan, count, *refs):
-    grads, buckets, vector = refs[:count], refs[count], refs[count + 1]
-    out = refs[count + 2 : 2 * count + 2]
-    arrived, vector_all = refs[2 * count + 2 : 2 * count + 4]
-    rest = refs[2 * count + 4 :]
-    scratch = [rest[7 * i : 7 * i + 7] for i in range(count)]
-    send, recv, load, own_sem, row_send, row_recv, vec_send, vec_recv = rest[7 * count :]
+WIDE = 256
+
+
+class Group:
+    def __init__(self, z0, nz, height, sources, out):
+        self.z0, self.nz, self.height, self.sources, self.out = z0, nz, height, sources, out
+
+    def scratch(self):
+        nz, h, n = self.nz, self.height, D // WIDE
+        shapes = [(2, nz, 2, 2, h), (n, nz, 2, 2, h)] + [(n, nz, 2, h // 2)] * 2
+        shapes += [(n, nz, h // 2)] * 2 + [(n, 3, h)]
+        return [pltpu.VMEM(shape + (WIDE,), LOW) for shape in shapes]
+
+
+def each_block(group, refs, wide, core, body):
+    for start, stop, left, right, base, together in group.sources:
+        def one(step, carry, left=left, right=right, base=base, together=together):
+            index = step * together
+            part = refs[left][pl.ds(index - base, together), core]
+            product = multiply(part.reshape(-1, part.shape[-1]), refs[right][:, wide])
+            product = product.reshape(together, group.height, WIDE)
+            for k in range(together):
+                at = index + k
+                body((at // 4, (at // 2) % 2, at % 2), product[k])
+            return carry
+
+        lax.fori_loop(start // together, stop // together, one, 0)
+
+
+def scatter_kernel(groups, n_left, *refs):
+    operands = refs[:n_left]
+    side, buckets, vector = refs[n_left : n_left + 3]
+    out = refs[n_left + 3 : n_left + 6]
+    arrived, vector_all = refs[n_left + 6 : n_left + 8]
+    rest = refs[n_left + 8 :]
+    scratch = [rest[7 * i : 7 * i + 7] for i in range(len(groups))]
+    side_scratch = rest[7 * len(groups) : 7 * len(groups) + 7]
+    (send, recv, z_send, z_recv, load, row_send, row_recv, vec_send, vec_recv) = rest[
+        7 * len(groups) + 7 :
+    ]
     z, y, x, c = place()
     n = 32
     me = my_rank()
@@ -487,75 +609,146 @@
     copies = Copies(send, recv)
     to_x, to_y, to_core, to_z = neighbours(z, y, x, c)
     own = [
-        pltpu.make_async_copy(buckets.at[me], arrived.at[me], own_sem.at[0]),
-        pltpu.make_async_copy(vector.at[me], vector_all.at[me], own_sem.at[1]),
+        pltpu.make_async_copy(buckets.at[me], arrived.at[me], load.at[0]),
+        pltpu.make_async_copy(vector.at[me], vector_all.at[me], load.at[1]),
     ]
     for copy in own:
         copy.start()
-
-    def chunk(slot, i, start, low_size, high_size):
-        held, from_core, low_1, high_1, low_2, high_2, from_z = scratch[i]
-        grad, size = grads[i], low_size + high_size
-        part = pl.ds(start, size)
-        low, high = pl.ds(start, low_size), pl.ds(start + low_size, high_size)
-        core = copies.start(grad.at[:, :, :, 1 - c, part], from_core.at[:, :, :, part], to_core)
-        mine = pltpu.make_async_copy(
-            grad.at[:, :, :, c, part], held.at[:, :, :, part], load.at[slot]
-        )
-        mine.start()
-        yield
-        mine.wait()
+    sent_before = {}
+
+    def product_chunk(slot, which, index):
+        group = groups[which]
+        outgoing, held, low_1, high_1, low_2, high_2, from_z = scratch[which]
+        nz, h = group.nz, group.height
+        wide = pl.ds(index * WIDE, WIDE)
+        low, high = pl.ds(0, h // 2), pl.ds(h // 2, h // 2)
+        here = index % 2
+        if index >= 2:
+            copies.sent(sent_before[which, index - 2])
+
+        def send_off(where, value):
+            outgoing[(here,) + where] = value.astype(LOW)
+
+        each_block(group, operands, wide, 1 - c, send_off)
+        core = copies.start(outgoing.at[here], held.at[index], to_core)
+        sent_before[which, index] = core
+        yield
         core.wait_recv()
 
-        add_blocks(
-            held,
-            from_core,
-            (4, 2, 2),
-            lambda a, b, d: (a, b, d, part),
-            lambda a, b, d: (a, b, d, part),
-        )
-        first = copies.start(held.at[:, 1 - y, :, low], low_1.at[:, :, low], to_y)
-        second = copies.start(held.at[:, :, 1 - x, high], high_1.at[:, :, high], to_x)
+        def add_own(where, value):
+            spot = (index,) + where
+            held[spot] = (value + held[spot].astype(jnp.float32)).astype(LOW)
+
+        each_block(group, operands, wide, c, add_own)
+        first = copies.start(held.at[index, :, 1 - y, :, low], low_1.at[index], to_y)
+        second = copies.start(held.at[index, :, :, 1 - x, high], high_1.at[index], to_x)
         yield
         first.wait_recv()
         second.wait_recv()
         add_blocks(
-            held, low_1, (4, 2), lambda a, d: (a, y, d, low), lambda a, d: (a, d, low)
+            held, low_1, (nz, 2), lambda a, d: (index, a, y, d, low), lambda a, d: (index, a, d)
         )
         add_blocks(
-            held, high_1, (4, 2), lambda a, b: (a, b, x, high), lambda a, b: (a, b, high)
+            held, high_1, (nz, 2), lambda a, b: (index, a, b, x, high), lambda a, b: (index, a, b)
         )
-        first = copies.start(held.at[:, y, 1 - x, low], low_2.at[:, low], to_x)
-        second = copies.start(held.at[:, 1 - y, x, high], high_2.at[:, high], to_y)
+        first = copies.start(held.at[index, :, y, 1 - x, low], low_2.at[index], to_x)
+        second = copies.start(held.at[index, :, 1 - y, x, high], high_2.at[index], to_y)
         yield
         first.wait_recv()
         second.wait_recv()
-        add_blocks(held, low_2, (4,), lambda a: (a, y, x, low), lambda a: (a, low))
-        add_blocks(held, high_2, (4,), lambda a: (a, y, x, high), lambda a: (a, high))
+        add_blocks(held, low_2, (nz,), lambda a: (index, a, y, x, low), lambda a: (index, a))
+        add_blocks(held, high_2, (nz,), lambda a: (index, a, y, x, high), lambda a: (index, a))
+
+        def along(level, back):
+            return pltpu.make_async_remote_copy(
+                src_ref=held.at[index, level, y, x],
+                dst_ref=from_z.at[index, back],
+                send_sem=z_send.at[slot, level],
+                recv_sem=z_recv.at[slot, back],
+                device_id=device(group.z0 + level, y, x, c),
+                device_id_type=MESH,
+            )
+
+        for level in range(nz):
+            away = z != group.z0 + level
+
+            @pl.when(away)
+            def _(level=level):
+                along(level, (z - group.z0 - level + 3) % 4).start()
+
+        yield
+
+        def finish():
+            for back in range(3):
+                along(0, back).wait_recv()
+            mine = held[index, z - group.z0, y, x].astype(jnp.float32)
+            for back in range(3):
+                mine = mine + from_z[index, back].astype(jnp.float32)
+            out[group.out][:, wide] = mine
+
+        if nz == 4:
+            finish()
+        else:
+            pl.when((z >= group.z0) & (z < group.z0 + nz))(finish)
+        yield
+        for level in range(nz):
+            away = z != group.z0 + level
+
+            @pl.when(away)
+            def _(level=level):
+                along(level, (z - group.z0 - level + 3) % 4).wait_send()
+
+        yield
+
+    def side_chunk():
+        held, from_core, low_1, high_1, low_2, high_2, from_z = side_scratch
+        size = held.shape[3]
+        half = size // 32 * 16 + 16
+        low, high = pl.ds(0, half), pl.ds(half, size - half)
+        core = copies.start(side.at[:, :, :, 1 - c], from_core, to_core)
+        mine = pltpu.make_async_copy(side.at[:, :, :, c], held, load.at[2])
+        mine.start()
+        yield
+        mine.wait()
+        core.wait_recv()
+        add_blocks(held, from_core, (4, 2, 2), lambda *w: w, lambda *w: w)
+        first = copies.start(held.at[:, 1 - y, :, low], low_1, to_y)
+        second = copies.start(held.at[:, :, 1 - x, high], high_1, to_x)
+        yield
+        first.wait_recv()
+        second.wait_recv()
+        add_blocks(held, low_1, (4, 2), lambda a, d: (a, y, d, low), lambda a, d: (a, d))
+        add_blocks(held, high_1, (4, 2), lambda a, b: (a, b, x, high), lambda a, b: (a, b))
+        first = copies.start(held.at[:, y, 1 - x, low], low_2, to_x)
+        second = copies.start(held.at[:, 1 - y, x, high], high_2, to_y)
+        yield
+        first.wait_recv()
+        second.wait_recv()
+        add_blocks(held, low_2, (4,), lambda a: (a, y, x, low), lambda a: (a,))
+        add_blocks(held, high_2, (4,), lambda a: (a, y, x, high), lambda a: (a,))
         along = [
-            copies.start(held.at[(z + k) % 4, y, x, part], from_z.at[k - 1, part], to_z[k - 1])
+            copies.start(held.at[(z + k) % 4, y, x], from_z.at[k - 1], to_z[k - 1])
             for k in (1, 2, 3)
         ]
         yield
         for copy in along:
             copy.wait_recv()
-        total = held[z, y, x, part].astype(jnp.float32)
+        total = held[z, y, x].astype(jnp.float32)
         for k in range(3):
-            total = total + from_z[k, part].astype(jnp.float32)
-        out[i][part] = total
-        yield
-
-    chunks = [chunk(slot, *p) for slot, p in enumerate(plan)]
-    order = list(range(len(plan)))
-    for step in range(len(plan) + 4):
-        order += [i for i in range(min(step, len(plan) - 1), -1, -1) if 0 <= step - i < 4]
+            total = total + from_z[k].astype(jnp.float32)
+        out[2][...] = total
+        yield
+        yield
+
+    parts = [(which, index) for index in range(D // WIDE) for which in ORDER]
+    chunks = [side_chunk()] + [product_chunk(slot, *p) for slot, p in enumerate(parts)]
     exchange_start(vector, vector_all, vec_send, vec_recv, n)
-    live = [iter(one) for one in chunks]
-    for index in order[: len(plan)]:
-        next(live[index])
-    exchange_start(buckets, arrived, row_send, row_recv, n)
-    for index in order[len(plan) :]:
-        next(live[index])
+    for step in range(len(chunks) + 5):
+        for index in range(min(step, len(chunks) - 1), -1, -1):
+            if step - index < 6:
+                next(chunks[index], None)
+        if step == ROWS_AT:
+            exchange_start(buckets, arrived, row_send, row_recv, n)
     exchange_wait(vector, vector_all, vec_send, vec_recv, n)
     exchange_wait(buckets, arrived, row_send, row_recv, n)
     copies.drain()
@@ -563,55 +756,64 @@
         copy.wait()
 
 
-def scatter_plan(heights):
-    plan = []
-    for i, height in enumerate(heights):
-        start = 0
-        while start < height:
-            size = min(64, height - start)
-            low = (size // 2 + 15) // 16 * 16
-            plan.append((i, start, low, size - low))
-            start += size
-    return plan
-
-
-def scatter_grads(arrays, buckets, vector):
-    count = len(arrays)
-    heights = [a.shape[4] for a in arrays]
-    plan = scatter_plan(heights)
-    total = 8 * len(plan)
+ROWS_AT = 0
+ORDER = (0, 1, 2)
+
+
+def scatter_grads(pairs, side, buckets, vector):
+    blocked = []
+    for i, pair in enumerate(pairs):
+        height = FF // 32 if i == 0 else 256
+        blocked.append(pair if i % 2 else pair.reshape(-1, 2, height, pair.shape[1]))
+    groups = [
+        Group(0, 4, FF // 32, [(0, 16, 0, 1, 0, 2)], 1),
+        Group(2, 2, 256, [(0, 8, 2, 3, 0, 1)], 0),
+        Group(0, 2, 256, [(0, 6, 4, 5, 0, 1), (6, 8, 6, 7, 6, 1)], 0),
+    ]
+    height = side.shape[4]
+    half = height // 32 * 16 + 16
     hbm = pl.BlockSpec(memory_space=pl.ANY)
     vmem = pl.BlockSpec(memory_space=pltpu.VMEM)
     dma = pltpu.SemaphoreType.DMA
-    scratch = []
-    for h in heights:
-        for lead in ((4, 2, 2), (4, 2, 2), (4, 2), (4, 2), (4,), (4,), (3,)):
-            scratch.append(pltpu.VMEM(lead + (h, D), LOW))
+    scratch = [shape for group in groups for shape in group.scratch()]
+    for lead in (
+        (4, 2, 2, height),
+        (4, 2, 2, height),
+        (4, 2, half),
+        (4, 2, height - half),
+        (4, half),
+        (4, height - half),
+        (3, height),
+    ):
+        scratch.append(pltpu.VMEM(lead + (D,), LOW))
+    chunks = len(groups) * D // WIDE
+    total = 5 * chunks + 8
+    shape = jax.ShapeDtypeStruct
     return pl.pallas_call(
-        functools.partial(scatter_kernel, plan, count),
+        functools.partial(scatter_kernel, groups, len(pairs)),
         name="scatter_grads",
-        out_shape=tuple(jax.ShapeDtypeStruct((h, D), jnp.float32) for h in heights)
-        + (
-            jax.ShapeDtypeStruct(buckets.shape, buckets.dtype),
-            jax.ShapeDtypeStruct(vector.shape, vector.dtype),
+        out_shape=(
+            shape((256, D), jnp.float32),
+            shape((FF // 32, D), jnp.float32),
+            shape((height, D), jnp.float32),
+            shape(buckets.shape, buckets.dtype),
+            shape(vector.shape, vector.dtype),
         ),
-        in_specs=[hbm] * (count + 2),
-        out_specs=tuple([vmem] * count + [hbm, hbm]),
+        in_specs=[vmem] * len(pairs) + [hbm] * 3,
+        out_specs=(vmem, vmem, vmem, hbm, hbm),
         scratch_shapes=scratch
         + [
             dma((total,)),
             dma((total,)),
-            dma((len(plan),)),
-            dma((2,)),
-            dma((32,)),
-            dma((32,)),
-            dma((32,)),
-            dma((32,)),
-        ],
+            dma((chunks, 4)),
+            dma((chunks, 3)),
+            dma((3,)),
+        ]
+        + [dma((32,))] * 4,
         compiler_params=pltpu.CompilerParams(
-            collective_id=1, has_side_effects=True, vmem_limit_bytes=60 * 1024 * 1024
+            collective_id=1, has_side_effects=True, vmem_limit_bytes=64000 * 1024
         ),
-    )(*arrays, buckets, vector)
+    )(*blocked, side, buckets, vector)
 
 
 def sum_kernel(values, out, landed, total, send, recv, send_again, recv_again):
@@ -690,29 +892,67 @@
     half = lax.all_to_all(split, "fsdp", split_axis=0, concat_axis=0, tiled=True)
     return lax.all_to_all(half, "dp", split_axis=1, concat_axis=1, tiled=True).reshape(shape)
 
-def gather_blocks(arrays, found):
-    if special():
-        gathered = gather_weights(arrays, found)
-        return [g.reshape((-1, a.shape[-1])) for g, a in zip(gathered, arrays)], gathered[-1]
-    full = [lax.all_gather(a, BOTH, axis=0, tiled=True) for a in arrays]
-    return full, swap(found)
-
-
-def reduce_blocks(grads, buckets, vector):
+def ask_rows(blocks, local_row, local_counts, block_rows, capacity):
+    n = lax.axis_size(BOTH)
+    onehot = (blocks[:, None] == jnp.arange(n)[None, :]).astype(jnp.int32)
+    rank = jnp.sum(jnp.cumsum(onehot, axis=0) * onehot, axis=1) - 1
+    slot = blocks * capacity + rank
+    bucket_ids = jnp.full((n * capacity,), -1, jnp.int32).at[slot].set(local_row)
+    message = jnp.concatenate(
+        [
+            bucket_ids.reshape(n, capacity),
+            jnp.broadcast_to(local_counts[None, :], (n, MICRO)),
+        ],
+        axis=1,
+    )
+    answer = swap(message)
+    asked = answer[:, :capacity].reshape(-1)
+    to_slot = (jnp.arange(n * capacity)[:, None] == slot[None, :]).astype(LOW)
+    from_slot = (asked[:, None] == jnp.arange(block_rows)[None, :]).astype(LOW)
+    return to_slot, from_slot, jnp.sum(answer[:, capacity:], axis=0)
+
+
+def gather_blocks(arrays, blocks, local_row, local_counts, table, capacity):
     n = lax.axis_size(BOTH)
     if special():
-        blocks = [g.astype(LOW).reshape(4, 2, 2, 2, -1, g.shape[-1]) for g in grads]
-        shaped = vector.reshape(n, -1, 128)
-        *parts, arrived, pieces = scatter_grads(blocks, buckets, shaped)
-        return parts, arrived, jnp.sum(pieces, axis=0).reshape(-1)
-    parts = [
-        lax.psum_scatter(g.astype(jnp.float32), BOTH, scatter_dimension=0, tiled=True)
-        for g in grads
+        row = local_row.astype(jnp.int32)
+        values = jnp.stack([row // 256, row % 256, jnp.ones_like(row)], axis=1).astype(LOW)
+        tally = jnp.pad(local_counts.astype(jnp.float32), (3, 125 - MICRO)).reshape(1, 128)
+        *gathered, rows, to_slot, from_slot, answer = gather_weights(
+            arrays, blocks.reshape(1, -1), jnp.pad(values, ((0, 0), (0, 125))), tally, table
+        )
+        full = [g.reshape((-1, a.shape[-1])) for g, a in zip(gathered, arrays)]
+        counts = jnp.sum(answer[:, 0, 3 : 3 + MICRO], axis=0)
+        return full, rows, to_slot, from_slot.reshape(n * capacity, -1), counts
+    to_slot, from_slot, counts = ask_rows(
+        blocks, local_row, local_counts, table.shape[0], capacity
+    )
+    found = multiply(from_slot, table).astype(LOW).reshape(n, capacity, D)
+    full = [lax.all_gather(a, BOTH, axis=0, tiled=True) for a in arrays]
+    return full, swap(found), to_slot, from_slot, counts.astype(jnp.float32)
+
+
+def reduce_blocks(pairs, grad_pos, grad_head, buckets, vector):
+    n = lax.axis_size(BOTH)
+    if special():
+        side = jnp.concatenate([grad_pos.astype(LOW), grad_head.astype(LOW)], axis=0)
+        grad_in, grad_down, grad_side, arrived, pieces = scatter_grads(
+            pairs, side.reshape(4, 2, 2, 2, -1, D), buckets, vector.reshape(n, -1, 128)
+        )
+        return grad_side, grad_in, grad_down, arrived, jnp.sum(pieces, axis=0).reshape(-1)
+    down, up, joint, attended = [
+        multiply(pairs[2 * i], pairs[2 * i + 1]) for i in range(4)
     ]
+
+    def own(value):
+        return lax.psum_scatter(value, BOTH, scatter_dimension=0, tiled=True)
+
     return (
-        parts,
+        own(jnp.concatenate([grad_pos, grad_head], axis=0)),
+        own(jnp.concatenate([joint, attended, up], axis=0)),
+        own(down),
         swap(buckets),
-        lax.psum_scatter(vector, BOTH, scatter_dimension=0, tiled=True),
+        own(vector),
     )
 
 
@@ -757,39 +997,25 @@
     capacity = max(2, 2 * tokens // n_blocks)
     flat_ids = token_ids.reshape(tokens)
     blocks = flat_ids // block_rows
-    onehot = (blocks[:, None] == jnp.arange(n_blocks)[None, :]).astype(jnp.int32)
-    rank = jnp.sum(jnp.cumsum(onehot, axis=0) * onehot, axis=1) - 1
-    slot = blocks * capacity + rank
-    bucket_ids = jnp.full((n_blocks * capacity,), -1, jnp.int32).at[slot].set(flat_ids)
-    message = jnp.concatenate(
-        [
-            bucket_ids.reshape(n_blocks, capacity),
-            jnp.broadcast_to(local_counts.astype(jnp.int32)[None, :], (n_blocks, MICRO)),
-        ],
-        axis=1,
-    )
-    answer = swap(message)
-    asked = answer[:, :capacity].reshape(-1)
-    counts = jnp.sum(answer[:, capacity:], axis=0).astype(jnp.float32)
-    asked_row = jnp.where(asked >= 0, asked - my_index * block_rows, -1)
-    found = jnp.take(
-        word_table.astype(LOW), jnp.clip(asked_row, 0, block_rows - 1), axis=0
-    ).reshape(n_blocks, capacity, D)
-    seq_count = jnp.sum(member * counts[None, :], axis=1)
-    token_weight = (mask_float / (seq_count * MICRO)[:, None]).reshape(tokens)
     label_float = labels.astype(jnp.float32).reshape(tokens)
 
     side_rows_local = side_mat.shape[0]
     vec_local = vectors.shape[0]
     vector_row = jnp.pad(vectors.astype(LOW).reshape(1, -1), ((0, 15), (0, D - vec_local)))
-    (side_all, weight_in, weight_down), returned = gather_blocks(
+    (side_all, weight_in, weight_down), returned, to_slot, from_slot, counts = gather_blocks(
         [
             jnp.concatenate([side_mat.astype(LOW), vector_row], axis=0),
             layer_in[0].astype(LOW).T,
             layer_down[0].astype(LOW),
         ],
-        found,
-    )
+        blocks,
+        flat_ids - blocks * block_rows,
+        local_counts.astype(jnp.int32),
+        word_table.astype(LOW),
+        capacity,
+    )
+    seq_count = jnp.sum(member * counts[None, :], axis=1)
+    token_weight = (mask_float / (seq_count * MICRO)[:, None]).reshape(tokens)
     side_all = side_all.reshape(n_blocks, side_rows_local + 16, D)
     side_full = side_all[:, :side_rows_local].reshape(-1, D)
     vector_full = side_all[:, side_rows_local, :vec_local].reshape(-1)
@@ -802,8 +1028,7 @@
     head_bias = all_vectors[global_offset + 2 * D : global_offset + 3 * D]
     predictor = all_vectors[global_offset + 3 * D : global_offset + 4 * D]
     predictor_low = vector_full[global_offset + 3 * D : global_offset + 4 * D]
-    to_slot = (slot[:, None] == jnp.arange(n_blocks * capacity)[None, :]).astype(LOW)
-    own_rows = multiply(to_slot, returned.reshape(n_blocks * capacity, D))
+    own_rows = multiply_left(to_slot, returned.reshape(n_blocks * capacity, D))
     embedded = (own_rows.reshape(seq_dev, length, D) + pos_rows[None, :, :]).reshape(tokens, D)
     hidden = layer_norm(embedded, gain_emb, shift_emb)
     pieces = layer_slices(all_vectors, 0)
@@ -819,29 +1044,21 @@
     grad_head = multiply_left(final_low, d_head_low)
     d_head_bias = jnp.sum(d_head_low.astype(jnp.float32), axis=0)
     d_hidden = multiply_right(d_head_low, head_mat)
-    d_hidden, grads_in, grad_down, grad_pieces = layer_backward(
+    d_hidden, pairs, grad_pieces = layer_backward(
         d_hidden, weight_in, weight_down, pieces, kept, seq_dev
     )
     d_embedded, d_gain_emb, d_shift_emb = norm_back(embedded, gain_emb, shift_emb, d_hidden)
     grad_pos = jnp.sum(d_embedded.reshape(seq_dev, length, D), axis=0)
     grad_vector = jnp.concatenate([grad_pieces, d_gain_emb, d_shift_emb, d_head_bias, d_predictor])
     buckets = (
-        multiply_left(to_slot, d_embedded.astype(LOW))
+        multiply(to_slot, d_embedded.astype(LOW))
         .astype(LOW)
         .reshape(n_blocks, capacity, D)
     )
-    kind = LOW if special() else jnp.float32
-    (grad_side, grad_in_t, grad_down), arrived, grad_vec = reduce_blocks(
-        [
-            jnp.concatenate([grad_pos.astype(kind), grad_head.astype(kind)], axis=0),
-            jnp.concatenate([g.astype(kind) for g in grads_in], axis=0),
-            grad_down,
-        ],
-        buckets,
-        grad_vector,
-    )
-    from_slot = (asked_row[None, :] == jnp.arange(block_rows)[:, None]).astype(LOW)
-    grad_word = multiply(from_slot, arrived.reshape(n_blocks * capacity, D))
+    grad_side, grad_in_t, grad_down, arrived, grad_vec = reduce_blocks(
+        pairs, grad_pos, grad_head, buckets, grad_vector
+    )
+    grad_word = multiply_left(from_slot, arrived.reshape(n_blocks * capacity, D))
     grad_in = grad_in_t.T
 
     col_local = layer_in.shape[2]

time: 739 us -> 649 us (0.88)
  Pallas kernels: 411 us -> 380 us
  matrix products: 158 us -> 135 us
  other arithmetic: 99.7 us -> 79.2 us
  local copies, waits for them, and re-layouts: 47 us -> 38.5 us
  starting transfers between devices: 8.34 us -> 0 us
    pallas_call x1, Pallas kernels: 224 us -> 184 us  [gather_weights(): pl.pallas_call(functools.partial(gather_kernel, plan, count), name='gathe...]
    dot_general x8 -> x5, matrix products: 34.1 us -> 19.7 us  [multiply(): return jnp.dot(left_side, right_side, preferred_element_type=jnp.float32)]
    pallas_call x1, Pallas kernels: 170 us -> 180 us  [scatter_grads(): pl.pallas_call(functools.partial(scatter_kernel, groups, len(pairs)), nam...]
    concatenate x3 -> x1, other arithmetic: 11.4 us -> 1.97 us  [reduce_blocks(): jnp.concatenate([grad_pos.astype(LOW), grad_head.astype(LOW)], axis=0)]
    all_to_all x1 -> x0, starting transfers between devices: 8.34 us -> none  [swap(): lax.all_to_all(split, 'fsdp', split_axis=0, concat_axis=0, tiled=True)]
    dot_general x6 -> x5, matrix products: 27.9 us -> 22.6 us  [multiply_left(): lax.dot_general(left_side, right_side, (((0,), (0,)), ((), ())), preferre...]
  transfers between devices with their start and end apart: 1 -> 0, of which waited for: 0 -> 0; matrix products, arithmetic and copies ran while one was open for 2% -> 0% of each run, Pallas kernels for 0% -> 0%
where the time goes in v2:
time: 649 us; the launch traced here: 639 us
  Pallas kernels  380 us (59%)
  matrix products  135 us (21%)
  other arithmetic  79.2 us (12%)
  local copies, waits for them, and re-layouts  38.5 us (6%)
    pallas_call x1, Pallas kernels, gather_weights(): pl.pallas_call(functools.partial(gather_kernel, plan, count), name='gathe...  184 us
    pallas_call x1, Pallas kernels, scatter_grads(): pl.pallas_call(functools.partial(scatter_kernel, groups, len(pairs)), nam...  180 us
    dot_general x5, matrix products, multiply_right(): lax.dot_general(left_side, right_side, (((1,), (1,)), ((), ())), preferre...  54 us
    dot_general x5, matrix products, multiply_left(): lax.dot_general(left_side, right_side, (((0,), (0,)), ((), ())), preferre...  22.6 us
    dot_general x5, matrix products, multiply(): return jnp.dot(left_side, right_side, preferred_element_type=jnp.float32)  19.7 us
    pallas_call x1, Pallas kernels, sum_over_devices(): pl.pallas_call(sum_kernel, name='sum_over_devices', out_shape=jax.ShapeDt...  15.7 us

profile of v2, /device:TPU:0, one launch (start us, length us, event | category | flops | bytes accessed | tf_op | source)
XLA Modules:
  0.0 638.8 jit_solution(9931935592341867516)
XLA Ops:
  19.5 3.7 convert_element_type.230.refs_6_
  23.2 183.7 %gather_weights.1 = (bf16[4,2,2,2,64,1024]{5,4,3,2,1,0:T(8,128)(2,1)}, bf16[4,2,2,2,256,1024]{5,4,3,2,1,0:T(8,128)(2,1)}, bf16[4,2,2,2,128,1024]{5,4,3,2,1,0:T(8...) custom-call(bf16[64,1024]{1,0:T(8,128)(2,1)} %fusion.63.refs_0_, ...), custom_call_target="tpu_custom_call" | custom-call | tf_op jit(solution)/shard_map/gather_weights/pallas_call | solution.py:526
  217.0 7.6 %add_convert_fusion.1 = bf16[512,3072]{1,0:T(8,128)(2,1)} fusion(bf16[512,1024]{1,0:T(8,128)(2,1)S(1)} %fusion.45.refs_5_, bf16[8192,1024]{1,0:T(8,128)(2,1)} %bitcast.259, f32[3072]{0:T(1024)S(1)} %pad_maximum_fusion.3), kind=kOutput, calls=%fused_computation.32 | convolution fusion | flops 3224371200 | bytes 10498048 | tf_op jit(solution)/shard_map/dot_general | solution.py:63
  224.6 4.7 copy.109
  229.3 8.1 %slice.226 = bf16[2,2,2,2,256,1024]{5,4,3,2,1,0:T(8,128)(2,1)} slice(bf16[4,2,2,2,256,1024]{5,4,3,2,1,0:T(8,128)(2,1)} %get-tuple-element.32), slice={[2:4], [0:2], [0:2], [0:2], [0:256], [0:1024]} | slice | bytes 16777216 | tf_op jit(solution)/shard_map/slice | solution.py:153
  237.4 7.5 %multiply_reduce_fusion.1 = (f32[16,512]{1,0:T(8,128)S(1)}, f32[16,512,512]{1,2,0:T(8,128)}) fusion(bf16[1,512,3,16,64]{1,4,3,2,0:T(8,128)(2,1)S(1)} %bitcast.242), kind=kOutput, calls=%fused_computation.6 | convolution fusion | flops 545251328 | bytes 18907136 | tf_op jit(solution)/shard_map/vmap(qhe,khe->hqk)/dot_general | solution.py:98
  244.9 8.6 %fusion = f32[16,512]{1,0:T(8,128)S(1)} fusion(f32[16,512,512]{1,2,0:T(8,128)} %get-tuple-element.267, f32[16,512]{1,0:T(8,128)S(1)} %get-tuple-element.266), kind=kLoop, calls=%fused_computation.5 | loop fusion | flops 12574720 | bytes 16842752 | tf_op jit(solution)/shard_map/vmap()/reduce_sum | solution.py:103
  254.1 7.9 %fusion.52 = bf16[16,64,512]{2,1,0:T(8,128)(2,1)S(1)} fusion(f32[16,512,512]{1,2,0:T(8,128)} %get-tuple-element.267, f32[16,512]{1,0:T(8,128)S(1)} %fusion, f32[16,512]{1,0:T(8,128)S(1)} %get-tuple-element.266, bf16[1,512,3,16,64]{1,4,3,2,0:T(8,128)(2,1)} %bitcast.241), kind=kOutput, calls=%fused_computation.114 | convolution fusion | flops 554172416 | bytes 18939904 | tf_op jit(solution)/shard_map/vmap(hqk,khe->qhe)/dot_general | solution.py:105
  263.4 3.4 fusion.132
  267.6 26.5 %multiply_convert_fusion.1 = (bf16[4096,512]{1,0:T(8,128)(2,1)S(1)}, f32[4096,512]{1,0:T(8,128)}, f32[4096,512]{1,0:T(8,128)}) fusion(f32[4096]{0:T(1024)S(1)} %bitcast.307, bf16[4096,1024]{1,0:T(8,128)(2,1)} %bitcast.251, bf16[512,1024]{1,0:T(8,128)(2,1)S(1)} %fusion.46.refs_3_), kind=kOutput, calls=%fused_computation.14 | convolution fusion | flops 4433379328 | bytes 30425088 | tf_op jit(solution)/shard_map/dot_general | solution.py:63
  294.2 4.8 fusion.133
  299.4 5.6 multiply_convert_fusion.2
  310.4 2.8 convolution_convert_fusion.1
  313.5 14.4 %convert_reduce_fusion = (f32[4096]{0:T(1024)S(1)}, bf16[4096,512]{1,0:T(8,128)(2,1)}) fusion(f32[4096,512]{1,0:T(8,128)} %get-tuple-element.216, f32[4096,512]{1,0:T(8,128)} %get-tuple-element.270, f32[4096]{0:T(1024)S(1)} %bitcast.308, bf16[4096,1024]{1,0:T(8,128)(2,1)} %bitcast.339, bf16[512,1024]{1,0:T(8,128)(2,1)S(1)} %get-tuple-element.200.refs_1_), kind=kOutput, calls=%fused_computation.11 | convolution fusion | flops 4330614784 | bytes 30441472 | tf_op jit(solution)/shard_map/dot_general | solution.py:63
  327.9 7.0 %multiply_reduce_fusion.6 = (f32[1024]{0:T(1024)S(1)}, f32[512]{0:T(512)S(1)}, f32[1024]{0:T(1024)S(1)}, f32[512,1024]{1,0:T(8,128)S(1)}) fusion(f32[512,1024]{1,0:T(8,128)S(1)} %get-tuple-element.269, f32[512]{0:T(512)S(1)} %fusion.90, f32[512]{0:T(512)S(1)} %broadcast_multiply_fusion.2, f32[1024]{0:T(1024)S(1)} %bitcast.290, ...), kind=kOutput, calls=%fused_computation.66 | convolution fusion | flops 4300207616 | bytes 18894848 | tf_op jit(solution)/shard_map/dot_general | solution.py:57
  338.5 2.8 fusion.53
  342.1 7.7 %fusion.47 = bf16[1,512,1,16,64]{1,4,3,2,0:T(8,128)(2,1)S(1)} fusion(bf16[512,16,64]{0,2,1:T(8,128)(2,1)S(1)} %bitcast.249, f32[16,512,512]{1,2,0:T(8,128)} %get-tuple-element.267, f32[16,512]{1,0:T(8,128)S(1)} %copy-done.23), kind=kOutput, calls=%fused_computation.113 | convolution fusion | flops 549453824 | bytes 18907136 | tf_op jit(solution)/shard_map/vmap(hqk,qhe->khe)/dot_general | solution.py:118
  349.8 11.3 %multiply_reduce_fusion = (f32[16,512]{1,0:T(8,128)S(1)}, f32[16,512,512]{1,2,0:T(8,128)}) fusion(f32[16,512,512]{1,2,0:T(8,128)} %get-tuple-element.267, f32[16,512]{1,0:T(8,128)S(1)} %copy-done.23, bf16[512,16,64]{0,2,1:T(8,128)(2,1)S(1)} %bitcast.250, bf16[1,512,3,16,64]{1,4,3,2,0:T(8,128)(2,1)S(1)} %bitcast.243), kind=kOutput, calls=%fused_computation.1 | convolution fusion | flops 553639936 | bytes 35717120 | tf_op jit(solution)/shard_map/vmap(qhe,khe->hqk)/dot_general | solution.py:124
  361.1 11.8 %multiply_convert_fusion = bf16[16,512,512]{1,2,0:T(8,128)(2,1)S(1)} fusion(f32[16,512,512]{1,2,0:T(8,128)} %get-tuple-element.277, f32[16,512,512]{1,2,0:T(8,128)} %get-tuple-element.267, f32[16,512]{1,0:T(8,128)S(1)} %get-tuple-element.276, f32[16,512]{1,0:T(8,128)S(1)} %copy-done.23), kind=kLoop, calls=%fused_computation | loop fusion | flops 20971520 | bytes 42008576 | tf_op jit(solution)/shard_map/vmap()/convert_element_type | solution.py:126
  379.3 8.3 %multiply_reduce_fusion.4 = (f32[1024]{0:T(1024)S(1)}, f32[512]{0:T(512)S(1)}, f32[1024]{0:T(1024)S(1)}, f32[512,1024]{1,0:T(8,128)S(1)}) fusion(f32[512,1024]{1,0:T(8,128)S(1)} %copy-done.1, f32[512]{0:T(512)S(1)} %copy-done.37, f32[512]{0:T(512)S(1)} %copy-done.35, f32[1024]{0:T(1024)S(1)} %bitcast.286, bf16[512,3072]{0,1:T(8,128)(2,1)} %bitcast.246, ...), kind=kOutput, calls=%fused_computation.63 | convolution fusion | flops 3226465792 | bytes 15749120 | tf_op jit(solution)/shard_map/dot_general | solution.py:53
  394.1 180.5 %scatter_grads.1 = (f32[256,1024]{1,0:T(8,128)}, f32[128,1024]{1,0:T(8,128)}, f32[48,1024]{1,0:T(8,128)}, bf16[32,32,1024]{2,1,0:T(8,128)(2,1)}, f32[32,4,128]{2,1,0:T(4,128)}) custom-call(bf16[16,2,128,512]{3,2,1,0:T(8,128)(2,1)} %bitcast.264, bf16[512,1024]{1,0:T(8,128)(2,1)} %copy-done.14, bf16[8,2,256,512]{3,2,1,0:T(8,128)(2,1)} %bitcast.265, ...), custom_call_target="tpu_custom_call" | custom-call | tf_op jit(solution)/shard_map/scatter_grads/pallas_call | solution.py:792
  574.7 6.6 %fusion.22 = (f32[960]{0:T(1024)S(1)}, f32[960,1024,1]{1,0,2:T(8,128)}) fusion(bf16[32,32,960]{2,1,0:T(8,128)(2,1)} %get-tuple-element.40, bf16[32,32,1024]{2,1,0:T(8,128)(2,1)} %get-tuple-element.41), kind=kOutput, calls=%fused_computation.43 | convolution fusion | flops 2016214016 | bytes 7999232 | tf_op jit(solution)/shard_map/dot_general | solution.py:57
  590.8 15.7 %sum_over_devices.1 = f32[32,4,128]{2,1,0:T(4,128)} custom-call(f32[32,4,128]{2,1,0:T(4,128)} %bitcast.275), custom_call_target="tpu_custom_call" | custom-call | tf_op jit(solution)/shard_map/sum_over_devices/pallas_call | solution.py:865
  631.7 6.8 %fusion.111 = (bf16[960,1024]{1,0:T(8,128)(2,1)}, f32[960,1024]{1,0:T(8,128)}) fusion(f32[960,1024]{1,0:T(8,128)} %param.27, f32[]{:T(128)} %bitcast.100, f32[1024]{0:T(1024)S(1)} %get-tuple-element.178, f32[960]{0:T(1024)S(1)} %get-tuple-element.188, f32[960,1024,1]{1,0,2:T(8,128)} %get-tuple-element.280, f32[]{:T(128)S(6)} %div.389), kind=kLoop, calls=%fused_computation.303 | loop fusion | flops 5898240 | bytes 13770504 | tf_op jit(solution)/shard_map/convert_element_type | solution.py:1196
  (310 shorter events, 84.6 us)
Async XLA Ops:
  23.2 186.0 %copy-start.44 = (s32[1,512]{1,0:T(1,128)S(1)}, s32[1,512]{1,0:T(1,128)}, u32[]{:S(2)}) copy-start(s32[1,512]{1,0:T(1,128)} %param.23) | copy-start | bytes 6148
  215.2 48.2 %copy-start = (f32[512,1024]{1,0:T(8,128)}, f32[512,1024]{1,0:T(8,128)S(1)}, u32[]{:S(2)}) copy-start(f32[512,1024]{1,0:T(8,128)S(1)} %get-tuple-element.265) | copy-start | bytes 6291460
  215.2 48.2 %copy-start.34 = (f32[512]{0:T(512)}, f32[512]{0:T(512)S(1)}, u32[]{:S(2)}) copy-start(f32[512]{0:T(512)S(1)} %broadcast_multiply_fusion.3) | copy-start | bytes 6148
  215.6 47.8 %copy-start.36 = (f32[512]{0:T(512)}, f32[512]{0:T(512)S(1)}, u32[]{:S(2)}) copy-start(f32[512]{0:T(512)S(1)} %fusion.89) | copy-start | bytes 6148
  215.6 47.8 %copy-start.31 = (f32[2,1,512]{2,1,0:T(1,128)}, f32[2,1,512]{2,1,0:T(1,128)S(1)}, u32[]{:S(2)}) copy-start(f32[2,1,512]{2,1,0:T(1,128)S(1)} %get-tuple-element.243) | copy-start | bytes 12292
  266.8 27.4 %slice-start.2 = ((s8[8388608]{0:T(1024)(128)(4,1)}), s8[4194304]{0:T(1024)(128)(4,1)S(1)}, s32[]{:S(2)}) async-start(s8[8388608]{0:T(1024)(128)(4,1)} %bitcast.340), calls=%async_computation.2 | async-start | bytes 8388608
  267.6 26.6 %copy-start.13 = (bf16[512,1024]{1,0:T(8,128)(2,1)}, bf16[512,1024]{1,0:T(8,128)(2,1)S(1)}, u32[]{:S(2)}) copy-start(bf16[512,1024]{1,0:T(8,128)(2,1)S(1)} %fusion.46.refs_3_) | copy-start | bytes 3145732
  267.6 26.6 %slice-start.3 = ((s8[8388608]{0:T(1024)(128)(4,1)}), s8[4194304]{0:T(1024)(128)(4,1)S(1)}, s32[]{:S(2)}) async-start(s8[8388608]{0:T(1024)(128)(4,1)} %bitcast.340), calls=%async_computation.3 | async-start | bytes 8388608
  582.1 40.2 %copy-start.50 = (f32[48]{0:T(128)}, f32[48]{0:T(128)S(1)}, u32[]{:S(2)}) copy-start(f32[48]{0:T(128)S(1)} %get-tuple-element.192) | copy-start | bytes 580
  583.5 48.3 %copy-start.28 = (f32[960]{0:T(1024)}, f32[960]{0:T(1024)S(1)}, u32[]{:S(2)}) copy-start(f32[960]{0:T(1024)S(1)} %get-tuple-element.188) | copy-start | bytes 11524
  583.7 42.3 %copy-start.43 = (f32[1,256]{1,0:T(1,128)}, f32[1,256]{1,0:T(1,128)S(1)}, u32[]{:S(2)}) copy-start(f32[1,256]{1,0:T(1,128)S(1)} %get-tuple-element.194) | copy-start | bytes 3076
  586.8 24.9 %copy-start.30 = (f32[1,1024]{1,0:T(1,128)S(1)}, f32[1,1024]{1,0:T(1,128)}, u32[]{:S(2)}) copy-start(f32[1,1024]{1,0:T(1,128)} %broadcast_multiply_fusion) | copy-start | bytes 12292
  586.9 27.0 %copy-start.52 = (f32[1024]{0:T(1024)S(1)}, f32[1024]{0:T(1024)}, u32[]{:S(2)}) copy-start(f32[1024]{0:T(1024)} %param.35) | copy-start | bytes 12292
  586.9 28.4 %copy-start.42 = (f32[1,1024]{1,0:T(1,128)S(1)}, f32[1,1024]{1,0:T(1,128)}, u32[]{:S(2)}) copy-start(f32[1,1024]{1,0:T(1,128)} %param.33) | copy-start | bytes 12292
  586.9 29.0 %copy-start.24 = (f32[1,3,1024]{2,0,1:T(1,128)S(1)}, f32[1,3,1024]{2,0,1:T(1,128)}, u32[]{:S(2)}) copy-start(f32[1,3,1024]{2,0,1:T(1,128)} %param.30) | copy-start | bytes 36868
  586.9 29.0 %copy-start.54 = (f32[3]{0:T(128)S(1)}, f32[3]{0:T(128)}, u32[]{:S(2)}) copy-start(f32[3]{0:T(128)} %constant.316) | copy-start | bytes 40
  586.9 29.1 %copy-start.66 = (f32[3]{0:T(128)S(1)}, f32[3]{0:T(128)}, u32[]{:S(2)}) copy-start(f32[3]{0:T(128)} %constant.323) | copy-start | bytes 40
  586.9 29.2 %copy-start.53 = (pred[3,256]{1,0:T(4,128)(4,1)S(1)}, pred[3,256]{1,0:T(4,128)(4,1)}, u32[]{:S(2)}) copy-start(pred[3,256]{1,0:T(4,128)(4,1)} %get-tuple-element.196) | copy-start | bytes 2308
  586.9 30.7 %copy-start.46 = (f32[2,1024]{1,0:T(2,128)S(1)}, f32[2,1024]{1,0:T(2,128)}, u32[]{:S(2)}) copy-start(f32[2,1024]{1,0:T(2,128)} %param.37) | copy-start | bytes 24580
  586.9 30.7 %copy-start.56 = (f32[2]{0:T(128)S(1)}, f32[2]{0:T(128)}, u32[]{:S(2)}) copy-start(f32[2]{0:T(128)} %constant.318) | copy-start | bytes 28
  586.9 30.9 %copy-start.68 = (f32[2]{0:T(128)S(1)}, f32[2]{0:T(128)}, u32[]{:S(2)}) copy-start(f32[2]{0:T(128)} %constant.324) | copy-start | bytes 28
  587.0 35.4 %copy-start.22 = (f32[48,1024]{1,0:T(8,128)S(1)}, f32[48,1024]{1,0:T(8,128)}, u32[]{:S(2)}) copy-start(f32[48,1024]{1,0:T(8,128)} %param.28) | copy-start | bytes 589828
  587.0 35.4 %copy-start.69 = (pred[48]{0:T(512)(128)(4,1)S(1)}, pred[48]{0:T(512)(128)(4,1)}, u32[]{:S(2)}) copy-start(pred[48]{0:T(512)(128)(4,1)} %add_compare_fusion) | copy-start | bytes 148
  587.0 36.2 %copy-start.17 = (f32[1,128,1024]{2,1,0:T(8,128)S(1)}, f32[1,128,1024]{2,1,0:T(8,128)}, u32[]{:S(2)}) copy-start(f32[1,128,1024]{2,1,0:T(8,128)} %param.26) | copy-start | bytes 1572868
  (51 other events, 412.0 us)

commit v3 on v2

--- a/solution.py
+++ b/solution.py
@@ -94,64 +94,128 @@
     return jnp.array(sizes + [D, D, D, D], jnp.float32)
 
 
-def attend(queries, key_rows, values):
-    scores = jnp.einsum(
-        "qhe,khe->hqk", queries, key_rows, preferred_element_type=jnp.float32
-    ) * HEAD_DIM ** (-0.5)
-    peak_score = jnp.max(scores, axis=-1, keepdims=True)
-    exponent = jnp.exp(scores - peak_score)
-    running = jnp.sum(exponent, axis=-1, keepdims=True)
-    soft_probs = exponent / running
-    context = jnp.einsum(
-        "hqk,khe->qhe", soft_probs.astype(jnp.bfloat16), values, preferred_element_type=jnp.float32
-    )
-    return (context, peak_score + jnp.log(running))
-
-
-def attend_back(queries, key_rows, values, log_total, d_context):
-    score_scale = HEAD_DIM ** (-0.5)
-    scores = (
-        jnp.einsum("qhe,khe->hqk", queries, key_rows, preferred_element_type=jnp.float32)
-        * score_scale
-    )
-    soft_probs = jnp.exp(scores - log_total)
-    d_values = jnp.einsum(
-        "hqk,qhe->khe",
-        soft_probs.astype(jnp.bfloat16),
-        d_context,
-        preferred_element_type=jnp.float32,
-    )
-    d_probs = jnp.einsum("qhe,khe->hqk", d_context, values, preferred_element_type=jnp.float32)
-    d_scores = soft_probs * (d_probs - jnp.sum(d_probs * soft_probs, axis=-1, keepdims=True))
-    d_scores_low = d_scores.astype(jnp.bfloat16)
-    d_queries = (
-        jnp.einsum("hqk,khe->qhe", d_scores_low, key_rows, preferred_element_type=jnp.float32)
-        * score_scale
-    )
-    d_keys = (
-        jnp.einsum("hqk,qhe->khe", d_scores_low, queries, preferred_element_type=jnp.float32)
-        * score_scale
-    )
-    return jnp.stack([d_queries, d_keys, d_values], axis=1)
+def head_parts(ref):
+    both = ref[...]
+    return both[:, :HEAD_DIM], both[:, HEAD_DIM:]
+
+
+def key_scores(queries, key_rows):
+    return multiply_right(key_rows, queries) * HEAD_DIM ** (-0.5)
+
+
+def attend_kernel(q_ref, k_ref, v_ref, context_ref, total_ref):
+    contexts = []
+    for head, (queries, key_rows, values) in enumerate(
+        zip(head_parts(q_ref), head_parts(k_ref), head_parts(v_ref))
+    ):
+        scores = key_scores(queries, key_rows)
+        peak = jnp.max(scores, axis=0, keepdims=True)
+        exponent = jnp.exp(scores - peak)
+        running = jnp.sum(exponent, axis=0, keepdims=True)
+        soft_probs = (exponent / running).astype(LOW)
+        contexts.append(multiply_left(values, soft_probs))
+        total_ref[head] = peak + jnp.log(running)
+    context_ref[...] = jnp.concatenate(contexts, axis=0).T.astype(LOW)
+
+
+def attend_back_kernel(q_ref, k_ref, v_ref, d_ref, total_ref, out_ref):
+    scale = HEAD_DIM ** (-0.5)
+    for head, (queries, key_rows, values, d_context) in enumerate(
+        zip(head_parts(q_ref), head_parts(k_ref), head_parts(v_ref), head_parts(d_ref))
+    ):
+        soft_probs = jnp.exp(key_scores(queries, key_rows) - total_ref[head])
+        d_values = multiply(soft_probs.astype(LOW), d_context)
+        d_probs = multiply_right(values, d_context)
+        inner = jnp.sum(d_probs * soft_probs, axis=0, keepdims=True)
+        d_scores = (soft_probs * (d_probs - inner)).astype(LOW)
+        part = pl.ds(head * HEAD_DIM, HEAD_DIM)
+        out_ref[0, part] = (multiply_left(key_rows, d_scores) * scale).astype(LOW)
+        out_ref[1, part] = (multiply(d_scores, queries) * scale).T.astype(LOW)
+        out_ref[2, part] = d_values.T.astype(LOW)
+
+
+def attention_specs(tokens, length):
+    pairs = HEADS // 2
+    wide = 2 * HEAD_DIM
+
+    def joint(third):
+        return pl.BlockSpec((length, wide), lambda s, i: (s, third * pairs + i))
+
+    total = pl.BlockSpec((2, 1, length), lambda s, i: (i, 0, s))
+    return (tokens // length, pairs), [joint(0), joint(1), joint(2)], joint(0), total
+
+
+def attend(projected, seq_dev):
+    tokens = projected.shape[0]
+    grid, ins, context, total = attention_specs(tokens, tokens // seq_dev)
+    return pl.pallas_call(
+        attend_kernel,
+        name="attend",
+        grid=grid,
+        in_specs=ins,
+        out_specs=(context, total),
+        out_shape=(
+            jax.ShapeDtypeStruct((tokens, D), LOW),
+            jax.ShapeDtypeStruct((HEADS, 1, tokens), jnp.float32),
+        ),
+    )(projected, projected, projected)
+
+
+def attend_back(projected, log_total, d_context, seq_dev):
+    tokens = projected.shape[0]
+    length = tokens // seq_dev
+    grid, ins, context, total = attention_specs(tokens, length)
+    return pl.pallas_call(
+        attend_back_kernel,
+        name="attend_back",
+        grid=grid,
+        in_specs=ins + [context, total],
+        out_specs=pl.BlockSpec((3, 2 * HEAD_DIM, length), lambda s, i: (0, i, s)),
+        out_shape=jax.ShapeDtypeStruct((3, D, tokens), LOW),
+    )(projected, projected, projected, d_context, log_total).reshape(3 * D, tokens)
+
+
+def lift_kernel(weight_ref, bias_ref, middle_ref, active_ref, slope_ref):
+    lifted = multiply_right(weight_ref[...], middle_ref[...]) + bias_ref[...]
+    cumulative = 0.5 + 0.5 * lax.erf(lifted * (0.5**0.5))
+    density = jnp.exp(-0.5 * lifted * lifted) * ((0.5 / math.pi) ** 0.5)
+    active_ref[...] = (lifted * cumulative).astype(LOW)
+    slope_ref[...] = cumulative + lifted * density
+
+
+def lift(weight_in, bias_up, middle_low):
+    tokens = middle_low.shape[0]
+    rows = 512
+    return pl.pallas_call(
+        lift_kernel,
+        name="lift",
+        grid=(FF // rows,),
+        in_specs=[
+            pl.BlockSpec((rows, D), lambda i: (4 * D // rows + i, 0)),
+            pl.BlockSpec((rows, 1), lambda i: (i, 0)),
+            pl.BlockSpec((tokens, D), lambda i: (0, 0)),
+        ],
+        out_specs=(
+            pl.BlockSpec((rows, tokens), lambda i: (i, 0)),
+            pl.BlockSpec((rows, tokens), lambda i: (i, 0)),
+        ),
+        out_shape=(
+            jax.ShapeDtypeStruct((FF, tokens), LOW),
+            jax.ShapeDtypeStruct((FF, tokens), jnp.float32),
+        ),
+    )(weight_in, bias_up[:, None], middle_low)
 
 
 def layer_forward(hidden, weight_in, weight_down, pieces, seq_dev):
     bias_q, bias_v, bias_o, gain_a, shift_a, bias_up, bias_down, gain_b, shift_b = pieces
-    tokens = hidden.shape[0]
-    length = tokens // seq_dev
     hidden_low = hidden.astype(jnp.bfloat16)
     joint_bias = jnp.concatenate([bias_q, jnp.zeros_like(bias_q), bias_v])
     projected = (multiply_right(hidden_low, weight_in[: 3 * D]) + joint_bias).astype(jnp.bfloat16)
-    heads_view = projected.reshape(seq_dev, length, 3, HEADS, HEAD_DIM)
-    context, log_total = jax.vmap(attend)(
-        heads_view[:, :, 0], heads_view[:, :, 1], heads_view[:, :, 2]
-    )
-    context_low = context.reshape(tokens, D).astype(jnp.bfloat16)
+    context_low, log_total = attend(projected, seq_dev)
     mid_in = hidden + (multiply_right(context_low, weight_in[3 * D : 4 * D]) + bias_o)
     middle = layer_norm(mid_in, gain_a, shift_a)
     middle_low = middle.astype(jnp.bfloat16)
-    lifted = multiply_right(weight_in[4 * D :], middle_low) + bias_up[:, None]
-    active_low = exact_gelu(lifted).astype(jnp.bfloat16)
+    active_low, slope = lift(weight_in, bias_up, middle_low)
     out_in = middle + (multiply_left(active_low, weight_down) + bias_down)
     output = layer_norm(out_in, gain_b, shift_b)
     return (
@@ -163,7 +227,7 @@
             context_low,
             mid_in,
             middle_low,
-            lifted,
+            slope,
             active_low,
             out_in,
         ),
@@ -179,30 +243,20 @@
         context_low,
         mid_in,
         middle_low,
-        lifted,
+        slope,
         active_low,
         out_in,
     ) = kept
-    tokens = mid_in.shape[0]
-    length = tokens // seq_dev
     d_out_in, d_gain_b, d_shift_b = norm_back(out_in, gain_b, shift_b, grad_out)
     d_down_low = d_out_in.astype(jnp.bfloat16)
-    d_lifted_low = gelu_back(lifted, multiply_right(weight_down, d_down_low)).astype(jnp.bfloat16)
+    d_lifted_low = (multiply_right(weight_down, d_down_low) * slope).astype(jnp.bfloat16)
     d_middle = d_out_in + multiply_left(d_lifted_low, weight_in[4 * D :])
     d_mid_in, d_gain_a, d_shift_a = norm_back(mid_in, gain_a, shift_a, d_middle)
     d_attended_low = d_mid_in.astype(jnp.bfloat16)
     d_context_low = multiply(d_attended_low, weight_in[3 * D : 4 * D]).astype(jnp.bfloat16)
-    heads_view = projected.reshape(seq_dev, length, 3, HEADS, HEAD_DIM)
-    d_heads = jax.vmap(attend_back)(
-        heads_view[:, :, 0],
-        heads_view[:, :, 1],
-        heads_view[:, :, 2],
-        log_total,
-        d_context_low.reshape(seq_dev, length, HEADS, HEAD_DIM),
-    )
-    d_projected_low = d_heads.reshape(tokens, 3 * D).astype(jnp.bfloat16)
-    d_hidden = d_mid_in + multiply(d_projected_low, weight_in[: 3 * D])
-    joint_sums = jnp.sum(d_projected_low.astype(jnp.float32), axis=0)
+    d_projected_low = attend_back(projected, log_total, d_context_low, seq_dev)
+    d_hidden = d_mid_in + multiply_left(d_projected_low, weight_in[: 3 * D])
+    joint_sums = jnp.sum(d_projected_low.astype(jnp.float32), axis=1)
     grad_pieces = jnp.concatenate(
         [
             joint_sums[:D],
@@ -223,7 +277,7 @@
             d_down_low,
             d_lifted_low,
             middle_low,
-            d_projected_low.T,
+            d_projected_low,
             hidden_low,
             d_attended_low.T,
             context_low,
@@ -481,6 +535,24 @@
 
     chunks = [chunk(*p) for p in plan]
     keep = pltpu.make_async_copy(found.at[me], rows.at[me], own_sem.at[count])
+
+    def row_copy(slot, target, source):
+        return pltpu.make_async_remote_copy(
+            src_ref=found.at[target],
+            dst_ref=rows.at[source],
+            send_sem=row_send.at[slot],
+            recv_sem=row_recv.at[source],
+            device_id=by_rank(target),
+            device_id_type=MESH,
+        )
+
+    def plane_rank(slot):
+        return (z + slot // 8) % 4 * 8 + (me + slot) % 8
+
+    def send_row(slot, carry):
+        row_copy(slot, plane_rank(slot), me).start()
+        return carry
+
     for index in gather_steps(plan):
         if index >= 0:
             next(chunks[index], None)
@@ -488,11 +560,17 @@
         task = -index - 1
         if task == 0:
             exchange_wait(message, answer, ask_send, ask_recv, n)
-        look_up(task, answer, table, from_slot, found)
-        if task == 3:
+        look_up((z + task) % 4, answer, table, from_slot, found)
+        if task == 0:
             keep.start()
-            exchange_start(found, rows, row_send, row_recv, n)
-    exchange_wait(found, rows, row_send, row_recv, n)
+        lax.fori_loop(max(task * 8, 1), task * 8 + 8, send_row, 0)
+
+    def finish_row(slot, carry):
+        row_copy(slot, plane_rank(slot), me).wait_send()
+        row_copy(slot, me, (me + slot) % n).wait_recv()
+        return carry
+
+    lax.fori_loop(1, n, finish_row, 0)
     keep.wait()
     copies.drain()
     for i in range(count):

time: 649 us -> 600 us (0.924)
  matrix products: 135 us -> 74.5 us
  Pallas kernels: 380 us -> 422 us
  other arithmetic: 79.2 us -> 50.5 us
    pallas_call x0 -> x3, Pallas kernels: none -> 46.6 us  [the longest x1 19.1 us: attend_back(): pl.pallas_call(attend_back_kernel, name='attend_back', grid=grid, in_spec...]
    dot_general x6 -> x0, matrix products: 38.4 us -> none  [the longest x1 11.3 us: attend_back(): jnp.einsum('qhe,khe->hqk', d_context, values, preferred_element_type=jnp....]
    dot_general x5 -> x4, matrix products: 54 us -> 21.8 us  [multiply_right(): lax.dot_general(left_side, right_side, (((1,), (1,)), ((), ())), preferre...]
    dot_general x5 -> x6, matrix products: 22.6 us -> 36.3 us  [multiply_left(): lax.dot_general(left_side, right_side, (((0,), (0,)), ((), ())), preferre...]
    convert_element_type x1 -> x0, other arithmetic: 11.8 us -> none  [attend_back(): d_scores_low = d_scores.astype(jnp.bfloat16)]
    reduce_sum x2 -> x1, other arithmetic: 10.7 us -> 0.5 us  [layer_backward(): joint_sums = jnp.sum(d_projected_low.astype(jnp.float32), axis=1)]
    convert_element_type x3 -> x0, local copies, waits for them, and re-layouts: 6.57 us -> none  [the longest x1 4.7 us: layer_forward(): (multiply_right(hidden_low, weight_in[:3 * D]) + joint_bias).astype(jnp.b...]
    unnamed x168 -> x144, local copies, waits for them, and re-layouts: 8.33 us -> 13.6 us
where the time goes in v3:
time: 600 us; the launch traced here: 591 us
  Pallas kernels  422 us (70%)
  matrix products  74.5 us (12%)
  other arithmetic  50.5 us (8%)
  local copies, waits for them, and re-layouts  37.8 us (6%)
  between operations  6.35 us (1%)
    pallas_call x1, Pallas kernels, gather_weights(): pl.pallas_call(functools.partial(gather_kernel, plan, count), name='gathe...  184 us
    pallas_call x1, Pallas kernels, scatter_grads(): pl.pallas_call(functools.partial(scatter_kernel, groups, len(pairs)), nam...  176 us
    dot_general x6, matrix products, multiply_left(): lax.dot_general(left_side, right_side, (((0,), (0,)), ((), ())), preferre...  36.3 us
    dot_general x4, matrix products, multiply_right(): lax.dot_general(left_side, right_side, (((1,), (1,)), ((), ())), preferre...  21.8 us
    pallas_call x1, Pallas kernels, attend_back(): pl.pallas_call(attend_back_kernel, name='attend_back', grid=grid, in_spec...  19.1 us
    dot_general x4, matrix products, multiply(): return jnp.dot(left_side, right_side, preferred_element_type=jnp.float32)  16.4 us
    pallas_call x1, Pallas kernels, sum_over_devices(): pl.pallas_call(sum_kernel, name='sum_over_devices', out_shape=jax.ShapeDt...  16 us
    pallas_call x1, Pallas kernels, lift(): pl.pallas_call(lift_kernel, name='lift', grid=(FF // rows,), in_specs=[pl...  14.1 us

profile of v3, /device:TPU:0, one launch (start us, length us, event | category | flops | bytes accessed | tf_op | source)
XLA Modules:
  0.0 591.1 jit_solution(8809350571083255041)
XLA Ops:
  10.4 3.7 convert_element_type.187.refs_6_
  14.1 183.8 %gather_weights.1 = (bf16[4,2,2,2,64,1024]{5,4,3,2,1,0:T(8,128)(2,1)}, bf16[4,2,2,2,256,1024]{5,4,3,2,1,0:T(8,128)(2,1)}, bf16[4,2,2,2,128,1024]{5,4,3,2,1,0:T(8...) custom-call(bf16[64,1024]{1,0:T(8,128)(2,1)} %fusion.44.refs_0_, ...), custom_call_target="tpu_custom_call" | custom-call | tf_op jit(solution)/shard_map/gather_weights/pallas_call | solution.py:604
  201.0 2.5 slice.274
  207.0 7.6 %add_convert_fusion.q_ref.k_ref.v_ref = bf16[512,3072]{1,0:T(8,128)(2,1)} fusion(bf16[512,1024]{1,0:T(8,128)(2,1)S(1)} %fusion.32.refs_5_, bf16[8192,1024]{1,0:T(8,128)(2,1)} %bitcast.231, f32[3072]{0:T(1024)S(1)} %pad_maximum_fusion.3), kind=kOutput, calls=%fused_computation.3 | convolution fusion | flops 3224371200 | bytes 10498048 | tf_op jit(solution)/shard_map/dot_general | solution.py:63
  214.6 13.3 %attend.1 = (bf16[512,1024]{1,0:T(8,128)(2,1)}, f32[16,1,512]{2,1,0:T(1,128)}) custom-call(bf16[512,3072]{1,0:T(8,128)(2,1)} %add_convert_fusion.q_ref.k_ref.v_ref, bf16[512,3072]{1,0:T(8,128)(2,1)} %add_convert_fusion.q_ref.k_ref.v_ref, bf16[512,3072]{1,0:T(8,128)(2,1)} %add_convert_fusion.q_ref.k_ref.v_ref), custom_call_target="tpu_custom_call" | custom-call | tf_op jit(solution)/shard_map/attend/pallas_call | solution.py:151
  227.9 3.4 fusion.109
  234.1 14.1 %lift.1 = (bf16[4096,512]{1,0:T(8,128)(2,1)}, f32[4096,512]{1,0:T(8,128)}) custom-call(bf16[8192,1024]{1,0:T(8,128)(2,1)} %bitcast.233, f32[4096,1]{1,0:T(8,128)} %bitcast.239, bf16[512,1024]{1,0:T(8,128)(2,1)} %fusion.33.middle_ref.refs_3_), custom_call_target="tpu_custom_call" | custom-call | tf_op jit(solution)/shard_map/lift/pallas_call | solution.py:189
  248.2 10.1 %fusion.110 = (f32[512]{0:T(512)S(1)}, f32[512,1024]{1,0:T(8,128)S(1)}) fusion(f32[1024]{0:T(1024)S(1)} %bitcast.313, bf16[4096,512]{1,0:T(8,128)(2,1)} %get-tuple-element.41, bf16[4096,1024]{1,0:T(8,128)(2,1)} %bitcast.320, f32[1024]{0:T(1024)S(1)} %bitcast.284, f32[1024]{0:T(1024)S(1)} %bitcast.270, f32[512]{0:T(512)S(1)} %fusion.71, ...), kind=kOutput, calls=%fused_computation.290 | convolution fusion | flops 4298636800 | bytes 16795648 | tf_op jit(solution)/shard_map/dot_general | solution.py:57
  258.7 7.5 %multiply_convert_fusion.1 = (bf16[512,1024]{1,0:T(8,128)(2,1)}, f32[512,1024]{1,0:T(8,128)}, f32[512,1024]{1,0:T(8,128)}) fusion(f32[1024]{0:T(1024)S(1)} %bitcast.302, bf16[1536,1024]{1,0:T(8,128)(2,1)S(1)} %bitcast.242, f32[512,1024]{1,0:T(8,128)S(1)} %get-tuple-element.271, f32[1024]{0:T(1024)S(1)} %bitcast.310, f32[1024]{0:T(1024)S(1)} %bitcast.298, ...), kind=kOutput, calls=%fused_computation.43 | convolution fusion | flops 1110966272 | bytes 9453568 | tf_op jit(solution)/shard_map/dot_general | solution.py:53
  271.4 4.0 convert_reduce_fusion.2
  279.6 9.0 %convert_reduce_fusion = (f32[4096]{0:T(1024)S(1)}, bf16[4096,512]{1,0:T(8,128)(2,1)}) fusion(f32[4096,512]{1,0:T(8,128)} %get-tuple-element.44, bf16[4096,1024]{1,0:T(8,128)(2,1)S(1)} %bitcast.323, bf16[512,1024]{1,0:T(8,128)(2,1)S(1)} %get-tuple-element.208.refs_1_), kind=kOutput, calls=%fused_computation | convolution fusion | flops 4303351808 | bytes 22036480 | tf_op jit(solution)/shard_map/dot_general | solution.py:63
  288.7 8.1 %slice.245 = bf16[2,2,2,2,256,1024]{5,4,3,2,1,0:T(8,128)(2,1)} slice(bf16[4,2,2,2,256,1024]{5,4,3,2,1,0:T(8,128)(2,1)} %get-tuple-element.36), slice={[2:4], [0:2], [0:2], [0:2], [0:256], [0:1024]} | slice | bytes 16777216 | tf_op jit(solution)/shard_map/slice | solution.py:253
  296.8 10.3 %multiply_reduce_fusion.4 = (f32[1024]{0:T(1024)S(1)}, f32[512]{0:T(512)S(1)}, f32[1024]{0:T(1024)S(1)}, f32[512,1024]{1,0:T(8,128)S(1)}) fusion(f32[512,1024]{1,0:T(8,128)S(1)} %copy-done.2, f32[512]{0:T(512)S(1)} %fusion.71, f32[512]{0:T(512)S(1)} %broadcast_multiply_fusion.2, f32[1024]{0:T(1024)S(1)} %bitcast.271, ...), kind=kOutput, calls=%fused_computation.37 | convolution fusion | flops 4300207616 | bytes 18894848 | tf_op jit(solution)/shard_map/dot_general | solution.py:57
  308.1 4.7 fusion.36.d_ref
  312.8 19.1 %attend_back.1 = bf16[3,1024,512]{2,1,0:T(8,128)(2,1)} custom-call(bf16[512,3072]{1,0:T(8,128)(2,1)} %add_convert_fusion.q_ref.k_ref.v_ref, bf16[512,3072]{1,0:T(8,128)(2,1)} %add_convert_fusion.q_ref.k_ref.v_ref, bf16[512,3072]{1,0:T(8,128)(2,1)} %add_convert_fusion.q_ref.k_ref.v_ref, bf16[512,1024]{1,0:T(8,128)(2,1)} %fusion.36.d_ref, ...), custom_call_target="tpu_custom_call" | custom-call | tf_op jit(solution)/shard_map/attend_back/pallas_call | solution.py:168
  334.2 3.4 convolution_convert_fusion.1
  337.7 6.4 %multiply_reduce_fusion.2 = (f32[1024]{0:T(1024)S(1)}, f32[512]{0:T(512)S(1)}, f32[1024]{0:T(1024)S(1)}, f32[512,1024]{1,0:T(8,128)S(1)}) fusion(f32[512,1024]{1,0:T(8,128)S(1)} %get-tuple-element.267, f32[512]{0:T(512)S(1)} %fusion.70, f32[512]{0:T(512)S(1)} %broadcast_multiply_fusion.3, f32[1024]{0:T(1024)S(1)} %bitcast.267, ...), kind=kOutput, calls=%fused_computation.34 | convolution fusion | flops 3226465792 | bytes 15749120 | tf_op jit(solution)/shard_map/dot_general | solution.py:57
  347.0 2.6 convolution_convert_fusion
  351.0 175.6 %scatter_grads.1 = (f32[256,1024]{1,0:T(8,128)}, f32[128,1024]{1,0:T(8,128)}, f32[48,1024]{1,0:T(8,128)}, bf16[32,32,1024]{2,1,0:T(8,128)(2,1)}, f32[32,4,128]{2,1,0:T(4,128)}) custom-call(bf16[16,2,128,512]{3,2,1,0:T(8,128)(2,1)} %bitcast.246, bf16[512,1024]{1,0:T(8,128)(2,1)} %copy-done.16, bf16[8,2,256,512]{3,2,1,0:T(8,128)(2,1)} %bitcast.247, ...), custom_call_target="tpu_custom_call" | custom-call | tf_op jit(solution)/shard_map/scatter_grads/pallas_call | solution.py:870
  531.0 4.6 fusion.9
  541.9 16.0 %sum_over_devices.1 = f32[32,4,128]{2,1,0:T(4,128)} custom-call(f32[32,4,128]{2,1,0:T(4,128)} %bitcast.255), custom_call_target="tpu_custom_call" | custom-call | tf_op jit(solution)/shard_map/sum_over_devices/pallas_call | solution.py:943
  562.4 2.5 copy.89
  567.5 2.6 copy.90
  578.1 6.9 %fusion.90 = (bf16[960,1024]{1,0:T(8,128)(2,1)}, f32[960,1024]{1,0:T(8,128)}) fusion(f32[960,1024]{1,0:T(8,128)} %param.27, f32[]{:T(128)} %bitcast.69, f32[1024]{0:T(1024)S(1)} %get-tuple-element.186, f32[960]{0:T(1024)S(1)} %get-tuple-element.196, f32[960,1024,1]{1,0,2:T(8,128)} %copy-done.3, f32[]{:T(128)S(6)} %div.378), kind=kLoop, calls=%fused_computation.275 | loop fusion | flops 5898240 | bytes 13770504 | tf_op jit(solution)/shard_map/convert_element_type | solution.py:1274
  (272 shorter events, 62.7 us)
Async XLA Ops:
  248.2 10.5 %copy-start.11 = (bf16[32,48,1024]{2,1,0:T(8,128)(2,1)S(1)}, bf16[32,48,1024]{2,1,0:T(8,128)(2,1)}, u32[]{:S(2)}) copy-start(bf16[32,48,1024]{2,1,0:T(8,128)(2,1)} %copy-done.10) | copy-start | bytes 9437188
  258.3 7.9 %copy-start.5 = (f32[512,1024]{1,0:T(8,128)}, f32[512,1024]{1,0:T(8,128)S(1)}, u32[]{:S(2)}) copy-start(f32[512,1024]{1,0:T(8,128)S(1)} %get-tuple-element.271) | copy-start | bytes 6291460
  258.7 12.1 %copy-start.44 = (s32[1,512]{1,0:T(1,128)S(1)}, s32[1,512]{1,0:T(1,128)}, u32[]{:S(2)}) copy-start(s32[1,512]{1,0:T(1,128)} %param.22) | copy-start | bytes 6148
  271.4 8.2 %slice-start = ((s8[8388608]{0:T(1024)(128)(4,1)}), s8[4194304]{0:T(1024)(128)(4,1)S(1)}, s32[]{:S(2)}) async-start(s8[8388608]{0:T(1024)(128)(4,1)} %bitcast.321), calls=%async_computation | async-start | bytes 8388608
  279.6 9.1 %copy-start.16 = (bf16[512,1024]{1,0:T(8,128)(2,1)}, bf16[512,1024]{1,0:T(8,128)(2,1)S(1)}, u32[]{:S(2)}) copy-start(bf16[512,1024]{1,0:T(8,128)(2,1)S(1)} %get-tuple-element.208.refs_1_) | copy-start | bytes 3145732
  288.7 8.1 %copy-start.2 = (f32[512,1024]{1,0:T(8,128)S(1)}, f32[512,1024]{1,0:T(8,128)}, u32[]{:S(2)}) copy-start(f32[512,1024]{1,0:T(8,128)} %copy-done.1) | copy-start | bytes 6291460
  350.9 177.2 %copy-start.46 = (f32[1,256]{1,0:T(1,128)S(1)}, f32[1,256]{1,0:T(1,128)}, u32[]{:S(2)}) copy-start(f32[1,256]{1,0:T(1,128)} %param.31) | copy-start | bytes 3076
  528.1 36.8 %copy-start.33 = (f32[1,256]{1,0:T(1,128)}, f32[1,256]{1,0:T(1,128)S(1)}, u32[]{:S(2)}) copy-start(f32[1,256]{1,0:T(1,128)S(1)} %get-tuple-element.202) | copy-start | bytes 3076
  536.3 41.7 %copy-start.29 = (f32[960]{0:T(1024)}, f32[960]{0:T(1024)S(1)}, u32[]{:S(2)}) copy-start(f32[960]{0:T(1024)S(1)} %get-tuple-element.196) | copy-start | bytes 11524
  537.6 21.7 %copy-start.26 = (f32[1,3,1024]{2,0,1:T(1,128)S(1)}, f32[1,3,1024]{2,0,1:T(1,128)}, u32[]{:S(2)}) copy-start(f32[1,3,1024]{2,0,1:T(1,128)} %param.30) | copy-start | bytes 36868
  537.6 21.7 %copy-start.49 = (f32[3]{0:T(128)S(1)}, f32[3]{0:T(128)}, u32[]{:S(2)}) copy-start(f32[3]{0:T(128)} %constant.263.clone) | copy-start | bytes 40
  537.6 22.8 %copy-start.42 = (f32[3]{0:T(128)S(1)}, f32[3]{0:T(128)}, u32[]{:S(2)}) copy-start(f32[3]{0:T(128)} %constant.280) | copy-start | bytes 40
  537.6 23.2 %copy-start.48 = (f32[3]{0:T(128)S(1)}, f32[3]{0:T(128)}, u32[]{:S(2)}) copy-start(f32[3]{0:T(128)} %constant.287) | copy-start | bytes 40
  538.6 26.3 %copy-start.4 = (f32[256,1024]{1,0:T(8,128)S(1)}, f32[256,1024]{1,0:T(8,128)}, u32[]{:S(2)}) copy-start(f32[256,1024]{1,0:T(8,128)} %get-tuple-element.46) | copy-start | bytes 3145732
  538.6 50.4 %copy-start.39 = (f32[48]{0:T(128)}, f32[48]{0:T(128)S(1)}, u32[]{:S(2)}) copy-start(f32[48]{0:T(128)S(1)} %get-tuple-element.200) | copy-start | bytes 580
  539.1 50.9 %copy-start.38 = (f32[512]{0:T(512)}, f32[512]{0:T(512)S(1)}, u32[]{:S(2)}) copy-start(f32[512]{0:T(512)S(1)} %get-tuple-element.194) | copy-start | bytes 6148
  567.4 9.2 %copy-start.41 = (f32[1024]{0:T(1024)S(1)}, f32[1024]{0:T(1024)}, u32[]{:S(2)}) copy-start(f32[1024]{0:T(1024)} %param.35) | copy-start | bytes 12292
  577.2 7.7 %copy-start.31 = (f32[1024]{0:T(1024)}, f32[1024]{0:T(1024)S(1)}, u32[]{:S(2)}) copy-start(f32[1024]{0:T(1024)S(1)} %get-tuple-element.186) | copy-start | bytes 12292
  578.0 7.0 %copy-start.37 = (f32[2,1024]{1,0:T(2,128)S(1)}, f32[2,1024]{1,0:T(2,128)}, u32[]{:S(2)}) copy-start(f32[2,1024]{1,0:T(2,128)} %param.37) | copy-start | bytes 24580
  578.0 7.0 %copy-start.43 = (f32[2]{0:T(128)S(1)}, f32[2]{0:T(128)}, u32[]{:S(2)}) copy-start(f32[2]{0:T(128)} %constant.282) | copy-start | bytes 28
  578.0 7.2 %copy-start.51 = (f32[2]{0:T(128)S(1)}, f32[2]{0:T(128)}, u32[]{:S(2)}) copy-start(f32[2]{0:T(128)} %constant.288) | copy-start | bytes 28
  578.0 11.0 %copy-start.24 = (f32[48,1024]{1,0:T(8,128)S(1)}, f32[48,1024]{1,0:T(8,128)}, u32[]{:S(2)}) copy-start(f32[48,1024]{1,0:T(8,128)} %param.28) | copy-start | bytes 589828
  578.0 11.8 %copy-start.52 = (f32[13]{0:T(128)S(1)}, f32[13]{0:T(128)}, u32[]{:S(2)}) copy-start(f32[13]{0:T(128)} %constant.284) | copy-start | bytes 160
  578.1 12.0 %copy-start.36 = (f32[512]{0:T(512)S(1)}, f32[512]{0:T(512)}, u32[]{:S(2)}) copy-start(f32[512]{0:T(512)} %param.29) | copy-start | bytes 6148
  (31 other events, 100.4 us)

commit v4 on v3

--- a/solution.py
+++ b/solution.py
@@ -204,6 +204,42 @@
             jax.ShapeDtypeStruct((FF, tokens), jnp.float32),
         ),
     )(weight_in, bias_up[:, None], middle_low)
+
+
+def lift_back_kernel(down_ref, d_ref, slope_ref, up_ref, out_ref, total_ref, sums_ref):
+    d_lifted = (multiply_right(down_ref[...], d_ref[...]) * slope_ref[...]).astype(LOW)
+    out_ref[...] = d_lifted
+    sums_ref[...] = jnp.sum(d_lifted.astype(jnp.float32), axis=1, keepdims=True)
+    part = multiply_left(d_lifted, up_ref[...])
+
+    @pl.when(pl.program_id(0) == 0)
+    def _():
+        total_ref[...] = part
+
+    @pl.when(pl.program_id(0) > 0)
+    def _():
+        total_ref[...] += part
+
+
+def lift_back(weight_in, weight_down, slope, d_down_low):
+    tokens = d_down_low.shape[0]
+    rows = 512
+    block = pl.BlockSpec((rows, D), lambda i: (i, 0))
+    whole = pl.BlockSpec((tokens, D), lambda i: (0, 0))
+    hidden = pl.BlockSpec((rows, tokens), lambda i: (i, 0))
+    d_lifted, d_middle, sums = pl.pallas_call(
+        lift_back_kernel,
+        name="lift_back",
+        grid=(FF // rows,),
+        in_specs=[block, whole, hidden, pl.BlockSpec((rows, D), lambda i: (4 * D // rows + i, 0))],
+        out_specs=(hidden, whole, pl.BlockSpec((rows, 1), lambda i: (i, 0))),
+        out_shape=(
+            jax.ShapeDtypeStruct((FF, tokens), LOW),
+            jax.ShapeDtypeStruct((tokens, D), jnp.float32),
+            jax.ShapeDtypeStruct((FF, 1), jnp.float32),
+        ),
+    )(weight_down, d_down_low, slope, weight_in)
+    return d_lifted, d_middle, sums[:, 0]
 
 
 def layer_forward(hidden, weight_in, weight_down, pieces, seq_dev):
@@ -249,8 +285,8 @@
     ) = kept
     d_out_in, d_gain_b, d_shift_b = norm_back(out_in, gain_b, shift_b, grad_out)
     d_down_low = d_out_in.astype(jnp.bfloat16)
-    d_lifted_low = (multiply_right(weight_down, d_down_low) * slope).astype(jnp.bfloat16)
-    d_middle = d_out_in + multiply_left(d_lifted_low, weight_in[4 * D :])
+    d_lifted_low, d_from_up, d_bias_up = lift_back(weight_in, weight_down, slope, d_down_low)
+    d_middle = d_out_in + d_from_up
     d_mid_in, d_gain_a, d_shift_a = norm_back(mid_in, gain_a, shift_a, d_middle)
     d_attended_low = d_mid_in.astype(jnp.bfloat16)
     d_context_low = multiply(d_attended_low, weight_in[3 * D : 4 * D]).astype(jnp.bfloat16)
@@ -264,7 +300,7 @@
             jnp.sum(d_attended_low.astype(jnp.float32), axis=0),
             d_gain_a,
             d_shift_a,
-            jnp.sum(d_lifted_low.astype(jnp.float32), axis=1),
+            d_bias_up,
             jnp.sum(d_down_low.astype(jnp.float32), axis=0),
             d_gain_b,
             d_shift_b,
@@ -1017,7 +1053,7 @@
         grad_in, grad_down, grad_side, arrived, pieces = scatter_grads(
             pairs, side.reshape(4, 2, 2, 2, -1, D), buckets, vector.reshape(n, -1, 128)
         )
-        return grad_side, grad_in, grad_down, arrived, jnp.sum(pieces, axis=0).reshape(-1)
+        return grad_side, grad_in, grad_down, arrived, pieces
     down, up, joint, attended = [
         multiply(pairs[2 * i], pairs[2 * i + 1]) for i in range(4)
     ]
@@ -1044,99 +1080,463 @@
     return jnp.maximum(1.0, jnp.sqrt(mean_square))
 
 
-def local(
-    token_ids,
-    labels,
-    loss_mask,
-    batch_of,
-    layer_in,
-    layer_down,
-    word_table,
-    side_mat,
-    vectors,
+DOWN, WORD, POS, HEAD, INNER, EXTRA = 0, 1, 2, 3, 4, 14
+LOSS_LANE, TOTAL_LANE = 13, 16
+
+
+def row_stats(gradient, rows_old):
+    square = gradient * gradient
+    floored = square + tiny_square
+    rows_new = decay_rate * rows_old + (1.0 - decay_rate) * jnp.mean(
+        floored, axis=1, keepdims=True
+    )
+    return rows_new, floored, square / rows_new
+
+
+def down_rows_sum(value):
+    return jnp.sum(value, axis=0, keepdims=True)
+
+
+def lanes(width=D):
+    return lax.broadcasted_iota(jnp.int32, (1, width), 1)
+
+
+def upright(row, count, start=0):
+    shape = (count, row.shape[1])
+    at = start + lax.broadcasted_iota(jnp.int32, shape, 0)
+    there = lax.broadcasted_iota(jnp.int32, shape, 1) == at
+    return jnp.sum(jnp.where(there, row, 0.0), axis=1, keepdims=True)
+
+
+def flat(column, width, start=0):
+    shape = (column.shape[0], width)
+    at = start + lax.broadcasted_iota(jnp.int32, shape, 0)
+    there = lax.broadcasted_iota(jnp.int32, shape, 1) == at
+    return jnp.sum(jnp.where(there, column, 0.0), axis=0, keepdims=True)
+
+
+def inner_part(rank):
+    return jnp.where(rank < 12, 0, jnp.where(rank < 16, 1, 2))
+
+
+def own_segment(rank):
+    start = rank * 512
+    bounds = piece_bounds()[1:]
+    inner = sum((jnp.where(start >= bound, 1, 0) for bound in bounds))
+    tail = sum((jnp.where(start >= bounds[-1] + D * k, 1, 0) for k in (1, 2, 3)))
+    return inner + tail
+
+
+def position_rows(rank, count):
+    rows = rank * count + lax.broadcasted_iota(jnp.int32, (count, 1), 0)
+    return rows < SEQ_LEN
+
+
+def stats_kernel(
+    g_in,
+    g_down,
+    g_side,
+    pieces,
+    word,
+    in_old,
+    down_old,
+    side_old,
+    word_old,
+    moment_old,
+    loss,
+    in_new,
+    down_new,
+    side_new,
+    word_new,
+    moment_new,
+    update,
+    payload,
+    held,
+):
+    rank = my_rank()
+    step = pl.program_id(0)
+
+    @pl.when(step == 0)
+    def _():
+        lane = lanes()
+        payload[...] = jnp.zeros_like(payload)
+        held[...] = jnp.zeros_like(held)
+        word_new[...] = jnp.zeros_like(word_new)
+        rows, floored, weighted = row_stats(g_in[...], upright(in_old[...], g_in.shape[0]))
+        in_new[...] = flat(rows, in_new.shape[1])
+        total, total_weighted = down_rows_sum(floored), down_rows_sum(weighted)
+        which = inner_part(rank)
+        for k in range(3):
+            mine = jnp.where(which == k, 1.0, 0.0)
+            payload[8 + k : 9 + k] = total * mine
+            payload[11 + k : 12 + k] = total_weighted * mine
+        rows, floored, weighted = row_stats(g_down[...], upright(down_old[...], g_down.shape[0]))
+        down_new[...] = flat(rows, down_new.shape[1])
+        payload[0:1] = down_rows_sum(floored)
+        payload[1:2] = down_rows_sum(weighted)
+        extra = jnp.where(lane == TOTAL_LANE + DOWN, down_rows_sum(rows), 0.0)
+        rows, floored, weighted = row_stats(g_side[...], upright(side_old[...], g_side.shape[0]))
+        side_new[...] = flat(rows, side_new.shape[1])
+        first = position_rows(rank, g_side.shape[0])
+        for k, pick in ((0, first), (1, jnp.logical_not(first))):
+            payload[4 + k : 5 + k] = down_rows_sum(jnp.where(pick, floored, 0.0))
+            payload[6 + k : 7 + k] = down_rows_sum(jnp.where(pick, weighted, 0.0))
+            part = down_rows_sum(jnp.where(pick, rows, 0.0))
+            extra = jnp.where(lane == TOTAL_LANE + POS + k, part, extra)
+        gradient = pieces[0]
+        for k in range(1, pieces.shape[0]):
+            gradient = gradient + pieces[k]
+        moment = decay_rate * moment_old[...] + (1.0 - decay_rate) * (
+            gradient * gradient + tiny_square
+        )
+        change = gradient * lax.rsqrt(moment)
+        moment_new[...] = moment
+        update[...] = change
+        squares = jnp.sum(down_rows_sum(change * change), axis=1, keepdims=True)
+        extra = jnp.where(lane == own_segment(rank), squares, extra)
+        payload[EXTRA : EXTRA + 1] = jnp.where(lane == LOSS_LANE, loss[...], extra)
+
+    start = step * word.shape[0]
+    rows, floored, weighted = row_stats(
+        word[...], upright(word_old[...], word.shape[0], start)
+    )
+    word_new[...] += flat(rows, word_new.shape[1], start)
+    held[0:1] += down_rows_sum(floored)
+    held[1:2] += down_rows_sum(weighted)
+    held[2:3] += jnp.broadcast_to(down_rows_sum(rows), (1, D))
+
+    @pl.when(step == pl.num_programs(0) - 1)
+    def _():
+        payload[2:3] = held[0:1]
+        payload[3:4] = held[1:2]
+        extra = payload[EXTRA : EXTRA + 1]
+        payload[EXTRA : EXTRA + 1] = jnp.where(
+            lanes() == TOTAL_LANE + WORD, held[2:3], extra
+        )
+
+
+def lane_of(row, lane):
+    return jnp.sum(jnp.where(lanes() == lane, row, 0.0), axis=1, keepdims=True)
+
+
+def clip_scale(weighted, cols_new, mean_rows, size):
+    mean_square = jnp.sum(weighted / cols_new, axis=1, keepdims=True) * mean_rows / size
+    return learn_rate / jnp.maximum(1.0, jnp.sqrt(mean_square))
+
+
+def step_of(gradient, rows_new, cols_new, mean_rows, rate):
+    return rate * gradient * lax.rsqrt(rows_new * cols_new / mean_rows)
+
+
+def update_kernel(
+    summed,
+    w_in,
+    w_down,
+    w_side,
+    w_vec,
+    w_word,
+    g_in,
+    g_down,
+    g_side,
+    change,
+    g_word,
     in_rows,
-    in_cols,
-    down_rows,
     down_cols,
-    word_rows,
     word_cols,
-    side_rows,
     side_cols,
-    vec_moment,
+    in_cols_new,
+    down_rows_new,
+    side_rows_new,
+    word_rows_new,
+    new_in,
+    in_copy,
+    new_down,
+    down_copy,
+    new_side,
+    side_copy,
+    new_vec,
+    vec_copy,
+    new_word,
+    word_copy,
+    in_rows_new,
+    down_cols_new,
+    word_cols_new,
+    side_cols_new,
+    loss,
 ):
-    seq_dev, length = token_ids.shape
-    tokens = seq_dev * length
-    n_blocks = lax.axis_size(BOTH)
+    rank = my_rank()
+    half = 1.0 - decay_rate
+    extra = summed[EXTRA : EXTRA + 1]
+
+    def total(lane):
+        return lane_of(extra, TOTAL_LANE + lane)
+
+    word_factor = decay_rate * word_cols[...] + half * summed[2:3] / VOCAB
+    word_mean = total(WORD) / VOCAB
+    word_rate = clip_scale(summed[3:4], word_factor, word_mean, VOCAB * D)
+
+    @pl.when(pl.program_id(0) == 0)
+    def _():
+        word_cols_new[...] = word_factor
+        loss[...] = lane_of(extra, LOSS_LANE)
+        which = inner_part(rank)
+        factor = jnp.zeros((1, D), jnp.float32)
+        mean = jnp.zeros((1, 1), jnp.float32)
+        rate = jnp.zeros((1, 1), jnp.float32)
+        for k, width in enumerate((3 * D, D, FF)):
+            mine = which == k
+            rows = decay_rate * in_rows[k : k + 1] + half * summed[8 + k : 9 + k] / width
+            in_rows_new[k : k + 1] = rows
+            center = jnp.mean(rows, axis=1, keepdims=True)
+            speed = clip_scale(summed[11 + k : 12 + k], rows, center, D * width)
+            factor = jnp.where(mine, rows, factor)
+            mean = jnp.where(mine, center, mean)
+            rate = jnp.where(mine, speed, rate)
+        change_in = step_of(g_in[...], upright(in_cols_new[...], g_in.shape[0]), factor, mean, rate)
+        fresh = w_in[...] - change_in.T
+        new_in[...] = fresh
+        in_copy[...] = fresh.astype(LOW)
+        factor = decay_rate * down_cols[...] + half * summed[0:1] / FF
+        down_cols_new[...] = factor
+        mean = total(DOWN) / FF
+        rate = clip_scale(summed[1:2], factor, mean, FF * D)
+        rows = upright(down_rows_new[...], g_down.shape[0])
+        fresh = w_down[...] - step_of(g_down[...], rows, factor, mean, rate)
+        new_down[...] = fresh
+        down_copy[...] = fresh.astype(LOW)
+        steps = []
+        rows = upright(side_rows_new[...], g_side.shape[0])
+        for k, count in ((0, SEQ_LEN), (1, D)):
+            factor = decay_rate * side_cols[k : k + 1] + half * summed[4 + k : 5 + k] / count
+            side_cols_new[k : k + 1] = factor
+            mean = total(POS + k) / count
+            rate = clip_scale(summed[6 + k : 7 + k], factor, mean, count * D)
+            steps.append(step_of(g_side[...], rows, factor, mean, rate))
+        first = position_rows(rank, g_side.shape[0])
+        fresh = w_side[...] - jnp.where(first, steps[0], steps[1])
+        new_side[...] = fresh
+        side_copy[...] = fresh.astype(LOW)
+        segment = own_segment(rank)
+        size = jnp.where(segment == 5, float(FF), float(D))
+        clip = jnp.maximum(1.0, jnp.sqrt(lane_of(extra, segment) / size))
+        fresh = w_vec[...] - learn_rate * change[...] / clip
+        new_vec[...] = fresh
+        vec_copy[...] = fresh.astype(LOW)
+
+    count = g_word.shape[0]
+    rows = upright(word_rows_new[...], count, pl.program_id(0) * count)
+    fresh = w_word[...] - step_of(g_word[...], rows, word_factor, word_mean, word_rate)
+    new_word[...] = fresh
+    word_copy[...] = fresh.astype(LOW)
+
+
+def adapt_fused(given, grads, local_loss):
+    (
+        layer_in,
+        layer_down,
+        word_table,
+        side_mat,
+        vectors,
+        in_rows,
+        in_cols,
+        down_rows,
+        down_cols,
+        word_rows,
+        word_cols,
+        side_rows,
+        side_cols,
+        vec_moment,
+    ) = given
+    g_in, g_down, g_word, g_side, pieces = grads
+    shape = jax.ShapeDtypeStruct
+    single = jnp.float32
+    words = word_table.shape[0]
+    tile = words // 4
+
+    def whole(*dims):
+        return pl.BlockSpec(dims, lambda i: (0,) * len(dims))
+
+    def tiled(width):
+        return pl.BlockSpec((tile, width), lambda i: (i, 0))
+
+    h_in, h_down, h_side = g_in.shape[0], g_down.shape[0], g_side.shape[0]
+    vec_shape = pieces.shape[1:]
+    in_new, down_new, side_new, word_new, moment_new, change, payload = pl.pallas_call(
+        stats_kernel,
+        name="stats",
+        grid=(4,),
+        in_specs=[
+            whole(h_in, D),
+            whole(h_down, D),
+            whole(h_side, D),
+            whole(*pieces.shape),
+            tiled(D),
+            whole(1, h_in),
+            whole(1, h_down),
+            whole(1, h_side),
+            whole(1, words),
+            whole(*vec_shape),
+            whole(1, 1),
+        ],
+        out_specs=(
+            whole(1, h_in),
+            whole(1, h_down),
+            whole(1, h_side),
+            whole(1, words),
+            whole(*vec_shape),
+            whole(*vec_shape),
+            whole(16, D),
+        ),
+        out_shape=(
+            shape((1, h_in), single),
+            shape((1, h_down), single),
+            shape((1, h_side), single),
+            shape((1, words), single),
+            shape(vec_shape, single),
+            shape(vec_shape, single),
+            shape((16, D), single),
+        ),
+        scratch_shapes=[pltpu.VMEM((3, D), single)],
+    )(
+        g_in,
+        g_down,
+        g_side,
+        pieces,
+        g_word,
+        in_cols.reshape(1, -1),
+        down_rows.reshape(1, -1),
+        side_rows.reshape(1, -1),
+        word_rows.reshape(1, -1),
+        vec_moment.reshape(vec_shape),
+        local_loss.reshape(1, 1),
+    )
+    summed = sum_over_devices(payload.reshape(-1)).reshape(16, D)
+    outs = [
+        (whole(D, h_in), shape((D, h_in), single)),
+        (whole(D, h_in), shape((D, h_in), LOW)),
+        (whole(h_down, D), shape((h_down, D), single)),
+        (whole(h_down, D), shape((h_down, D), LOW)),
+        (whole(h_side, D), shape((h_side, D), single)),
+        (whole(h_side, D), shape((h_side, D), LOW)),
+        (whole(*vec_shape), shape(vec_shape, single)),
+        (whole(*vec_shape), shape(vec_shape, LOW)),
+        (tiled(D), shape((words, D), single)),
+        (tiled(D), shape((words, D), LOW)),
+        (whole(3, D), shape((3, D), single)),
+        (whole(1, D), shape((1, D), single)),
+        (whole(1, D), shape((1, D), single)),
+        (whole(2, D), shape((2, D), single)),
+        (whole(1, 1), shape((1, 1), single)),
+    ]
+    (
+        new_in,
+        in_copy,
+        new_down,
+        down_copy,
+        new_side,
+        side_copy,
+        new_vec,
+        vec_copy,
+        new_word,
+        word_copy,
+        in_rows_new,
+        down_cols_new,
+        word_cols_new,
+        side_cols_new,
+        loss,
+    ) = pl.pallas_call(
+        update_kernel,
+        name="update",
+        grid=(4,),
+        in_specs=[
+            whole(16, D),
+            whole(D, h_in),
+            whole(h_down, D),
+            whole(h_side, D),
+            whole(*vec_shape),
+            tiled(D),
+            whole(h_in, D),
+            whole(h_down, D),
+            whole(h_side, D),
+            whole(*vec_shape),
+            tiled(D),
+            whole(3, D),
+            whole(1, D),
+            whole(1, D),
+            whole(2, D),
+            whole(1, h_in),
+            whole(1, h_down),
+            whole(1, h_side),
+            whole(1, words),
+        ],
+        out_specs=tuple(spec for spec, _ in outs),
+        out_shape=tuple(kind for _, kind in outs),
+    )(
+        summed,
+        layer_in[0],
+        layer_down[0],
+        side_mat,
+        vectors.reshape(vec_shape),
+        word_table,
+        g_in,
+        g_down,
+        g_side,
+        change,
+        g_word,
+        in_rows[0],
+        down_cols,
+        word_cols.reshape(1, D),
+        side_cols,
+        in_new,
+        down_new,
+        side_new,
+        word_new,
+    )
+    return (
+        loss[0, 0],
+        new_in[None],
+        in_rows_new[None],
+        in_new.reshape(1, -1),
+        in_copy[None],
+        new_down[None],
+        down_new.reshape(1, -1),
+        down_cols_new,
+        down_copy[None],
+        new_word,
+        word_new.reshape(-1),
+        word_cols_new.reshape(-1),
+        word_copy,
+        new_side,
+        side_new.reshape(-1),
+        side_cols_new,
+        side_copy,
+        new_vec.reshape(-1),
+        moment_new.reshape(-1),
+        vec_copy.reshape(-1),
+    )
+
+
+def adapt(given, grads, local_loss):
+    (
+        layer_in,
+        layer_down,
+        word_table,
+        side_mat,
+        vectors,
+        in_rows,
+        in_cols,
+        down_rows,
+        down_cols,
+        word_rows,
+        word_cols,
+        side_rows,
+        side_cols,
+        vec_moment,
+    ) = given
+    grad_in_t, grad_down, grad_word, grad_side, grad_vec = grads
     my_index = lax.axis_index(BOTH)
-    mask_float = loss_mask.astype(jnp.float32)
-    member = batch_of[:, None] == jnp.arange(MICRO)[None, :]
-    local_counts = jnp.sum(member * jnp.sum(loss_mask, axis=1)[:, None], axis=0)
-    block_rows = word_table.shape[0]
-    capacity = max(2, 2 * tokens // n_blocks)
-    flat_ids = token_ids.reshape(tokens)
-    blocks = flat_ids // block_rows
-    label_float = labels.astype(jnp.float32).reshape(tokens)
-
     side_rows_local = side_mat.shape[0]
     vec_local = vectors.shape[0]
-    vector_row = jnp.pad(vectors.astype(LOW).reshape(1, -1), ((0, 15), (0, D - vec_local)))
-    (side_all, weight_in, weight_down), returned, to_slot, from_slot, counts = gather_blocks(
-        [
-            jnp.concatenate([side_mat.astype(LOW), vector_row], axis=0),
-            layer_in[0].astype(LOW).T,
-            layer_down[0].astype(LOW),
-        ],
-        blocks,
-        flat_ids - blocks * block_rows,
-        local_counts.astype(jnp.int32),
-        word_table.astype(LOW),
-        capacity,
-    )
-    seq_count = jnp.sum(member * counts[None, :], axis=1)
-    token_weight = (mask_float / (seq_count * MICRO)[:, None]).reshape(tokens)
-    side_all = side_all.reshape(n_blocks, side_rows_local + 16, D)
-    side_full = side_all[:, :side_rows_local].reshape(-1, D)
-    vector_full = side_all[:, side_rows_local, :vec_local].reshape(-1)
-    all_vectors = vector_full.astype(jnp.float32)
-    pos_rows = side_full[:SEQ_LEN].astype(jnp.float32)
-    head_mat = side_full[SEQ_LEN:]
-    global_offset = LAYERS * (8 * D + FF)
-    gain_emb = all_vectors[global_offset : global_offset + D]
-    shift_emb = all_vectors[global_offset + D : global_offset + 2 * D]
-    head_bias = all_vectors[global_offset + 2 * D : global_offset + 3 * D]
-    predictor = all_vectors[global_offset + 3 * D : global_offset + 4 * D]
-    predictor_low = vector_full[global_offset + 3 * D : global_offset + 4 * D]
-    own_rows = multiply_left(to_slot, returned.reshape(n_blocks * capacity, D))
-    embedded = (own_rows.reshape(seq_dev, length, D) + pos_rows[None, :, :]).reshape(tokens, D)
-    hidden = layer_norm(embedded, gain_emb, shift_emb)
-    pieces = layer_slices(all_vectors, 0)
-    hidden, kept = layer_forward(hidden, weight_in, weight_down, pieces, seq_dev)
-    final_low = hidden.astype(LOW)
-    head_pre = multiply(final_low, head_mat) + head_bias
-    head_act_low = exact_gelu(head_pre).astype(LOW)
-    logits = multiply(head_act_low, predictor_low)
-    local_loss = jnp.sum(token_weight * (jax.nn.softplus(logits) - label_float * logits))
-    d_logits = token_weight * (jax.nn.sigmoid(logits) - label_float)
-    d_predictor = jnp.sum(d_logits[:, None] * head_act_low.astype(jnp.float32), axis=0)
-    d_head_low = gelu_back(head_pre, d_logits[:, None] * predictor[None, :]).astype(LOW)
-    grad_head = multiply_left(final_low, d_head_low)
-    d_head_bias = jnp.sum(d_head_low.astype(jnp.float32), axis=0)
-    d_hidden = multiply_right(d_head_low, head_mat)
-    d_hidden, pairs, grad_pieces = layer_backward(
-        d_hidden, weight_in, weight_down, pieces, kept, seq_dev
-    )
-    d_embedded, d_gain_emb, d_shift_emb = norm_back(embedded, gain_emb, shift_emb, d_hidden)
-    grad_pos = jnp.sum(d_embedded.reshape(seq_dev, length, D), axis=0)
-    grad_vector = jnp.concatenate([grad_pieces, d_gain_emb, d_shift_emb, d_head_bias, d_predictor])
-    buckets = (
-        multiply(to_slot, d_embedded.astype(LOW))
-        .astype(LOW)
-        .reshape(n_blocks, capacity, D)
-    )
-    grad_side, grad_in_t, grad_down, arrived, grad_vec = reduce_blocks(
-        pairs, grad_pos, grad_head, buckets, grad_vector
-    )
-    grad_word = multiply_left(from_slot, arrived.reshape(n_blocks * capacity, D))
     grad_in = grad_in_t.T
 
     col_local = layer_in.shape[2]
@@ -1280,6 +1680,121 @@
         new_moment,
         new_vectors.astype(LOW),
     )
+
+
+def local(
+    token_ids,
+    labels,
+    loss_mask,
+    batch_of,
+    layer_in,
+    layer_down,
+    word_table,
+    side_mat,
+    vectors,
+    in_rows,
+    in_cols,
+    down_rows,
+    down_cols,
+    word_rows,
+    word_cols,
+    side_rows,
+    side_cols,
+    vec_moment,
+):
+    seq_dev, length = token_ids.shape
+    tokens = seq_dev * length
+    n_blocks = lax.axis_size(BOTH)
+    my_index = lax.axis_index(BOTH)
+    mask_float = loss_mask.astype(jnp.float32)
+    member = batch_of[:, None] == jnp.arange(MICRO)[None, :]
+    local_counts = jnp.sum(member * jnp.sum(loss_mask, axis=1)[:, None], axis=0)
+    block_rows = word_table.shape[0]
+    capacity = max(2, 2 * tokens // n_blocks)
+    flat_ids = token_ids.reshape(tokens)
+    blocks = flat_ids // block_rows
+    label_float = labels.astype(jnp.float32).reshape(tokens)
+
+    side_rows_local = side_mat.shape[0]
+    vec_local = vectors.shape[0]
+    vector_row = jnp.pad(vectors.astype(LOW).reshape(1, -1), ((0, 15), (0, D - vec_local)))
+    (side_all, weight_in, weight_down), returned, to_slot, from_slot, counts = gather_blocks(
+        [
+            jnp.concatenate([side_mat.astype(LOW), vector_row], axis=0),
+            layer_in[0].astype(LOW).T,
+            layer_down[0].astype(LOW),
+        ],
+        blocks,
+        flat_ids - blocks * block_rows,
+        local_counts.astype(jnp.int32),
+        word_table.astype(LOW),
+        capacity,
+    )
+    seq_count = jnp.sum(member * counts[None, :], axis=1)
+    token_weight = (mask_float / (seq_count * MICRO)[:, None]).reshape(tokens)
+    side_all = side_all.reshape(n_blocks, side_rows_local + 16, D)
+    side_full = side_all[:, :side_rows_local].reshape(-1, D)
+    vector_full = side_all[:, side_rows_local, :vec_local].reshape(-1)
+    all_vectors = vector_full.astype(jnp.float32)
+    pos_rows = side_full[:SEQ_LEN].astype(jnp.float32)
+    head_mat = side_full[SEQ_LEN:]
+    global_offset = LAYERS * (8 * D + FF)
+    gain_emb = all_vectors[global_offset : global_offset + D]
+    shift_emb = all_vectors[global_offset + D : global_offset + 2 * D]
+    head_bias = all_vectors[global_offset + 2 * D : global_offset + 3 * D]
+    predictor = all_vectors[global_offset + 3 * D : global_offset + 4 * D]
+    predictor_low = vector_full[global_offset + 3 * D : global_offset + 4 * D]
+    own_rows = multiply_left(to_slot, returned.reshape(n_blocks * capacity, D))
+    embedded = (own_rows.reshape(seq_dev, length, D) + pos_rows[None, :, :]).reshape(tokens, D)
+    hidden = layer_norm(embedded, gain_emb, shift_emb)
+    pieces = layer_slices(all_vectors, 0)
+    hidden, kept = layer_forward(hidden, weight_in, weight_down, pieces, seq_dev)
+    final_low = hidden.astype(LOW)
+    head_pre = multiply(final_low, head_mat) + head_bias
+    head_act_low = exact_gelu(head_pre).astype(LOW)
+    logits = multiply(head_act_low, predictor_low)
+    local_loss = jnp.sum(token_weight * (jax.nn.softplus(logits) - label_float * logits))
+    d_logits = token_weight * (jax.nn.sigmoid(logits) - label_float)
+    d_predictor = jnp.sum(d_logits[:, None] * head_act_low.astype(jnp.float32), axis=0)
+    d_head_low = gelu_back(head_pre, d_logits[:, None] * predictor[None, :]).astype(LOW)
+    grad_head = multiply_left(final_low, d_head_low)
+    d_head_bias = jnp.sum(d_head_low.astype(jnp.float32), axis=0)
+    d_hidden = multiply_right(d_head_low, head_mat)
+    d_hidden, pairs, grad_pieces = layer_backward(
+        d_hidden, weight_in, weight_down, pieces, kept, seq_dev
+    )
+    d_embedded, d_gain_emb, d_shift_emb = norm_back(embedded, gain_emb, shift_emb, d_hidden)
+    grad_pos = jnp.sum(d_embedded.reshape(seq_dev, length, D), axis=0)
+    grad_vector = jnp.concatenate([grad_pieces, d_gain_emb, d_shift_emb, d_head_bias, d_predictor])
+    buckets = (
+        multiply(to_slot, d_embedded.astype(LOW))
+        .astype(LOW)
+        .reshape(n_blocks, capacity, D)
+    )
+    grad_side, grad_in_t, grad_down, arrived, grad_vec = reduce_blocks(
+        pairs, grad_pos, grad_head, buckets, grad_vector
+    )
+    grad_word = multiply_left(from_slot, arrived.reshape(n_blocks * capacity, D))
+    given = (
+        layer_in,
+        layer_down,
+        word_table,
+        side_mat,
+        vectors,
+        in_rows,
+        in_cols,
+        down_rows,
+        down_cols,
+        word_rows,
+        word_cols,
+        side_rows,
+        side_cols,
+        vec_moment,
+    )
+    grads = (grad_in_t, grad_down, grad_word, grad_side, grad_vec)
+    if special():
+        return adapt_fused(given, grads, local_loss)
+    return adapt(given, grads, local_loss)
 
 
 def solution(mesh):

time: 600 us -> 577 us (0.962)
  Pallas kernels: 422 us -> 457 us
  matrix products: 74.5 us -> 54.5 us
  local copies, waits for them, and re-layouts: 37.8 us -> 18.8 us
  other arithmetic: 50.5 us -> 34.4 us
    pallas_call x0 -> x3, Pallas kernels: none -> 35.2 us  [the longest x1 19.1 us: lift_back(): pl.pallas_call(lift_back_kernel, name='lift_back', grid=(FF // rows,), in...]
    slice x6 -> x0, local copies, waits for them, and re-layouts: 10.7 us -> none  [the longest x1 8.1 us: layer_backward(): d_middle = d_out_in + multiply_left(d_lifted_low, weight_in[4 * D:])]
    dot_general x4 -> x3, matrix products: 21.8 us -> 13.2 us  [multiply_right(): lax.dot_general(left_side, right_side, (((1,), (1,)), ((), ())), preferre...]
    convert_element_type x5 -> x0, other arithmetic: 8.31 us -> none  [the longest x1 6.86 us: local(): new_word.astype(LOW)]
    dot_general x6 -> x5, matrix products: 36.3 us -> 28.9 us  [multiply_left(): lax.dot_general(left_side, right_side, (((0,), (0,)), ((), ())), preferre...]
    unnamed x144 -> x58, local copies, waits for them, and re-layouts: 13.6 us -> 7.65 us
where the time goes in v4:
time: 577 us; the launch traced here: 567 us
  Pallas kernels  457 us (79%)
  matrix products  54.5 us (9%)
  other arithmetic  34.4 us (6%)
  local copies, waits for them, and re-layouts  18.8 us (3%)
    pallas_call x1, Pallas kernels, gather_weights(): pl.pallas_call(functools.partial(gather_kernel, plan, count), name='gathe...  184 us
    pallas_call x1, Pallas kernels, scatter_grads(): pl.pallas_call(functools.partial(scatter_kernel, groups, len(pairs)), nam...  175 us
    dot_general x5, matrix products, multiply_left(): lax.dot_general(left_side, right_side, (((0,), (0,)), ((), ())), preferre...  28.9 us
    pallas_call x1, Pallas kernels, attend_back(): pl.pallas_call(attend_back_kernel, name='attend_back', grid=grid, in_spec...  19.3 us
    pallas_call x1, Pallas kernels, lift_back(): pl.pallas_call(lift_back_kernel, name='lift_back', grid=(FF // rows,), in...  19.1 us
    pallas_call x1, Pallas kernels, sum_over_devices(): pl.pallas_call(sum_kernel, name='sum_over_devices', out_shape=jax.ShapeDt...  16 us
    pallas_call x1, Pallas kernels, lift(): pl.pallas_call(lift_kernel, name='lift', grid=(FF // rows,), in_specs=[pl...  14.1 us
    dot_general x3, matrix products, multiply_right(): lax.dot_general(left_side, right_side, (((1,), (1,)), ((), ())), preferre...  13.2 us

profile of v4, /device:TPU:0, one launch (start us, length us, event | category | flops | bytes accessed | tf_op | source)
XLA Modules:
  0.0 567.4 jit_solution(10826426934213518563)
XLA Ops:
  14.1 3.7 convert_element_type.98.refs_6_
  17.8 183.9 %gather_weights.1 = (bf16[4,2,2,2,64,1024]{5,4,3,2,1,0:T(8,128)(2,1)}, bf16[4,2,2,2,256,1024]{5,4,3,2,1,0:T(8,128)(2,1)}, bf16[4,2,2,2,128,1024]{5,4,3,2,1,0:T(8...) custom-call(bf16[64,1024]{1,0:T(8,128)(2,1)} %fusion.37.refs_0_, ...), custom_call_target="tpu_custom_call" | custom-call | tf_op jit(solution)/shard_map/gather_weights/pallas_call | solution.py:640
  205.8 2.5 slice.158
  212.9 7.6 %add_convert_fusion.q_ref.k_ref.v_ref = bf16[512,3072]{1,0:T(8,128)(2,1)} fusion(bf16[512,1024]{1,0:T(8,128)(2,1)S(1)} %fusion.27.refs_5_, bf16[8192,1024]{1,0:T(8,128)(2,1)} %bitcast.137, f32[3072]{0:T(1024)S(1)} %pad_maximum_fusion.1), kind=kOutput, calls=%fused_computation.1 | convolution fusion | flops 3224371200 | bytes 10498048 | tf_op jit(solution)/shard_map/dot_general | solution.py:63
  220.5 13.2 %attend.1 = (bf16[512,1024]{1,0:T(8,128)(2,1)}, f32[16,1,512]{2,1,0:T(1,128)}) custom-call(bf16[512,3072]{1,0:T(8,128)(2,1)} %add_convert_fusion.q_ref.k_ref.v_ref, bf16[512,3072]{1,0:T(8,128)(2,1)} %add_convert_fusion.q_ref.k_ref.v_ref, bf16[512,3072]{1,0:T(8,128)(2,1)} %add_convert_fusion.q_ref.k_ref.v_ref), custom_call_target="tpu_custom_call" | custom-call | tf_op jit(solution)/shard_map/attend/pallas_call | solution.py:151
  233.7 3.5 fusion.57
  239.9 14.1 %lift.1 = (bf16[4096,512]{1,0:T(8,128)(2,1)}, f32[4096,512]{1,0:T(8,128)}) custom-call(bf16[8192,1024]{1,0:T(8,128)(2,1)} %bitcast.139, f32[4096,1]{1,0:T(8,128)} %bitcast.146, bf16[512,1024]{1,0:T(8,128)(2,1)} %fusion.28.middle_ref.refs_3_), custom_call_target="tpu_custom_call" | custom-call | tf_op jit(solution)/shard_map/lift/pallas_call | solution.py:189
  254.0 10.1 %fusion.58 = (f32[512]{0:T(512)S(1)}, f32[512,1024]{1,0:T(8,128)S(1)}) fusion(f32[1024]{0:T(1024)S(1)} %bitcast.200, bf16[4096,512]{1,0:T(8,128)(2,1)} %get-tuple-element.66, bf16[4096,1024]{1,0:T(8,128)(2,1)} %bitcast.147, f32[1024]{0:T(1024)S(1)} %bitcast.176, f32[1024]{0:T(1024)S(1)} %bitcast.167, f32[512]{0:T(512)S(1)} %fusion.46, ...), kind=kOutput, calls=%fused_computation.155 | convolution fusion | flops 4298636800 | bytes 16795648 | tf_op jit(solution)/shard_map/dot_general | solution.py:57
  264.4 5.6 multiply_convert_fusion
  272.5 2.2 multiply_reduce_fusion.2
  275.4 2.8 convolution_convert_fusion.1
  279.5 19.1 %lift_back.1 = (bf16[4096,512]{1,0:T(8,128)(2,1)}, f32[512,1024]{1,0:T(8,128)}, f32[4096,1]{1,0:T(8,128)}) custom-call(bf16[4096,1024]{1,0:T(8,128)(2,1)} %bitcast.148, bf16[512,1024]{1,0:T(8,128)(2,1)} %get-tuple-element.174.d_ref.refs_1_, f32[4096,512]{1,0:T(8,128)} %get-tuple-element.69.slope_ref, bf16[8192,1024]{1,0:T(8,128)(2,1)} %bitcast.140), custom_call_target="tpu_custom_call" | custom-call | tf_op jit(solution)/shard_map/lift_back/pallas_call | solution.py:230
  298.6 3.9 multiply_reduce_fusion.3
  304.5 2.2 reduce.6
  309.9 3.8 fusion.31.d_ref
  313.7 19.3 %attend_back.1 = bf16[3,1024,512]{2,1,0:T(8,128)(2,1)} custom-call(bf16[512,3072]{1,0:T(8,128)(2,1)} %add_convert_fusion.q_ref.k_ref.v_ref, bf16[512,3072]{1,0:T(8,128)(2,1)} %add_convert_fusion.q_ref.k_ref.v_ref, bf16[512,3072]{1,0:T(8,128)(2,1)} %add_convert_fusion.q_ref.k_ref.v_ref, bf16[512,1024]{1,0:T(8,128)(2,1)} %fusion.31.d_ref, ...), custom_call_target="tpu_custom_call" | custom-call | tf_op jit(solution)/shard_map/attend_back/pallas_call | solution.py:168
  333.0 8.3 %multiply_reduce_fusion.1 = (f32[1024]{0:T(1024)S(1)}, f32[512]{0:T(512)S(1)}, f32[1024]{0:T(1024)S(1)}, f32[512,1024]{1,0:T(8,128)S(1)}) fusion(f32[512,1024]{1,0:T(8,128)S(1)} %get-tuple-element.206, f32[512]{0:T(512)S(1)} %fusion.45, f32[512]{0:T(512)S(1)} %broadcast_multiply_fusion.2, f32[1024]{0:T(1024)S(1)} %bitcast.172, ...), kind=kOutput, calls=%fused_computation.23 | convolution fusion | flops 3226465792 | bytes 15749120 | tf_op jit(solution)/shard_map/dot_general | solution.py:57
  344.6 2.6 convolution_convert_fusion
  347.2 2.0 pad_maximum_fusion
  349.2 175.3 %scatter_grads.1 = (f32[256,1024]{1,0:T(8,128)}, f32[128,1024]{1,0:T(8,128)}, f32[48,1024]{1,0:T(8,128)}, bf16[32,32,1024]{2,1,0:T(8,128)(2,1)}, f32[32,4,128]{2,1,0:T(4,128)}) custom-call(bf16[16,2,128,512]{3,2,1,0:T(8,128)(2,1)} %bitcast.153, bf16[512,1024]{1,0:T(8,128)(2,1)} %get-tuple-element.174.d_ref.refs_1_, bf16[8,2,256,512]{3,2,1,0:T(8,128)(2,1)} %bitcast.154, ...), custom_call_target="tpu_custom_call" | custom-call | tf_op jit(solution)/shard_map/scatter_grads/pallas_call | solution.py:906
  524.5 6.3 %convolution_bitcast_fusion.word.g_word = f32[960,1024]{1,0:T(8,128)} fusion(bf16[32,32,960]{2,1,0:T(8,128)(2,1)} %get-tuple-element.78, bf16[32,32,1024]{2,1,0:T(8,128)(2,1)} %get-tuple-element.79), kind=kOutput, calls=%fused_computation.55 | convolution fusion | flops 2013265920 | bytes 7995392 | tf_op jit(solution)/shard_map/dot_general | solution.py:57
  530.8 6.7 %stats.1 = (f32[1,256]{1,0:T(1,128)}, f32[1,128]{1,0:T(1,128)}, f32[1,48]{1,0:T(1,128)}, f32[1,960]{1,0:T(1,128)}, f32[4,128]{1,0:T(4,128)}, /*index=5*/f32[4,128]{1,0:T(4,128)}, f32[16,1024]{1,0:T(8,128)}) custom-call(f32[256,1024]{1,0:T(8,128)} %get-tuple-element.74.g_in, f32[128,1024]{1,0:T(8,128)} %get-tuple-element.75.g_down, ...), custom_call_target="tpu_custom_call" | custom-call | tf_op jit(solution)/shard_map/stats/pallas_call | solution.py:1364
  539.0 16.0 %sum_over_devices.1 = f32[32,4,128]{2,1,0:T(4,128)} custom-call(f32[32,4,128]{2,1,0:T(4,128)} %reshape.435.values), custom_call_target="tpu_custom_call" | custom-call | tf_op jit(solution)/shard_map/sum_over_devices/pallas_call | solution.py:979
  556.5 9.3 %update.1 = (f32[1024,256]{1,0:T(8,128)}, bf16[1024,256]{1,0:T(8,128)(2,1)}, f32[128,1024]{1,0:T(8,128)}, bf16[128,1024]{1,0:T(8,128)(2,1)}, f32[48,1024]{1,0:T(...) custom-call(f32[16,1024]{1,0:T(8,128)} %reshape_reshape.11.summed, ...), custom_call_target="tpu_custom_call" | custom-call | tf_op jit(solution)/shard_map/update/pallas_call | solution.py:1447
  (117 shorter events, 40.5 us)
Async XLA Ops:
  0.7 12.4 %copy-start.6 = (f32[1,1024,256]{2,1,0:T(8,128)S(1)}, f32[1,1024,256]{2,1,0:T(8,128)}, u32[]{:S(2)}) copy-start(f32[1,1024,256]{2,1,0:T(8,128)} %param.22) | copy-start | bytes 3145732
  17.8 186.2 %copy-start.13 = (s32[1,512]{1,0:T(1,128)S(1)}, s32[1,512]{1,0:T(1,128)}, u32[]{:S(2)}) copy-start(s32[1,512]{1,0:T(1,128)} %param.20) | copy-start | bytes 6148
  205.8 2.6 copy-start.9
  205.8 2.8 copy-start.10
  208.3 1.6 copy-start.4
  211.0 9.6 %copy-start.7 = (bf16[512,1024]{1,0:T(8,128)(2,1)}, bf16[512,1024]{1,0:T(8,128)(2,1)S(1)}, u32[]{:S(2)}) copy-start(bf16[512,1024]{1,0:T(8,128)(2,1)S(1)} %fusion.27.refs_5_) | copy-start | bytes 3145732
  237.1 1.4 copy-start
  254.0 10.5 %copy-start.5 = (bf16[32,48,1024]{2,1,0:T(8,128)(2,1)S(1)}, bf16[32,48,1024]{2,1,0:T(8,128)(2,1)}, u32[]{:S(2)}) copy-start(bf16[32,48,1024]{2,1,0:T(8,128)(2,1)} %copy-done.4) | copy-start | bytes 9437188
  275.4 2.8 copy-start.3
  298.6 4.0 copy-start.1
  342.0 1.9 copy-start.2
  342.2 2.4 copy-start.11
  344.6 2.6 copy-start.12
  344.6 2.6 copy-start.8
